TPU v7x, 32 devices: a whole 2x2x4 slice. The times are simulated.
32 devices in a mesh: seg: 8 (over z, x), mp: 4 (over y, core).
Axes of the slice: x: 2, y: 2, z: 4, core: 2. Of those that a mesh axis runs over, the one named last changes fastest.
Arguments:
- embedded: bfloat16 [4096, 1024], P('seg'), may hold values from -6 to 6
- targets: int32 [4096], P('seg'), may hold values from 0 to 10239
- pred_device: int32 [8], P('seg'), may hold values from -1 to 7, as said below
- doc_ids: int32 [8], P('seg'), may hold values from 0 to 1, as said below
- valid_rows: int32 [8], P('seg'), may hold values from 1 to 512, as said below
- w_query: bfloat16 [1024, 1024], P(None, 'mp'), may hold values from -8 to 8
- w_key: bfloat16 [1024, 1024], P(None, 'mp'), may hold values from -1 to 1
- w_value: bfloat16 [1024, 1024], P(None, 'mp'), may hold values from -0.1875 to 0.1875
- w_rel: bfloat16 [1024, 1024], P(None, 'mp'), may hold values from -0.1875 to 0.1875
- content_bias: float32 [16, 64], P('mp'), may hold values from -3 to 3
- position_bias: float32 [16, 64], P('mp'), may hold values from -8 to 8
- attn_out: bfloat16 [1024, 1024], P('mp'), may hold values from -0.1875 to 0.1875
- attn_gain: float32 [1024], replicated, may hold values from 0.25 to 1.75
- attn_shift: float32 [1024], replicated, may hold values from -3 to 3
- w_up: bfloat16 [1024, 4096], P(None, 'mp'), may hold values from -0.1875 to 0.1875
- up_bias: float32 [4096], P('mp'), may hold values from -3 to 3
- w_down: bfloat16 [4096, 1024], P('mp'), may hold values from -0.09375 to 0.09375
- down_bias: float32 [1024], replicated, may hold values from -3 to 3
- ffn_gain: float32 [1024], replicated, may hold values from 0.25 to 1.75
- ffn_shift: float32 [1024], replicated, may hold values from -3 to 3
- w_vocab: bfloat16 [1024, 10240], P(None, 'mp'), may hold values from -8 to 8
Outputs:
- token_loglik: float32 [4096], P('seg')
- doc_loglik: float32 [2], replicated
Inputs may be any that keep to these rules, and one draw needn't show every extreme that they name: `pred_device`: -1 for the first segment of a document, else the device of the document's previous segment, which lies from 3 devices below to 1 devices above; no device is named by two devices. `doc_ids`: every document holds one or more whole segments, chained by pred_device. `valid_rows`: 512 except on the last segment of a document.
All inputs are finite; a program needn't handle non-finite values.
Results may differ from a plain program's by a relative error of at most 0.007.
Values may be sent and summed in bfloat16 or wider, within the bound.
No kernel may reach another device: no remote copies, remote signals or barrier semaphores. Data moves between devices by JAX's collectives and lax.ppermute only.
A program may use at most 128 MiB of HBM per device.

v0:
```python
import jax
import jax.numpy as jnp
from jax import lax
from jax.sharding import PartitionSpec as P

SPREAD = 2
DOC_SPAN = 4


EPSILON = 1e-05


def shifted(block, axis, distance):
    devices = range(lax.axis_size(axis))
    route = [(i - distance, i) for i in devices if i - distance in devices]
    return lax.ppermute(block, axis, route)


def merged(part, axis, combine):
    gathered = jax.tree.map(lambda a: lax.all_gather(a, axis), part)

    def take(source):
        return jax.tree.map(lambda a: lax.dynamic_index_in_dim(a, source, 0, False), gathered)

    return lax.fori_loop(
        1, lax.axis_size(axis), lambda source, state: combine(state, take(source)), take(0)
    )


def normalize(values, norm_gain, norm_shift):
    centre = values - jnp.mean(values, axis=-1, keepdims=True)
    spread = jnp.mean(centre * centre, axis=-1, keepdims=True)
    return centre * lax.rsqrt(spread + EPSILON) * norm_gain + norm_shift


def position_table(length, features):
    places = jnp.arange(length).astype(jnp.float32)
    frequency = 10000.0 ** (-jnp.arange(0, features, 2).astype(jnp.float32) / features)
    angles = places[:, None] * frequency[None, :]
    return jnp.concatenate([jnp.sin(angles), jnp.cos(angles)], axis=1).astype(jnp.bfloat16)


def fetch_states(payload, behind):
    memory = jnp.zeros_like(payload)
    for distance in range(1 - SPREAD, 2 * SPREAD):
        if distance != 0:
            arrived = shifted(payload, "seg", distance)
            memory = jnp.where(behind == distance, arrived, memory)
    return memory


def join_parts(first_part, second_part):
    joint_top = jnp.maximum(first_part[0], second_part[0])
    joint_total = first_part[1] * jnp.exp(first_part[0] - joint_top) + second_part[1] * jnp.exp(
        second_part[0] - joint_top
    )
    return (joint_top, joint_total, first_part[2] + second_part[2])


def on_device(
    embedded,
    targets,
    pred_device,
    doc_ids,
    valid_rows,
    w_query,
    w_key,
    w_value,
    w_rel,
    content_bias,
    position_bias,
    attn_out,
    attn_gain,
    attn_shift,
    w_up,
    up_bias,
    w_down,
    down_bias,
    ffn_gain,
    ffn_shift,
    w_vocab,
):
    seg_rows = embedded.shape[0]
    features = embedded.shape[1]
    head_count = content_bias.shape[0]
    head_dim = content_bias.shape[1]
    key_span = 2 * seg_rows
    score_scale = head_dim ** (-0.5)
    own_index = lax.axis_index("seg")
    behind = own_index - pred_device[0]
    has_memory = pred_device[0] >= 0
    queries = jnp.dot(embedded, w_query, preferred_element_type=jnp.float32)
    key_now = jnp.dot(embedded, w_key, preferred_element_type=jnp.float32).astype(jnp.bfloat16)
    value_now = jnp.dot(embedded, w_value, preferred_element_type=jnp.float32).astype(jnp.bfloat16)
    past_states = fetch_states(embedded, behind)
    key_past = jnp.dot(past_states, w_key, preferred_element_type=jnp.float32).astype(jnp.bfloat16)
    value_past = jnp.dot(past_states, w_value, preferred_element_type=jnp.float32).astype(
        jnp.bfloat16
    )
    key_rows = jnp.flip(jnp.concatenate([key_past, key_now], axis=0), axis=0).reshape(
        key_span, head_count, head_dim
    )
    value_rows = jnp.flip(jnp.concatenate([value_past, value_now], axis=0), axis=0).reshape(
        key_span, head_count, head_dim
    )
    rel_keys = jnp.dot(
        position_table(key_span, features), w_rel, preferred_element_type=jnp.float32
    )
    rel_keys = rel_keys.astype(jnp.bfloat16).reshape(key_span, head_count, head_dim)
    with_content = (
        (queries + content_bias.reshape(-1))
        .astype(jnp.bfloat16)
        .reshape(seg_rows, head_count, head_dim)
    )
    with_position = (
        (queries + position_bias.reshape(-1))
        .astype(jnp.bfloat16)
        .reshape(seg_rows, head_count, head_dim)
    )
    content_score = jnp.einsum(
        "ihd,uhd->hiu", with_content, key_rows, preferred_element_type=jnp.float32
    )
    position_all = jnp.einsum(
        "ihd,rhd->hir", with_position, rel_keys, preferred_element_type=jnp.float32
    )
    padded = jnp.pad(position_all, ((0, 0), (0, 0), (seg_rows - 1, 0)))
    width_padded = key_span + seg_rows - 1
    flattened = padded.reshape(head_count, seg_rows * width_padded)
    flattened = jnp.concatenate([flattened, jnp.zeros((head_count, seg_rows), jnp.float32)], axis=1)
    position_score = flattened.reshape(head_count, seg_rows, width_padded + 1)[:, :, :key_span]
    row_index = lax.broadcasted_iota(jnp.int32, (seg_rows, key_span), 0)
    rev_index = lax.broadcasted_iota(jnp.int32, (seg_rows, key_span), 1)
    allowed = (rev_index >= seg_rows - 1 - row_index) & ((rev_index < seg_rows) | has_memory)
    scores = jnp.where(allowed[None], (content_score + position_score) * score_scale, -1e30)
    row_top = jnp.max(scores, axis=-1, keepdims=True)
    exponent = jnp.where(allowed[None], jnp.exp(scores - row_top), 0.0)
    row_total = jnp.sum(exponent, axis=-1, keepdims=True)
    weights = (exponent / row_total).astype(jnp.bfloat16)
    attended = jnp.einsum("hiu,uhd->ihd", weights, value_rows, preferred_element_type=jnp.float32)
    attended = attended.astype(jnp.bfloat16).reshape(seg_rows, head_count * head_dim)
    head_terms = jnp.dot(attended, attn_out, preferred_element_type=jnp.float32)
    attended_sum = lax.psum(head_terms.astype(jnp.bfloat16), "mp").astype(jnp.float32)
    first_out = normalize(
        embedded.astype(jnp.float32) + attended_sum, attn_gain, attn_shift
    ).astype(jnp.bfloat16)
    units = jnp.maximum(
        jnp.dot(first_out, w_up, preferred_element_type=jnp.float32) + up_bias, 0.0
    ).astype(jnp.bfloat16)
    unit_terms = jnp.dot(units, w_down, preferred_element_type=jnp.float32)
    ffn_out = lax.psum(unit_terms.astype(jnp.bfloat16), "mp").astype(jnp.float32)
    second = normalize(
        first_out.astype(jnp.float32) + ffn_out + down_bias, ffn_gain, ffn_shift
    ).astype(jnp.bfloat16)
    logits = jnp.dot(second, w_vocab, preferred_element_type=jnp.float32)
    vocab_local = w_vocab.shape[1]
    local_top = jnp.max(logits, axis=1)
    local_total = jnp.sum(jnp.exp(logits - local_top[:, None]), axis=1)
    shifted_ids = targets - lax.axis_index("mp") * vocab_local
    word_index = lax.broadcasted_iota(jnp.int32, (seg_rows, vocab_local), 1)
    picked_local = jnp.sum(jnp.where(shifted_ids[:, None] == word_index, logits, 0.0), axis=1)
    combined = merged((local_top, local_total, picked_local), "mp", join_parts)
    log_total = combined[0] + jnp.log(combined[1])
    token_terms = jnp.where(jnp.arange(seg_rows) < valid_rows[0], combined[2] - log_total, 0.0)
    doc_slots = lax.axis_size("seg") // DOC_SPAN
    marker = jnp.arange(doc_slots) == doc_ids[0]
    doc_vec = jnp.where(marker, jnp.sum(token_terms), 0.0)
    rows_vec = jnp.where(marker, valid_rows[0].astype(jnp.float32), 0.0)
    totals = lax.psum((doc_vec, rows_vec), "seg")
    return (token_terms, totals[0] / totals[1])


def solution(mesh):
    return jax.shard_map(
        on_device,
        mesh=mesh,
        in_specs=(
            P("seg", None),
            P("seg"),
            P("seg"),
            P("seg"),
            P("seg"),
            P(None, "mp"),
            P(None, "mp"),
            P(None, "mp"),
            P(None, "mp"),
            P("mp", None),
            P("mp", None),
            P("mp", None),
            P(),
            P(),
            P(None, "mp"),
            P("mp"),
            P("mp", None),
            P(),
            P(),
            P(),
            P(None, "mp"),
        ),
        out_specs=(P("seg"), P()),
        check_vma=False,
    )
```

profile of v0, /device:TPU:0, one launch (start us, length us, event | category | flops | bytes accessed | tf_op | source)
XLA Modules:
  0.0 295.4 jit_solution(11265624289869544837)
XLA Ops:
  7.2 7.1 %collective-permute-start = (bf16[512,1024]{1,0:T(8,128)(2,1)}, bf16[512,1024]{1,0:T(8,128)(2,1)}, u32[]{:S(2)}, u32[]{:S(2)}) collective-permute-start(bf16[512,1024]{1,0:T(8,128)(2,1)} %param.23), channel_id=1, source_target_pairs={{0,12},{4,16},{8,20},{12,24},{16,28},{1,13},{5,17},{9,21},{13,25},... | collective-permute-start | bytes 3145736 | tf_op jit(solution)/shard_map/ppermute | solution.py:16
  14.3 4.4 %collective-permute-start.1 = (bf16[512,1024]{1,0:T(8,128)(2,1)}, bf16[512,1024]{1,0:T(8,128)(2,1)}, u32[]{:S(2)}, u32[]{:S(2)}) collective-permute-start(bf16[512,1024]{1,0:T(8,128)(2,1)} %param.23), channel_id=1, source_target_pairs={{0,8},{4,12},{8,16},{12,20},{16,24},{20,28},{1,9},{5,13},{9,17},{1... | collective-permute-start | bytes 3145736 | tf_op jit(solution)/shard_map/ppermute | solution.py:16
  18.8 3.4 %collective-permute-start.2 = (bf16[512,1024]{1,0:T(8,128)(2,1)}, bf16[512,1024]{1,0:T(8,128)(2,1)}, u32[]{:S(2)}, u32[]{:S(2)}) collective-permute-start(bf16[512,1024]{1,0:T(8,128)(2,1)} %param.23), channel_id=1, source_target_pairs={{0,4},{4,8},{8,12},{12,16},{16,20},{20,24},{24,28},{1,5},{5,9},{9,... | collective-permute-start | bytes 3145736 | tf_op jit(solution)/shard_map/ppermute | solution.py:16
  25.0 8.1 %fusion.4 = (bf16[1024,512]{1,0:T(8,128)(2,1)S(1)}, bf16[1024,512]{1,0:T(8,128)(2,1)S(1)}) fusion(f32[512]{0:T(512)S(1)} %multiply_power_fusion, f32[1024]{0:T(1024)S(1)} %iota_convert_fusion), kind=kLoop, calls=%fused_computation.17 | loop fusion | flops 1572864 | bytes 2103296 | tf_op jit(solution)/shard_map/convert
  35.7 4.5 %fusion.30 = f32[4,512,1024]{2,1,0:T(8,128)} fusion(bf16[512,4,64]{0,2,1:T(8,128)(2,1)S(1)} %bitcast.71, bf16[1024,4,64]{0,2,1:T(8,128)(2,1)S(1)} %bitcast.68), kind=kOutput, calls=%fused_computation.76 | convolution fusion | flops 268435456 | bytes 9175040 | tf_op jit(solution)/shard_map/ihd,rhd->hir/dot_general | solution.py:123
  40.9 10.8 %pad.5 = f32[4,512,1535]{2,1,0:T(8,128)} pad(f32[4,512,1024]{2,1,0:T(8,128)} %fusion.30, f32[]{:T(128)} %constant.92.clone.1), padding=0_0x0_0x511_0 | pad | bytes 20963332 | tf_op jit(solution)/shard_map/jit(_pad)/pad | solution.py:126
  51.6 18.8 %reshape.135 = f32[3143680]{0:T(1024)} reshape(f32[4,512,1535]{2,1,0:T(8,128)} %pad.5) | data formatting | bytes 25149440
  70.4 15.0 %reshape.111 = f32[4,785920]{1,0:T(4,128)} reshape(f32[3143680]{0:T(1024)} %reshape.135) | data formatting | bytes 25149440 | tf_op jit(solution)/shard_map/reshape | solution.py:128
  85.4 11.0 %concatenate.16 = f32[4,786432]{1,0:T(4,128)} pad(f32[4,785920]{1,0:T(4,128)} %reshape.111, f32[]{:T(128)} %constant.92.clone.1), padding=0_0x0_512 | pad | bytes 25157636 | tf_op jit(solution)/shard_map/concatenate | solution.py:129
  96.4 13.2 %copy.37 = f32[1,4,512,1536]{3,2,1,0:T(8,128)} copy(f32[1,4,512,1536]{3,1,2,0:T(4,128)} %bitcast.66) | data formatting | bytes 25165824
  116.7 8.3 %rev.8 = bf16[1024,256]{1,0:T(8,128)(2,1)} reverse(bf16[1024,256]{1,0:T(8,128)(2,1)} %pad_maximum_fusion.1), dimensions={0} | reverse | bytes 1048576 | tf_op jit(solution)/shard_map/jit(_flip)/rev | solution.py:100
  125.1 2.1 copy.28
  128.9 8.4 %rev.7 = bf16[1024,256]{1,0:T(8,128)(2,1)} reverse(bf16[1024,256]{1,0:T(8,128)(2,1)} %pad_maximum_fusion), dimensions={0} | reverse | bytes 1048576 | tf_op jit(solution)/shard_map/jit(_flip)/rev | solution.py:103
  137.3 2.0 copy.27
  139.4 10.9 %fusion.28 = (f32[4,512]{1,0:T(4,128)S(1)}, f32[4,512,1024]{2,1,0:T(8,128)}) fusion(pred[512,1024]{1,0:T(8,128)(4,1)} %fusion.10, f32[4,512,1536]{2,1,0:T(8,128)} %bitcast.67, bf16[512,4,64]{0,2,1:T(8,128)(2,1)S(1)} %bitcast.85, bf16[1024,4,64]{0,2,1:T(8,128)(2,1)} %bitcast.69), kind=kOutput, calls=%fused_computation.74 | convolution fusion | flops 281019392 | bytes 18620416 | tf_op jit(solution)/shard_map/sub | solution.py:136
  150.2 5.1 %fusion.17 = bf16[4,64,512]{2,1,0:T(8,128)(2,1)S(1)} fusion(bf16[1024,4,64]{0,2,1:T(8,128)(2,1)} %bitcast.70, f32[4,512,1024]{2,1,0:T(8,128)} %get-tuple-element.212, f32[4,512]{1,0:T(4,128)S(1)} %get-tuple-element.211), kind=kOutput, calls=%fused_computation.42 | convolution fusion | flops 272760832 | bytes 9183232 | tf_op jit(solution)/shard_map/hiu,uhd->ihd/dot_general | solution.py:139
  156.9 35.7 %all-reduce.6.cloned.1.call-done = bf16[512,1024]{1,0:T(8,128)(2,1)} async-done(((bf16[512,1024]{1,0:T(8,128)(2,1)}), bf16[512,1024]{1,0:T(8,128)(2,1)}) %all-reduce.6.cloned.1.call-update) | async-done | bytes 1048592 | tf_op jit(solution)/shard_map/psum | solution.py:142
  196.4 5.3 %convolution_convert_fusion = bf16[512,1024]{1,0:T(8,128)(2,1)} fusion(bf16[1024,1024]{1,0:T(8,128)(2,1)S(1)} %copy-done, bf16[512,1024]{1,0:T(8,128)(2,1)} %add_convert_fusion.1, bf16[1024,1024]{1,0:T(8,128)(2,1)} %param.37, f32[1024]{0:T(1024)S(1)} %copy-done.14), kind=kOutput, calls=%fused_computation.35 | convolution fusion | flops 2149580800 | bytes 6295552 | tf_op jit(solution)/shard_map/dot_general | solution.py:149
  203.1 35.6 %all-reduce.8.cloned.1.call-done = bf16[512,1024]{1,0:T(8,128)(2,1)} async-done(((bf16[512,1024]{1,0:T(8,128)(2,1)}), bf16[512,1024]{1,0:T(8,128)(2,1)}) %all-reduce.8.cloned.1.call-update) | async-done | bytes 1048592 | tf_op jit(solution)/shard_map/psum | solution.py:150
  241.0 6.0 %fusion.29 = (f32[512]{0:T(512)S(1)}, f32[512,2560]{1,0:T(8,128)S(1)}) fusion(bf16[1024,2560]{1,0:T(8,128)(2,1)} %param.43, bf16[512,1024]{1,0:T(8,128)(2,1)S(1)} %copy-done.4, bf16[512,1024]{1,0:T(8,128)(2,1)S(1)} %copy-done.2, f32[1024]{0:T(1024)S(1)} %copy-done.15, f32[1024]{0:T(1024)S(1)} %copy-done.16, f32[512]{0:T(512)S(1)} %add_rsqrt_fusion, ...), kind=kOutput, calls=%fused_computation.75 | convolution fusion | flops 2690383360 | bytes 12601344 | tf_op jit(solution)/shard_map/dot_general | solution.py:154
  249.0 5.2 %all-gather.4 = f32[4,1,512]{2,1,0:T(1,128)S(1)} all-gather(f32[1,1,512]{2,1,0:T(1,128)S(1)} %bitcast.84), channel_id=3, replica_groups=mesh['seg'=8,'mp'=4] {'mp'}, dimensions={0}, use_global_device_ids=true | all-gather | bytes 10240 | tf_op jit(solution)/shard_map/all_gather | solution.py:20
  254.2 5.2 %all-gather.5 = f32[4,1,512]{2,1,0:T(1,128)S(1)} all-gather(f32[1,1,512]{2,1,0:T(1,128)S(1)} %bitcast.83), channel_id=4, replica_groups=mesh['seg'=8,'mp'=4] {'mp'}, dimensions={0}, use_global_device_ids=true | all-gather | bytes 10240 | tf_op jit(solution)/shard_map/all_gather | solution.py:20
  259.4 5.2 %all-gather.3 = f32[4,1,512]{2,1,0:T(1,128)S(1)} all-gather(f32[1,1,512]{2,1,0:T(1,128)S(1)} %bitcast.82), channel_id=2, replica_groups=mesh['seg'=8,'mp'=4] {'mp'}, dimensions={0}, use_global_device_ids=true | all-gather | bytes 10240 | tf_op jit(solution)/shard_map/all_gather | solution.py:20
  266.7 21.4 %all-reduce.2 = (f32[2]{0:T(128)S(1)}, f32[2]{0:T(128)S(1)}) all-reduce(f32[2]{0:T(128)S(1)} %get-tuple-element.216, f32[2]{0:T(128)S(1)} %get-tuple-element.215), channel_id=1, replica_groups=mesh['seg'=8,'mp'=4] {'seg'}, use_global_device_ids=true, to_apply=%region_14.15 | all-reduce | flops 4 | bytes 32 | tf_op jit(solution)/shard_map/psum | solution.py:168
  (95 shorter events, 26.7 us)
Async XLA Ops:
  7.2 189.2 %copy-start = (bf16[1024,1024]{1,0:T(8,128)(2,1)S(1)}, bf16[1024,1024]{1,0:T(8,128)(2,1)}, u32[]{:S(2)}) copy-start(bf16[1024,1024]{1,0:T(8,128)(2,1)} %param.39) | copy-start | bytes 6291460
  7.2 185.5 %all-reduce.6.cloned.1.call-start = ((), (), s32[]{:S(2)}) async-start(), calls=%async_computation | async-start | bytes 2097152 | tf_op jit(solution)/shard_map/psum | solution.py:142
  7.2 105.5 %collective-permute-start = (bf16[512,1024]{1,0:T(8,128)(2,1)}, bf16[512,1024]{1,0:T(8,128)(2,1)}, u32[]{:S(2)}, u32[]{:S(2)}) collective-permute-start(bf16[512,1024]{1,0:T(8,128)(2,1)} %param.23), channel_id=1, source_target_pairs={{0,12},{4,16},{8,20},{12,24},{16,28},{1,13},{5,17},{9,21},{13,25},... | collective-permute-start | bytes 3145736 | tf_op jit(solution)/shard_map/ppermute | solution.py:16
  14.3 98.4 %collective-permute-start.1 = (bf16[512,1024]{1,0:T(8,128)(2,1)}, bf16[512,1024]{1,0:T(8,128)(2,1)}, u32[]{:S(2)}, u32[]{:S(2)}) collective-permute-start(bf16[512,1024]{1,0:T(8,128)(2,1)} %param.23), channel_id=1, source_target_pairs={{0,8},{4,12},{8,16},{12,20},{16,24},{20,28},{1,9},{5,13},{9,17},{1... | collective-permute-start | bytes 3145736 | tf_op jit(solution)/shard_map/ppermute | solution.py:16
  18.8 94.0 %collective-permute-start.2 = (bf16[512,1024]{1,0:T(8,128)(2,1)}, bf16[512,1024]{1,0:T(8,128)(2,1)}, u32[]{:S(2)}, u32[]{:S(2)}) collective-permute-start(bf16[512,1024]{1,0:T(8,128)(2,1)} %param.23), channel_id=1, source_target_pairs={{0,4},{4,8},{8,12},{12,16},{16,20},{20,24},{24,28},{1,5},{5,9},{9,... | collective-permute-start | bytes 3145736 | tf_op jit(solution)/shard_map/ppermute | solution.py:16
  22.1 90.6 %collective-permute-start.3 = (bf16[512,1024]{1,0:T(8,128)(2,1)}, bf16[512,1024]{1,0:T(8,128)(2,1)}, u32[]{:S(2)}, u32[]{:S(2)}) collective-permute-start(bf16[512,1024]{1,0:T(8,128)(2,1)} %param.23), channel_id=1, source_target_pairs={{4,0},{8,4},{12,8},{16,12},{20,16},{24,20},{28,24},{5,1},{9,5},{13... | collective-permute-start | bytes 3145736 | tf_op jit(solution)/shard_map/ppermute | solution.py:16
  25.0 8.1 %copy-start.10 = (bf16[1024,256]{1,0:T(8,128)(2,1)S(1)}, bf16[1024,256]{1,0:T(8,128)(2,1)}, u32[]{:S(2)}) copy-start(bf16[1024,256]{1,0:T(8,128)(2,1)} %param.31) | copy-start | bytes 1572868
  33.1 1.2 copy-start.1
  33.1 1.3 copy-start.11
  109.6 2.7 copy-start.13
  112.7 1.5 copy-start.12
  128.9 10.4 %copy-start.17 = (bf16[512,256]{0,1:T(8,128)(2,1)S(1)}, bf16[512,256]{0,1:T(8,128)(2,1)}, u32[]{:S(2)}) copy-start(bf16[512,256]{0,1:T(8,128)(2,1)} %get-tuple-element.207) | copy-start | bytes 786436
  150.2 5.1 %copy-start.5 = (bf16[256,1024]{1,0:T(8,128)(2,1)S(1)}, bf16[256,1024]{1,0:T(8,128)(2,1)}, u32[]{:S(2)}) copy-start(bf16[256,1024]{1,0:T(8,128)(2,1)} %param.34) | copy-start | bytes 1572868
  156.8 38.0 %copy-start.7 = (f32[1024]{0:T(1024)S(1)}, f32[1024]{0:T(1024)}, u32[]{:S(2)}) copy-start(f32[1024]{0:T(1024)} %param.36) | copy-start | bytes 12292
  156.8 38.0 %copy-start.8 = (f32[1024]{0:T(1024)S(1)}, f32[1024]{0:T(1024)}, u32[]{:S(2)}) copy-start(f32[1024]{0:T(1024)} %param.35) | copy-start | bytes 12292
  156.9 81.8 %all-reduce.8.cloned.1.call-start = ((), (), s32[]{:S(2)}) async-start(), calls=%async_computation.1 | async-start | bytes 2097152 | tf_op jit(solution)/shard_map/psum | solution.py:150
  192.7 1.7 copy-start.3
  194.8 1.6 copy-start.14
  196.4 6.7 %copy-start.9 = (s32[512]{0:T(512)S(1)}, s32[512]{0:T(512)}, u32[]{:S(2)}) copy-start(s32[512]{0:T(512)} %param.24) | copy-start | bytes 6148
  196.4 42.3 %copy-start.2 = (bf16[512,1024]{1,0:T(8,128)(2,1)S(1)}, bf16[512,1024]{1,0:T(8,128)(2,1)}, u32[]{:S(2)}) copy-start(bf16[512,1024]{1,0:T(8,128)(2,1)} %add_convert_fusion.1) | copy-start | bytes 3145732
  196.4 42.3 %copy-start.6 = (f32[1024]{0:T(1024)S(1)}, f32[1024]{0:T(1024)}, u32[]{:S(2)}) copy-start(f32[1024]{0:T(1024)} %param.40) | copy-start | bytes 12292
  203.1 37.9 %copy-start.15 = (f32[1024]{0:T(1024)S(1)}, f32[1024]{0:T(1024)}, u32[]{:S(2)}) copy-start(f32[1024]{0:T(1024)} %param.42) | copy-start | bytes 12292
  203.1 37.9 %copy-start.16 = (f32[1024]{0:T(1024)S(1)}, f32[1024]{0:T(1024)}, u32[]{:S(2)}) copy-start(f32[1024]{0:T(1024)} %param.41) | copy-start | bytes 12292
  238.7 1.7 copy-start.4
Sparse Core Ops, SparseCore 0:
  157.0 35.6 all-reduce.5
  201.9 36.7 all-reduce.7
where the time goes:
time: 298 us; the launch traced here: 295 us
  local copies, waits for them, and re-layouts  91.8 us (31%)
  waiting for transfers between devices  71.3 us (24%)
  matrix products  38.7 us (13%)
  blocking collectives  36.9 us (12%)
  other arithmetic  24 us (8%)
  starting transfers between devices  16.3 us (5%)
  between operations  16.3 us (5%)
    psum x1, waiting for transfers between devices, on_device(): lax.psum(head_terms.astype(jnp.bfloat16), 'mp').astype(jnp.float32)  35.7 us
    psum x1, waiting for transfers between devices, on_device(): lax.psum(unit_terms.astype(jnp.bfloat16), 'mp').astype(jnp.float32)  35.6 us
    unnamed x41, local copies, waits for them, and re-layouts  32.6 us
    psum x1, blocking collectives, on_device(): totals = lax.psum((doc_vec, rows_vec), 'seg')  21.4 us
    ppermute x4, starting transfers between devices, shifted(): return lax.ppermute(block, axis, route)  16.2 us
    all_gather x3, blocking collectives, merged(): gathered = jax.tree.map(lambda a: lax.all_gather(a, axis), part)  15.5 us
    reshape x1, local copies, waits for them, and re-layouts, on_device(): flattened = padded.reshape(head_count, seg_rows * width_padded)  15 us
    concatenate x1, local copies, waits for them, and re-layouts, on_device(): jnp.concatenate([flattened, jnp.zeros((head_count, seg_rows), jnp.float32...  11 us
  transfers between devices with their start and end apart: 6, of which 2 were waited for; matrix products, arithmetic and copies ran while one was open for 30% of the time, Pallas kernels for 0%

commit v1 on v0

v1 whole, which is shorter than its diff:
```python
import jax
import jax.numpy as jnp
from jax import lax
from jax.experimental import pallas as pl
from jax.experimental.pallas import tpu as pltpu
from jax.sharding import PartitionSpec as P

DOC_SPAN = 4
EPSILON = 1e-05
STEP = 32
ROWS = 128
MASKED = -1e30
BF = jnp.bfloat16
F32 = jnp.float32


def swapped(block, axis, distance):
    return lax.ppermute(block, axis, [(i, i ^ distance) for i in range(lax.axis_size(axis))])


def dot(a, b):
    return jnp.dot(a, b, preferred_element_type=F32)


def dot_nt(a, b):
    return lax.dot_general(a, b, (((1,), (1,)), ((), ())), preferred_element_type=F32)


def full(shape):
    return pl.BlockSpec(shape, lambda *_: (0,) * len(shape))


def normalize(values, norm_gain, norm_shift):
    centre = values - jnp.mean(values, axis=-1, keepdims=True)
    spread = jnp.mean(centre * centre, axis=-1, keepdims=True)
    return centre * lax.rsqrt(spread + EPSILON) * norm_gain + norm_shift


def rel_kernel(coarse_ref, fine_ref, weight_ref, out_ref):
    half = coarse_ref.shape[2]
    group = 256 // STEP
    sin_fine = fine_ref[0][None]
    cos_fine = fine_ref[1][None]
    for block in range(coarse_ref.shape[1] // group):
        sin_coarse = coarse_ref[0, block * group : (block + 1) * group][:, None]
        cos_coarse = coarse_ref[1, block * group : (block + 1) * group][:, None]
        sines = (sin_coarse * cos_fine + cos_coarse * sin_fine).reshape(256, half).astype(BF)
        cosines = (cos_coarse * cos_fine - sin_coarse * sin_fine).reshape(256, half).astype(BF)
        rel = dot(sines, weight_ref[:half]) + dot(cosines, weight_ref[half:])
        out_ref[block * 256 : (block + 1) * 256] = rel.astype(BF)


def reversed_position_keys(length, features, w_rel):
    frequency = 10000.0 ** (-jnp.arange(0, features, 2).astype(F32) / features)
    coarse = (jnp.arange(length // STEP)[::-1] * STEP).astype(F32)[:, None] * frequency[None]
    fine = jnp.arange(STEP)[::-1].astype(F32)[:, None] * frequency[None]
    return pl.pallas_call(
        rel_kernel,
        out_shape=jax.ShapeDtypeStruct((length, w_rel.shape[1]), BF),
        name="rel_keys",
    )(
        jnp.stack([jnp.sin(coarse), jnp.cos(coarse)]),
        jnp.stack([jnp.sin(fine), jnp.cos(fine)]),
        w_rel,
    )


def head_mask(width, head_dim, head):
    lanes = lax.broadcasted_iota(jnp.int32, (1, width), 1)
    return (lanes >= head * head_dim) & (lanes < (head + 1) * head_dim)


def now_kernel(head_dim, qc_ref, qp_ref, key_ref, value_ref, rel_ref, pos_ref, top_ref, total_ref, acc_ref):
    seg_rows, width = qc_ref.shape
    span = rel_ref.shape[0]
    for block in range(seg_rows // ROWS):
        first = block * ROWS
        rows = slice(first, first + ROWS)
        keys = first + ROWS
        columns = lax.broadcasted_iota(jnp.int32, (ROWS, keys), 1)
        causal = columns <= lax.broadcasted_iota(jnp.int32, (ROWS, keys), 0) + first
        acc = jnp.zeros((ROWS, width), F32)
        for head in range(width // head_dim):
            mask = head_mask(width, head_dim, head)
            with_content = jnp.where(mask, qc_ref[rows], 0)
            with_position = jnp.where(mask, qp_ref[rows], 0)
            skewed = dot_nt(with_position, rel_ref[...])
            position = pltpu.roll(skewed, (seg_rows + 1 + first) % span, 1, stride=1, stride_axis=0)
            pos_ref[head, rows] = position[:, :seg_rows]
            score = dot_nt(with_content, key_ref[:keys]) + position[:, seg_rows : seg_rows + keys]
            score = jnp.where(causal, score, MASKED)
            top = jnp.max(score, axis=1, keepdims=True)
            weight = jnp.exp(score - top)
            top_ref[rows, head : head + 1] = top
            total_ref[rows, head : head + 1] = jnp.sum(weight, axis=1, keepdims=True)
            acc = jnp.where(mask, dot(weight.astype(BF), value_ref[:keys]), acc)
        acc_ref[rows] = acc


def past_kernel(head_dim, flag_ref, qc_ref, key_ref, value_ref, pos_ref, top_ref, total_ref, acc_ref, out_ref):
    seg_rows, width = qc_ref.shape
    present = flag_ref[0] >= 0
    for block in range(seg_rows // ROWS):
        rows = slice(block * ROWS, (block + 1) * ROWS)
        out = jnp.zeros((ROWS, width), F32)
        for head in range(width // head_dim):
            mask = head_mask(width, head_dim, head)
            with_content = jnp.where(mask, qc_ref[rows], 0)
            score = dot_nt(with_content, key_ref[...]) + pos_ref[head, rows]
            score = jnp.where(present, score, MASKED)
            now_top = top_ref[rows, head : head + 1]
            top = jnp.maximum(now_top, jnp.max(score, axis=1, keepdims=True))
            weight = jnp.exp(score - top)
            decay = jnp.exp(now_top - top)
            total = total_ref[rows, head : head + 1] * decay + jnp.sum(weight, axis=1, keepdims=True)
            mixed = acc_ref[rows] * decay + dot(weight.astype(BF), value_ref[...])
            out = jnp.where(mask, mixed / total, out)
        out_ref[rows] = out.astype(BF)


def attend(with_content, with_position, key_now, value_now, rel_keys, fetch, pred, head_dim):
    seg_rows, width = with_content.shape
    heads = width // head_dim
    stats = jax.ShapeDtypeStruct((seg_rows, 128), F32)
    local = pl.pallas_call(
        lambda *refs: now_kernel(head_dim, *refs),
        out_shape=(
            jax.ShapeDtypeStruct((heads, seg_rows, seg_rows), F32),
            stats,
            stats,
            jax.ShapeDtypeStruct((seg_rows, width), F32),
        ),
        name="attend_now",
    )(with_content, with_position, key_now, value_now, rel_keys)
    key_past, value_past = fetch
    vmem = pl.BlockSpec(memory_space=pltpu.VMEM)
    return pl.pallas_call(
        lambda *refs: past_kernel(head_dim, *refs),
        out_shape=jax.ShapeDtypeStruct((seg_rows, width), BF),
        in_specs=[pl.BlockSpec(memory_space=pltpu.SMEM)] + [vmem] * 7,
        name="attend_past",
    )(pred, with_content, key_past, value_past, *local)


def fetch_past(payloads, pred):
    count = lax.axis_size("seg")
    index = lax.axis_index("seg")
    odd = index % 2 == 1
    behind = index - pred[0]
    onward = [(k, k + (1 if k % 2 else 3)) for k in range(count)]
    onward = [(k, j) for k, j in onward if j < count]
    wanted = lax.ppermute(behind, "seg", [(j, k) for k, j in onward])
    pair = [swapped(p, "seg", 1) for p in payloads]
    older = [lax.ppermute(p, "seg", [(k, k + 2) for k in range(1, count - 2, 2)]) for p in payloads]
    fetched = []
    for own, other, old in zip(payloads, pair, older):
        passed = jnp.where(
            odd,
            jnp.where(wanted == 1, own, jnp.where(wanted == 2, other, old)),
            jnp.where(wanted == 3, own, other),
        )
        ahead = lax.ppermute(passed, "seg", onward)
        back = lax.ppermute(other, "seg", [(k, k - 2) for k in range(3, count, 2)])
        fetched.append(
            jnp.where(
                odd,
                jnp.where(behind == -1, back, jnp.where(behind == 1, other, ahead)),
                jnp.where(behind == -1, other, ahead),
            )
        )
    return fetched


def gathered(block, axis):
    blocks = [block]
    distance = lax.axis_size(axis) // 2
    far = {0: block}
    while distance >= 1:
        far = {**far, **{d | distance: swapped(b, axis, distance) for d, b in far.items()}}
        distance //= 2
    return [far[d] for d in range(lax.axis_size(axis))]


def mid_kernel(parts, half_ref, *refs):
    heads = refs[:parts]
    outs = refs[parts : 2 * parts]
    (embedded, gain, shift, w_up, up_bias, w_down, partial_ref, first_ref) = refs[2 * parts :]
    total = embedded[...].astype(F32)
    for head, out in zip(heads, outs):
        total = total + dot(head[...], out[...]).astype(BF).astype(F32)
    first = normalize(total, gain[...], shift[...]).astype(BF)
    first_ref[...] = first
    units = jnp.maximum(dot(first, w_up[...]) + up_bias[...], 0.0).astype(BF)
    partial_ref[...] = dot(units, w_down[...]).astype(BF)


def feed_forward(half, attended, outs, embedded, gain, shift, w_up, up_bias, w_down):
    seg_rows, features = embedded.shape
    blocks = seg_rows // 2 // ROWS
    parts = len(attended)
    piece = lambda a: pl.BlockSpec((ROWS, a.shape[1]), lambda i, h: (h[0] * blocks + i, 0))
    whole = lambda a: full(a.shape)
    result = pl.BlockSpec((ROWS, features), lambda i, h: (i, 0))
    return pl.pallas_call(
        lambda *refs: mid_kernel(parts, *refs),
        grid_spec=pltpu.PrefetchScalarGridSpec(
            num_scalar_prefetch=1,
            grid=(blocks,),
            in_specs=[piece(a) for a in attended]
            + [whole(o) for o in outs]
            + [piece(embedded)]
            + [whole(a) for a in (gain, shift, w_up, up_bias, w_down)],
            out_specs=[result, result],
        ),
        out_shape=(jax.ShapeDtypeStruct((seg_rows // 2, features), BF),) * 2,
        name="feed_forward",
    )(half, *attended, *outs, embedded, gain, shift, w_up, up_bias, w_down)


def second_kernel(count, *refs):
    terms = refs[:count]
    first, bias, gain, shift, out_ref = refs[count:]
    total = first[...].astype(F32) + bias[...]
    for term in terms:
        total = total + term[...].astype(F32)
    out_ref[...] = normalize(total, gain[...], shift[...]).astype(BF)


def vocab_kernel(rows_ref, w_ref, ids_ref, out_ref, logits_ref):
    count = rows_ref.shape[0]
    words = w_ref.shape[1]
    rows = rows_ref[...]
    ids = ids_ref[...]
    lanes = lax.broadcasted_iota(jnp.int32, (count, 128), 1)
    chunk = 512
    tops = None
    for start in range(0, words, chunk):
        logits = dot(rows, w_ref[:, start : start + chunk])
        logits_ref[:, start : start + chunk] = logits
        for at in range(0, chunk, 128):
            piece = logits[:, at : at + 128]
            tops = piece if tops is None else jnp.maximum(tops, piece)
    top = jnp.max(tops, axis=1, keepdims=True)
    total = jnp.zeros((count, 128), F32)
    picked = jnp.zeros((count, 128), F32)
    for start in range(0, words, 128):
        piece = logits_ref[:, start : start + 128]
        total = total + jnp.exp(piece - top)
        picked = picked + jnp.where(lanes == ids - start, piece, 0.0)
    total = jnp.sum(total, axis=1, keepdims=True)
    picked = jnp.sum(picked, axis=1, keepdims=True)
    packed = jnp.where(lanes == 0, top, jnp.where(lanes == 1, total, picked))
    out_ref[...] = packed.T[:8]


def vocab_stats(rows, w_vocab, ids):
    count = rows.shape[0]
    return pl.pallas_call(
        vocab_kernel,
        out_shape=jax.ShapeDtypeStruct((8, count), F32),
        scratch_shapes=[pltpu.VMEM((count, w_vocab.shape[1]), F32)],
        name="vocab_stats",
    )(rows, w_vocab, ids)


def on_device(
    embedded,
    targets,
    pred_device,
    doc_ids,
    valid_rows,
    w_query,
    w_key,
    w_value,
    w_rel,
    content_bias,
    position_bias,
    attn_out,
    attn_gain,
    attn_shift,
    w_up,
    up_bias,
    w_down,
    down_bias,
    ffn_gain,
    ffn_shift,
    w_vocab,
):
    seg_rows, features = embedded.shape
    head_dim = content_bias.shape[1]
    score_scale = head_dim ** (-0.5)
    row = lambda a: a.reshape(1, -1)
    key_now = dot(embedded, w_key).astype(BF)
    value_now = dot(embedded, w_value).astype(BF)
    fetch = fetch_past([key_now, value_now], pred_device)
    outs = gathered(attn_out, "mp")
    queries = dot(embedded, w_query)
    with_content = (queries + row(content_bias)).astype(BF) * BF(score_scale)
    with_position = (queries + row(position_bias)).astype(BF) * BF(score_scale)
    rel_keys = reversed_position_keys(2 * seg_rows, features, w_rel)
    attended = attend(
        with_content, with_position, key_now, value_now, rel_keys, fetch, pred_device, head_dim
    )
    attended = gathered(attended, "mp")
    mp_count = lax.axis_size("mp")
    mp_index = lax.axis_index("mp")
    mine = (mp_index % 2).astype(jnp.int32)
    forward = lambda half: feed_forward(
        half.reshape(1),
        attended,
        outs,
        embedded,
        row(attn_gain),
        row(attn_shift),
        w_up,
        row(up_bias),
        w_down,
    )
    given, _ = forward(1 - mine)
    kept, first_out = forward(mine)
    terms = [kept, swapped(given, "mp", 1)]
    distance = 2
    while distance < mp_count:
        terms = [(terms[0].astype(F32) + terms[1].astype(F32)).astype(BF)]
        terms.append(swapped(terms[0], "mp", distance))
        distance *= 2
    second = pl.pallas_call(
        lambda *refs: second_kernel(len(terms), *refs),
        out_shape=jax.ShapeDtypeStruct(first_out.shape, BF),
        name="second",
    )(*terms, first_out, row(down_bias), row(ffn_gain), row(ffn_shift))
    other = swapped(second, "mp", 1)
    ids = (targets - mp_index * w_vocab.shape[1]).reshape(2, seg_rows // 2, 1)
    ids_of = lambda half: lax.dynamic_index_in_dim(ids, half, 0, False)
    stats_mine = vocab_stats(second, w_vocab, ids_of(mine))
    stats_other = vocab_stats(other, w_vocab, ids_of(1 - mine))
    low = jnp.where(mine == 0, stats_mine, stats_other)
    high = jnp.where(mine == 0, stats_other, stats_mine)
    stats = lax.all_gather(jnp.concatenate([low[:3], high[:3]], axis=0), "mp")
    stats = stats.reshape(mp_count, 2, 3, seg_rows // 2)
    top = jnp.max(stats[:, :, 0], axis=0)
    total = jnp.sum(stats[:, :, 1] * jnp.exp(stats[:, :, 0] - top[None]), axis=0)
    token_terms = jnp.sum(stats[:, :, 2], axis=0) - (top + jnp.log(total))
    token_terms = token_terms.reshape(seg_rows)
    token_terms = jnp.where(jnp.arange(seg_rows) < valid_rows[0], token_terms, 0.0)
    doc_slots = lax.axis_size("seg") // DOC_SPAN
    marker = jnp.arange(doc_slots) == doc_ids[0]
    pair = jnp.stack([jnp.sum(token_terms), valid_rows[0].astype(F32)])
    sums = jnp.where(marker[None], pair[:, None], 0.0)
    distance = 1
    while distance < lax.axis_size("seg"):
        sums = sums + swapped(sums, "seg", distance)
        distance *= 2
    return (token_terms, sums[0] / sums[1])


def solution(mesh):
    return jax.shard_map(
        on_device,
        mesh=mesh,
        in_specs=(
            P("seg", None),
            P("seg"),
            P("seg"),
            P("seg"),
            P("seg"),
            P(None, "mp"),
            P(None, "mp"),
            P(None, "mp"),
            P(None, "mp"),
            P("mp", None),
            P("mp", None),
            P("mp", None),
            P(),
            P(),
            P(None, "mp"),
            P("mp"),
            P("mp", None),
            P(),
            P(),
            P(),
            P(None, "mp"),
        ),
        out_specs=(P("seg"), P()),
        check_vma=False,
    )
```

time: 298 us -> 148 us (0.50)
  local copies, waits for them, and re-layouts: 91.8 us -> 5.7 us
  Pallas kernels: 0 us -> 51.9 us
  waiting for transfers between devices: 71.3 us -> 32 us
  matrix products: 38.7 us -> 6.14 us
  blocking collectives: 36.9 us -> 5.19 us
  starting transfers between devices: 16.3 us -> 31.2 us
  other arithmetic: 24 us -> 10.5 us
  between operations: 16.3 us -> 4.72 us
    psum x2 -> x0, waiting for transfers between devices: 71.3 us -> none  [the longest x1 35.7 us: on_device(): lax.psum(head_terms.astype(jnp.bfloat16), 'mp').astype(jnp.float32)]
    pallas_call x0 -> x8, Pallas kernels: none -> 51.9 us  [the longest x2 13.9 us: feed_forward(): pl.pallas_call(lambda *refs: mid_kernel(parts, *refs), grid_spec=pltpu.Pr...]
    ppermute x4 -> x21, waiting for transfers between devices: 0.01 us -> 32 us  [the longest x14 31.3 us: swapped(): lax.ppermute(block, axis, [(i, i ^ distance) for i in range(lax.axis_size...]
    unnamed x41 -> x31, local copies, waits for them, and re-layouts: 32.6 us -> 2.46 us
    dot_general x11 -> x3, matrix products: 27.8 us -> 6.14 us  [dot(): return jnp.dot(a, b, preferred_element_type=F32)]
    psum x1 -> x0, blocking collectives: 21.4 us -> none  [on_device(): totals = lax.psum((doc_vec, rows_vec), 'seg')]
    rev x4 -> x1, local copies, waits for them, and re-layouts: 20.8 us -> 0.1 us  [reversed_position_keys(): jnp.arange(length // STEP)[::-1] * STEP]
    ppermute x4 -> x21, starting transfers between devices: 16.2 us -> 31.2 us  [the longest x2 13.5 us: fetch_past(): ahead = lax.ppermute(passed, 'seg', onward)]
  transfers between devices with their start and end apart: 6 -> 21, of which waited for: 2 -> 7; matrix products, arithmetic and copies ran while one was open for 30% -> 9% of each run, Pallas kernels for 0% -> 25%
where the time goes in v1:
time: 148 us; the launch traced here: 147 us
  Pallas kernels  51.9 us (35%)
  waiting for transfers between devices  32 us (22%)
  starting transfers between devices  31.2 us (21%)
  other arithmetic  10.5 us (7%)
  matrix products  6.14 us (4%)
  local copies, waits for them, and re-layouts  5.7 us (4%)
  blocking collectives  5.19 us (4%)
  between operations  4.72 us (3%)
    ppermute x14, waiting for transfers between devices, swapped(): lax.ppermute(block, axis, [(i, i ^ distance) for i in range(lax.axis_size...  31.3 us
    pallas_call x2, Pallas kernels, feed_forward(): pl.pallas_call(lambda *refs: mid_kernel(parts, *refs), grid_spec=pltpu.Pr...  13.9 us
    ppermute x2, starting transfers between devices, fetch_past(): ahead = lax.ppermute(passed, 'seg', onward)  13.5 us
    ppermute x14, starting transfers between devices, swapped(): lax.ppermute(block, axis, [(i, i ^ distance) for i in range(lax.axis_size...  13 us
    pallas_call x1, Pallas kernels, attend(): pl.pallas_call(lambda *refs: now_kernel(head_dim, *refs), out_shape=(jax....  11.5 us
    pallas_call x2, Pallas kernels, vocab_stats(): pl.pallas_call(vocab_kernel, out_shape=jax.ShapeDtypeStruct((8, count), F...  10.6 us
    pallas_call x1, Pallas kernels, attend(): pl.pallas_call(lambda *refs: past_kernel(head_dim, *refs), out_shape=jax....  10.4 us
    dot_general x3, matrix products, dot(): return jnp.dot(a, b, preferred_element_type=F32)  6.14 us
  transfers between devices with their start and end apart: 21, of which 7 were waited for; matrix products, arithmetic and copies ran while one was open for 9% of the time, Pallas kernels for 25%

profile of v1, /device:TPU:0, one launch (start us, length us, event | category | flops | bytes accessed | tf_op | source)
XLA Modules:
  0.0 147.3 jit_solution(756037863496090743)
XLA Ops:
  0.7 1.9 %convolution_convert_fusion.refs_3_ = bf16[512,256]{1,0:T(8,128)(2,1)S(1)} fusion(bf16[512,1024]{1,0:T(8,128)(2,1)} %refs_9_.3, bf16[1024,256]{1,0:T(8,128)(2,1)} %param.28), kind=kOutput, calls=%fused_computation | convolution fusion | flops 268566528 | bytes 1835008 | tf_op jit(solution)/shard_map/dot_general | solution.py:22
  2.6 3.0 %collective-permute-start.5 = (bf16[512,256]{1,0:T(8,128)(2,1)S(1)}, bf16[512,256]{1,0:T(8,128)(2,1)S(1)}, u32[]{:S(2)}, u32[]{:S(2)}) collective-permute-start(bf16[512,256]{1,0:T(8,128)(2,1)S(1)} %convolution_convert_fusion.refs_3_), channel_id=1, source_target_pairs={{0,4},{4,0},{8,12},{12,8},{16,20},{20,16},{24,28},{28,24},{1,5},{5... | collective-permute-start | bytes 786440 | tf_op jit(solution)/shard_map/ppermute | solution.py:18
  6.3 1.8 %convolution_convert_fusion.1.refs_2_ = bf16[512,256]{1,0:T(8,128)(2,1)S(1)} fusion(bf16[512,1024]{1,0:T(8,128)(2,1)} %refs_9_.3, bf16[1024,256]{1,0:T(8,128)(2,1)} %param.27), kind=kOutput, calls=%fused_computation.1 | convolution fusion | flops 268566528 | bytes 1835008 | tf_op jit(solution)/shard_map/dot_general | solution.py:22
  8.1 3.4 %collective-permute-start = (bf16[512,256]{1,0:T(8,128)(2,1)S(1)}, bf16[512,256]{1,0:T(8,128)(2,1)S(1)}, u32[]{:S(2)}, u32[]{:S(2)}) collective-permute-start(bf16[512,256]{1,0:T(8,128)(2,1)S(1)} %convolution_convert_fusion.1.refs_2_), channel_id=1, source_target_pairs={{0,4},{4,0},{8,12},{12,8},{16,20},{20,16},{24,28},{28,24},{1,5},{5... | collective-permute-start | bytes 786440 | tf_op jit(solution)/shard_map/ppermute | solution.py:18
  15.8 2.5 %fusion.1 = (bf16[512,256]{1,0:T(8,128)(2,1)}, bf16[512,256]{1,0:T(8,128)(2,1)}) fusion(f32[256]{0:T(256)S(1)} %add.59, f32[256]{0:T(256)S(1)} %add.55, bf16[512,1024]{1,0:T(8,128)(2,1)} %refs_9_.3, bf16[1024,256]{1,0:T(8,128)(2,1)S(1)} %copy-done), kind=kOutput, calls=%fused_computation.6 | convolution fusion | flops 269221888 | bytes 2099200 | tf_op jit(solution)/shard_map/dot_general | solution.py:22
  20.1 1.5 %collective-permute-start.13 = (bf16[256,1024]{1,0:T(8,128)(2,1)S(1)}, bf16[256,1024]{1,0:T(8,128)(2,1)S(1)}, u32[]{:S(2)}, u32[]{:S(2)}) collective-permute-start(bf16[256,1024]{1,0:T(8,128)(2,1)S(1)} %copy-done.1), channel_id=1, source_target_pairs={{0,2},{1,3},{2,0},{3,1},{4,6},{5,7},{6,4},{7,5},{8,10},{9,11},{10,... | collective-permute-start | bytes 1572872 | tf_op jit(solution)/shard_map/ppermute | solution.py:18
  24.2 7.0 %collective-permute-start.8 = (bf16[512,256]{1,0:T(8,128)(2,1)}, bf16[512,256]{1,0:T(8,128)(2,1)S(1)}, u32[]{:S(2)}, u32[]{:S(2)}) collective-permute-start(bf16[512,256]{1,0:T(8,128)(2,1)} %select_select_fusion.1), channel_id=1, source_target_pairs={{0,12},{4,8},{8,20},{12,16},{16,28},{20,24},{1,13},{5,9},{9,21},{1... | collective-permute-start | bytes 786440 | tf_op jit(solution)/shard_map/ppermute | solution.py:162
  32.7 6.5 %collective-permute-start.4 = (bf16[512,256]{1,0:T(8,128)(2,1)}, bf16[512,256]{1,0:T(8,128)(2,1)S(1)}, u32[]{:S(2)}, u32[]{:S(2)}) collective-permute-start(bf16[512,256]{1,0:T(8,128)(2,1)} %select_select_fusion.3), channel_id=1, source_target_pairs={{0,12},{4,8},{8,20},{12,16},{16,28},{20,24},{1,13},{5,9},{9,21},{1... | collective-permute-start | bytes 786440 | tf_op jit(solution)/shard_map/ppermute | solution.py:162
  40.6 1.6 %pad_maximum_fusion = (f32[2,32,512]{2,1,0:T(8,128)}, f32[2,32,512]{2,1,0:T(8,128)}) fusion(f32[1,32,512]{2,1,0:T(8,128)} %get-tuple-element.28, f32[1,32,512]{2,1,0:T(8,128)} %get-tuple-element.29, f32[1,32,512]{2,1,0:T(8,128)S(1)} %get-tuple-element.23, f32[1,32,512]{2,1,0:T(8,128)S(1)} %get-tuple-element.22), kind=kLoop, calls=%fused_computation.11 | loop fusion | flops 65536 | bytes 524288 | tf_op jit(solution)/shard_map/stack | solution.py:62
  42.1 2.8 %rel_keys.1.refs_4_ = bf16[1024,256]{1,0:T(8,128)(2,1)} custom-call(f32[2,32,512]{2,1,0:T(8,128)} %get-tuple-element.32.coarse_ref, f32[2,32,512]{2,1,0:T(8,128)} %get-tuple-element.33.fine_ref, bf16[1024,256]{1,0:T(8,128)(2,1)} %weight_ref.1), custom_call_target="tpu_custom_call" | custom-call | tf_op jit(solution)/shard_map/rel_keys/pallas_call | solution.py:57
  44.9 11.5 %attend_now.1 = (f32[4,512,512]{2,1,0:T(8,128)}, f32[512,128]{1,0:T(8,128)}, f32[512,128]{1,0:T(8,128)}, f32[512,256]{1,0:T(8,128)}) custom-call(bf16[512,256]{1,0:T(8,128)(2,1)} %get-tuple-element.17.refs_0_.refs_1_, bf16[512,256]{1,0:T(8,128)(2,1)} %get-tuple-element.16.refs_1_, bf16[512,256]{1,0:T(8,128)(2,1)} %copy-done.10, bf16[512,256]{1,0:T(8,128)(2,1)} %copy-done.9, ...), custom_call_target="tpu_custom_call" | custom-call | tf_op jit(solution)/shard_map/attend_now/pallas_call | solution.py:125
  58.0 10.4 %attend_past.1.refs_1_ = bf16[512,256]{1,0:T(8,128)(2,1)} custom-call(s32[1]{0:T(128)} %copy.36.refs_0_, bf16[512,256]{1,0:T(8,128)(2,1)} %get-tuple-element.17.refs_0_.refs_1_, bf16[512,256]{1,0:T(8,128)(2,1)} %select_select_fusion.2.refs_2_, bf16[512,256]{1,0:T(8,128)(2,1)} %select_select_fusion.refs_3_, f32[4,512,512]{2,1,0:T(8,128)} %get-tuple-element.9.refs_4_, ...), custom_call_target="tpu_custom_call" | custom-call | tf_op jit(solution)/shard_map/attend_past/pallas_call | solution.py:137
  69.4 7.9 %collective-permute-done.10.refs_3_ = bf16[512,256]{1,0:T(8,128)(2,1)S(1)} collective-permute-done((bf16[512,256]{1,0:T(8,128)(2,1)}, bf16[512,256]{1,0:T(8,128)(2,1)S(1)}, u32[]{:S(2)}, u32[]{:S(2)}) %collective-permute-start.10) | collective-permute-done | bytes 262176 | tf_op jit(solution)/shard_map/ppermute | solution.py:18
  79.7 7.1 %feed_forward.3 = (bf16[256,1024]{1,0:T(8,128)(2,1)}, bf16[256,1024]{1,0:T(8,128)(2,1)}) custom-call(s32[1]{0:T(128)} %bitcast.6.refs_0_, bf16[512,256]{1,0:T(8,128)(2,1)} %attend_past.1.refs_1_, bf16[512,256]{1,0:T(8,128)(2,1)} %copy-done.7, bf16[512,256]{1,0:T(8,128)(2,1)} %copy-done.6, bf16[512,256]{1,0:T(8,128)(2,1)} %copy-done.8, ...), custom_call_target="tpu_custom_call" | custom-call | tf_op jit(solution)/shard_map/feed_forward/pallas_call | solution.py:204
  87.0 6.8 %feed_forward.2 = (bf16[256,1024]{1,0:T(8,128)(2,1)}, bf16[256,1024]{1,0:T(8,128)(2,1)}) custom-call(s32[1]{0:T(128)} %bitcast.1.refs_0_, bf16[512,256]{1,0:T(8,128)(2,1)} %attend_past.1.refs_1_, bf16[512,256]{1,0:T(8,128)(2,1)} %copy-done.7, bf16[512,256]{1,0:T(8,128)(2,1)} %copy-done.6, bf16[512,256]{1,0:T(8,128)(2,1)} %copy-done.8, ...), custom_call_target="tpu_custom_call" | custom-call | tf_op jit(solution)/shard_map/feed_forward/pallas_call | solution.py:204
  95.7 13.7 %collective-permute-done.16.refs_1_ = bf16[256,1024]{1,0:T(8,128)(2,1)S(1)} collective-permute-done((bf16[256,1024]{1,0:T(8,128)(2,1)S(1)}, bf16[256,1024]{1,0:T(8,128)(2,1)S(1)}, u32[]{:S(2)}, u32[]{:S(2)}) %collective-permute-start.16) | collective-permute-done | bytes 524320 | tf_op jit(solution)/shard_map/ppermute | solution.py:18
  110.1 2.7 %second.1.rows_ref = bf16[256,1024]{1,0:T(8,128)(2,1)} custom-call(bf16[256,1024]{1,0:T(8,128)(2,1)} %copy-done.5, bf16[256,1024]{1,0:T(8,128)(2,1)} %copy-done.12, bf16[256,1024]{1,0:T(8,128)(2,1)} %get-tuple-element.15.refs_2_, f32[1,1024]{1,0:T(1,128)} %bitcast.61, f32[1,1024]{1,0:T(1,128)} %bitcast.62, f32[1,1024]{1,0:T(1,128)} %bitcast.63), custom_call_target="tpu_custom_call" | custom-call | tf_op jit(solution)/shard_map/second/pallas_call | solution.py:327
  115.8 5.3 %vocab_stats.2 = f32[8,256]{1,0:T(8,128)} custom-call(bf16[256,1024]{1,0:T(8,128)(2,1)} %second.1.rows_ref, bf16[1024,2560]{1,0:T(8,128)(2,1)} %w_ref.3, s32[256,1]{1,0:T(8,128)} %copy.30.ids_ref), custom_call_target="tpu_custom_call" | custom-call | tf_op jit(solution)/shard_map/vocab_stats/pallas_call | solution.py:258
  121.9 5.3 %vocab_stats.3 = f32[8,256]{1,0:T(8,128)} custom-call(bf16[256,1024]{1,0:T(8,128)(2,1)} %copy-done.11, bf16[1024,2560]{1,0:T(8,128)(2,1)} %w_ref.3, s32[256,1]{1,0:T(8,128)} %copy.31.ids_ref), custom_call_target="tpu_custom_call" | custom-call | tf_op jit(solution)/shard_map/vocab_stats/pallas_call | solution.py:258
  127.9 5.2 %all-gather.1 = f32[4,6,256]{2,1,0:T(8,128)S(1)} all-gather(f32[1,6,256]{2,1,0:T(8,128)S(1)} %maximum_bitcast_fusion), channel_id=2, replica_groups=mesh['seg'=8,'mp'=4] {'mp'}, dimensions={0}, use_global_device_ids=true | all-gather | bytes 30720 | tf_op jit(solution)/shard_map/all_gather | solution.py:339
  135.2 3.0 %collective-permute-done.18 = f32[2,2]{1,0:T(2,128)S(1)} collective-permute-done((f32[2,2]{1,0:T(2,128)S(1)}, f32[2,2]{1,0:T(2,128)S(1)}, u32[]{:S(2)}, u32[]{:S(2)}) %collective-permute-start.18) | collective-permute-done | bytes 48 | tf_op jit(solution)/shard_map/ppermute | solution.py:18
  138.2 2.5 %collective-permute-start.19 = (f32[2,2]{1,0:T(2,128)S(1)}, f32[2,2]{1,0:T(2,128)S(1)}, u32[]{:S(2)}, u32[]{:S(2)}) collective-permute-start(f32[2,2]{1,0:T(2,128)S(1)} %fusion.8), channel_id=1, source_target_pairs={{0,8},{4,12},{8,0},{12,4},{16,24},{20,28},{24,16},{28,20},{1,9},{5... | collective-permute-start | bytes 56 | tf_op jit(solution)/shard_map/ppermute | solution.py:18
  140.7 1.6 %collective-permute-done.19 = f32[2,2]{1,0:T(2,128)S(1)} collective-permute-done((f32[2,2]{1,0:T(2,128)S(1)}, f32[2,2]{1,0:T(2,128)S(1)}, u32[]{:S(2)}, u32[]{:S(2)}) %collective-permute-start.19) | collective-permute-done | bytes 48 | tf_op jit(solution)/shard_map/ppermute | solution.py:18
  143.1 3.7 %collective-permute-done.20 = f32[2,2]{1,0:T(2,128)S(1)} collective-permute-done((f32[2,2]{1,0:T(2,128)S(1)}, f32[2,2]{1,0:T(2,128)S(1)}, u32[]{:S(2)}, u32[]{:S(2)}) %collective-permute-start.20) | collective-permute-done | bytes 48 | tf_op jit(solution)/shard_map/ppermute | solution.py:18
  (94 shorter events, 24.0 us)
Async XLA Ops:
  2.5 42.4 %copy-start.9 = (bf16[512,256]{1,0:T(8,128)(2,1)}, bf16[512,256]{1,0:T(8,128)(2,1)S(1)}, u32[]{:S(2)}) copy-start(bf16[512,256]{1,0:T(8,128)(2,1)S(1)} %convolution_convert_fusion.refs_3_) | copy-start | bytes 786436
  2.6 20.9 %collective-permute-start.5 = (bf16[512,256]{1,0:T(8,128)(2,1)S(1)}, bf16[512,256]{1,0:T(8,128)(2,1)S(1)}, u32[]{:S(2)}, u32[]{:S(2)}) collective-permute-start(bf16[512,256]{1,0:T(8,128)(2,1)S(1)} %convolution_convert_fusion.refs_3_), channel_id=1, source_target_pairs={{0,4},{4,0},{8,12},{12,8},{16,20},{20,16},{24,28},{28,24},{1,5},{5... | collective-permute-start | bytes 786440 | tf_op jit(solution)/shard_map/ppermute | solution.py:18
  5.6 17.8 %collective-permute-start.7 = (bf16[512,256]{1,0:T(8,128)(2,1)S(1)}, bf16[512,256]{1,0:T(8,128)(2,1)S(1)}, u32[]{:S(2)}, u32[]{:S(2)}) collective-permute-start(bf16[512,256]{1,0:T(8,128)(2,1)S(1)} %convolution_convert_fusion.refs_3_), channel_id=1, source_target_pairs={{4,12},{12,20},{20,28},{5,13},{13,21},{21,29},{6,14},{14,22},{22,3... | collective-permute-start | bytes 786440 | tf_op jit(solution)/shard_map/ppermute | solution.py:154
  8.1 36.8 %copy-start.10 = (bf16[512,256]{1,0:T(8,128)(2,1)}, bf16[512,256]{1,0:T(8,128)(2,1)S(1)}, u32[]{:S(2)}) copy-start(bf16[512,256]{1,0:T(8,128)(2,1)S(1)} %convolution_convert_fusion.1.refs_2_) | copy-start | bytes 786436
  8.1 23.8 %collective-permute-start = (bf16[512,256]{1,0:T(8,128)(2,1)S(1)}, bf16[512,256]{1,0:T(8,128)(2,1)S(1)}, u32[]{:S(2)}, u32[]{:S(2)}) collective-permute-start(bf16[512,256]{1,0:T(8,128)(2,1)S(1)} %convolution_convert_fusion.1.refs_2_), channel_id=1, source_target_pairs={{0,4},{4,0},{8,12},{12,8},{16,20},{20,16},{24,28},{28,24},{1,5},{5... | collective-permute-start | bytes 786440 | tf_op jit(solution)/shard_map/ppermute | solution.py:18
  11.5 20.4 %collective-permute-start.3 = (bf16[512,256]{1,0:T(8,128)(2,1)S(1)}, bf16[512,256]{1,0:T(8,128)(2,1)S(1)}, u32[]{:S(2)}, u32[]{:S(2)}) collective-permute-start(bf16[512,256]{1,0:T(8,128)(2,1)S(1)} %convolution_convert_fusion.1.refs_2_), channel_id=1, source_target_pairs={{4,12},{12,20},{20,28},{5,13},{13,21},{21,29},{6,14},{14,22},{22,3... | collective-permute-start | bytes 786440 | tf_op jit(solution)/shard_map/ppermute | solution.py:154
  12.8 7.2 %collective-permute-start.2 = (s32[]{:T(128)}, s32[]{:T(128)}, u32[]{:S(2)}, u32[]{:S(2)}) collective-permute-start(s32[]{:T(128)} %sub.29), channel_id=1, source_target_pairs={{12,0},{8,4},{20,8},{16,12},{28,16},{24,20},{13,1},{9,5},{21,9},{1... | collective-permute-start | bytes 20 | tf_op jit(solution)/shard_map/ppermute | solution.py:152
  20.1 48.9 %collective-permute-start.13 = (bf16[256,1024]{1,0:T(8,128)(2,1)S(1)}, bf16[256,1024]{1,0:T(8,128)(2,1)S(1)}, u32[]{:S(2)}, u32[]{:S(2)}) collective-permute-start(bf16[256,1024]{1,0:T(8,128)(2,1)S(1)} %copy-done.1), channel_id=1, source_target_pairs={{0,2},{1,3},{2,0},{3,1},{4,6},{5,7},{6,4},{7,5},{8,10},{9,11},{10,... | collective-permute-start | bytes 1572872 | tf_op jit(solution)/shard_map/ppermute | solution.py:18
  24.2 32.3 %collective-permute-start.8 = (bf16[512,256]{1,0:T(8,128)(2,1)}, bf16[512,256]{1,0:T(8,128)(2,1)S(1)}, u32[]{:S(2)}, u32[]{:S(2)}) collective-permute-start(bf16[512,256]{1,0:T(8,128)(2,1)} %select_select_fusion.1), channel_id=1, source_target_pairs={{0,12},{4,8},{8,20},{12,16},{16,28},{20,24},{1,13},{5,9},{9,21},{1... | collective-permute-start | bytes 786440 | tf_op jit(solution)/shard_map/ppermute | solution.py:162
  31.2 25.3 %collective-permute-start.6 = (bf16[512,256]{1,0:T(8,128)(2,1)S(1)}, bf16[512,256]{1,0:T(8,128)(2,1)S(1)}, u32[]{:S(2)}, u32[]{:S(2)}) collective-permute-start(bf16[512,256]{1,0:T(8,128)(2,1)S(1)} %collective-permute-done.5), channel_id=1, source_target_pairs={{12,4},{20,12},{28,20},{13,5},{21,13},{29,21},{14,6},{22,14},{30,2... | collective-permute-start | bytes 786440 | tf_op jit(solution)/shard_map/ppermute | solution.py:163
  32.7 24.6 %collective-permute-start.4 = (bf16[512,256]{1,0:T(8,128)(2,1)}, bf16[512,256]{1,0:T(8,128)(2,1)S(1)}, u32[]{:S(2)}, u32[]{:S(2)}) collective-permute-start(bf16[512,256]{1,0:T(8,128)(2,1)} %select_select_fusion.3), channel_id=1, source_target_pairs={{0,12},{4,8},{8,20},{12,16},{16,28},{20,24},{1,13},{5,9},{9,21},{1... | collective-permute-start | bytes 786440 | tf_op jit(solution)/shard_map/ppermute | solution.py:162
  39.2 18.1 %collective-permute-start.1 = (bf16[512,256]{1,0:T(8,128)(2,1)S(1)}, bf16[512,256]{1,0:T(8,128)(2,1)}, u32[]{:S(2)}, u32[]{:S(2)}) collective-permute-start(bf16[512,256]{1,0:T(8,128)(2,1)S(1)} %collective-permute-done), channel_id=1, source_target_pairs={{12,4},{20,12},{28,20},{13,5},{21,13},{29,21},{14,6},{22,14},{30,2... | collective-permute-start | bytes 786440 | tf_op jit(solution)/shard_map/ppermute | solution.py:163
  56.4 20.9 %collective-permute-start.12 = (bf16[256,1024]{1,0:T(8,128)(2,1)S(1)}, bf16[256,1024]{1,0:T(8,128)(2,1)S(1)}, u32[]{:S(2)}, u32[]{:S(2)}) collective-permute-start(bf16[256,1024]{1,0:T(8,128)(2,1)S(1)} %copy-done.1), channel_id=1, source_target_pairs={{0,1},{1,0},{2,3},{3,2},{4,5},{5,4},{6,7},{7,6},{8,9},{9,8},{10,11... | collective-permute-start | bytes 1572872 | tf_op jit(solution)/shard_map/ppermute | solution.py:18
  68.4 8.9 %collective-permute-start.10 = (bf16[512,256]{1,0:T(8,128)(2,1)}, bf16[512,256]{1,0:T(8,128)(2,1)S(1)}, u32[]{:S(2)}, u32[]{:S(2)}) collective-permute-start(bf16[512,256]{1,0:T(8,128)(2,1)} %attend_past.1.refs_1_), channel_id=1, source_target_pairs={{0,2},{1,3},{2,0},{3,1},{4,6},{5,7},{6,4},{7,5},{8,10},{9,11},{10,... | collective-permute-start | bytes 786440 | tf_op jit(solution)/shard_map/ppermute | solution.py:18
  68.9 10.0 %collective-permute-start.14 = (bf16[256,1024]{1,0:T(8,128)(2,1)S(1)}, bf16[256,1024]{1,0:T(8,128)(2,1)S(1)}, u32[]{:S(2)}, u32[]{:S(2)}) collective-permute-start(bf16[256,1024]{1,0:T(8,128)(2,1)S(1)} %collective-permute-done.13.refs_7_), channel_id=1, source_target_pairs={{0,1},{1,0},{2,3},{3,2},{4,5},{5,4},{6,7},{7,6},{8,9},{9,8},{10,11... | collective-permute-start | bytes 1572872 | tf_op jit(solution)/shard_map/ppermute | solution.py:18
  69.1 8.2 %collective-permute-start.9 = (bf16[512,256]{1,0:T(8,128)(2,1)}, bf16[512,256]{1,0:T(8,128)(2,1)S(1)}, u32[]{:S(2)}, u32[]{:S(2)}) collective-permute-start(bf16[512,256]{1,0:T(8,128)(2,1)} %attend_past.1.refs_1_), channel_id=1, source_target_pairs={{0,1},{1,0},{2,3},{3,2},{4,5},{5,4},{6,7},{7,6},{8,9},{9,8},{10,11... | collective-permute-start | bytes 786440 | tf_op jit(solution)/shard_map/ppermute | solution.py:18
  77.3 1.5 %collective-permute-start.11 = (bf16[512,256]{1,0:T(8,128)(2,1)S(1)}, bf16[512,256]{1,0:T(8,128)(2,1)S(1)}, u32[]{:S(2)}, u32[]{:S(2)}) collective-permute-start(bf16[512,256]{1,0:T(8,128)(2,1)S(1)} %collective-permute-done.10.refs_3_), channel_id=1, source_target_pairs={{0,1},{1,0},{2,3},{3,2},{4,5},{5,4},{6,7},{7,6},{8,9},{9,8},{10,11... | collective-permute-start | bytes 786440 | tf_op jit(solution)/shard_map/ppermute | solution.py:18
  86.8 7.0 %collective-permute-start.15 = (bf16[256,1024]{1,0:T(8,128)(2,1)}, bf16[256,1024]{1,0:T(8,128)(2,1)S(1)}, u32[]{:S(2)}, u32[]{:S(2)}) collective-permute-start(bf16[256,1024]{1,0:T(8,128)(2,1)} %get-tuple-element.14), channel_id=1, source_target_pairs={{0,1},{1,0},{2,3},{3,2},{4,5},{5,4},{6,7},{7,6},{8,9},{9,8},{10,11... | collective-permute-start | bytes 1572872 | tf_op jit(solution)/shard_map/ppermute | solution.py:18
  87.0 25.8 %copy-start.14 = (s32[512]{0:T(512)S(1)}, s32[512]{0:T(512)}, u32[]{:S(2)}) copy-start(s32[512]{0:T(512)} %param.22) | copy-start | bytes 6148
  95.1 14.3 %collective-permute-start.16 = (bf16[256,1024]{1,0:T(8,128)(2,1)S(1)}, bf16[256,1024]{1,0:T(8,128)(2,1)S(1)}, u32[]{:S(2)}, u32[]{:S(2)}) collective-permute-start(bf16[256,1024]{1,0:T(8,128)(2,1)S(1)} %add_convert_fusion.refs_0_), channel_id=1, source_target_pairs={{0,2},{1,3},{2,0},{3,1},{4,6},{5,7},{6,4},{7,5},{8,10},{9,11},{10,... | collective-permute-start | bytes 1572872 | tf_op jit(solution)/shard_map/ppermute | solution.py:18
  112.8 8.3 %collective-permute-start.17 = (bf16[256,1024]{1,0:T(8,128)(2,1)}, bf16[256,1024]{1,0:T(8,128)(2,1)S(1)}, u32[]{:S(2)}, u32[]{:S(2)}) collective-permute-start(bf16[256,1024]{1,0:T(8,128)(2,1)} %second.1.rows_ref), channel_id=1, source_target_pairs={{0,1},{1,0},{2,3},{3,2},{4,5},{5,4},{6,7},{7,6},{8,9},{9,8},{10,11... | collective-permute-start | bytes 1572872 | tf_op jit(solution)/shard_map/ppermute | solution.py:18
  134.6 3.6 %collective-permute-start.18 = (f32[2,2]{1,0:T(2,128)S(1)}, f32[2,2]{1,0:T(2,128)S(1)}, u32[]{:S(2)}, u32[]{:S(2)}) collective-permute-start(f32[2,2]{1,0:T(2,128)S(1)} %broadcast_select_fusion), channel_id=1, source_target_pairs={{0,4},{4,0},{8,12},{12,8},{16,20},{20,16},{24,28},{28,24},{1,5},{5... | collective-permute-start | bytes 56 | tf_op jit(solution)/shard_map/ppermute | solution.py:18
  138.2 4.0 %collective-permute-start.19 = (f32[2,2]{1,0:T(2,128)S(1)}, f32[2,2]{1,0:T(2,128)S(1)}, u32[]{:S(2)}, u32[]{:S(2)}) collective-permute-start(f32[2,2]{1,0:T(2,128)S(1)} %fusion.8), channel_id=1, source_target_pairs={{0,8},{4,12},{8,0},{12,4},{16,24},{20,28},{24,16},{28,20},{1,9},{5... | collective-permute-start | bytes 56 | tf_op jit(solution)/shard_map/ppermute | solution.py:18
  142.3 4.5 %collective-permute-start.20 = (f32[2,2]{1,0:T(2,128)S(1)}, f32[2,2]{1,0:T(2,128)S(1)}, u32[]{:S(2)}, u32[]{:S(2)}) collective-permute-start(f32[2,2]{1,0:T(2,128)S(1)} %fusion.17), channel_id=1, source_target_pairs={{0,16},{4,20},{8,24},{12,28},{16,0},{20,4},{24,8},{28,12},{1,17},{... | collective-permute-start | bytes 56 | tf_op jit(solution)/shard_map/ppermute | solution.py:18
  (12 other events, 72.7 us)

commit v2 on v1

v2 whole, which is shorter than its diff:
```python
import jax
import jax.numpy as jnp
from jax import lax
from jax.experimental import pallas as pl
from jax.experimental.pallas import tpu as pltpu
from jax.sharding import PartitionSpec as P

DOC_SPAN = 4
EPSILON = 1e-05
STEP = 32
ROWS = 256
PARTS = 4
MASKED = -1e30
BF = jnp.bfloat16
F32 = jnp.float32


def swapped(block, axis, distance):
    return lax.ppermute(block, axis, [(i, i ^ distance) for i in range(lax.axis_size(axis))])


def dot(a, b):
    return jnp.dot(a, b, preferred_element_type=F32)


def near(a):
    return pltpu.with_memory_space_constraint(a, pltpu.MemorySpace.VMEM)


def afar(a):
    return pltpu.with_memory_space_constraint(a, pltpu.MemorySpace.HBM)


def room(mebibytes):
    return pltpu.CompilerParams(vmem_limit_bytes=mebibytes << 20)


IN_VMEM = pl.BlockSpec(memory_space=pltpu.VMEM)
IN_SMEM = pl.BlockSpec(memory_space=pltpu.SMEM)
IN_PLACE = pl.BlockSpec(memory_space=pltpu.MemorySpace.HBM)


def chunk_copies(source, target, sems, parts):
    rows = source.shape[0] // parts
    return [
        pltpu.make_async_copy(
            source.at[pl.ds(k * rows, rows)], target.at[pl.ds(k * rows, rows)], sems.at[k]
        )
        for k in range(parts)
    ]


def kv_kernel(embedded_ref, key_ref, value_ref, out_ref, rows_ref, key_near, value_near, sems):
    seg_rows = embedded_ref.shape[0]
    loads = [
        chunk_copies(source, target, sems.at[k], PARTS)
        for k, (source, target) in enumerate(
            [(key_ref, key_near), (embedded_ref, rows_ref), (value_ref, value_near)]
        )
    ]
    for copies in loads:
        for copy in copies:
            copy.start()
    for copy in loads[0] + loads[1]:
        copy.wait()
    out_ref[:seg_rows] = dot(rows_ref[...], key_near[...]).astype(BF)
    for copy in loads[2]:
        copy.wait()
    out_ref[seg_rows:] = dot(rows_ref[...], value_near[...]).astype(BF)


def keys_and_values(embedded, w_key, w_value):
    return pl.pallas_call(
        kv_kernel,
        out_shape=jax.ShapeDtypeStruct((2 * embedded.shape[0], w_key.shape[1]), BF),
        in_specs=[IN_PLACE] * 3,
        out_specs=IN_VMEM,
        scratch_shapes=[
            pltpu.VMEM(embedded.shape, BF),
            pltpu.VMEM(w_key.shape, BF),
            pltpu.VMEM(w_value.shape, BF),
            pltpu.SemaphoreType.DMA((3, PARTS)),
        ],
        compiler_params=room(12),
        name="keys_and_values",
    )(afar(embedded), afar(w_key), afar(w_value))


def load_kernel(count, *refs):
    sources, targets, sems = refs[:count], refs[count + 1 : 2 * count + 1], refs[2 * count + 1]
    copies = []
    for k, (source, target) in enumerate(zip(sources, targets)):
        copies += chunk_copies(source, target, sems.at[k], PARTS)
    for copy in copies:
        copy.start()
    for copy in copies:
        copy.wait()


def load(weights, after):
    count = len(weights)
    return pl.pallas_call(
        lambda *refs: load_kernel(count, *refs),
        out_shape=[jax.ShapeDtypeStruct(w.shape, w.dtype) for w in weights],
        in_specs=[IN_PLACE] * count + [pl.BlockSpec(memory_space=pl.ANY)],
        out_specs=[IN_VMEM] * count,
        scratch_shapes=[pltpu.SemaphoreType.DMA((count, PARTS))],
        compiler_params=room(4),
        name="load",
    )(*[afar(w) for w in weights], after)


def turned(a):
    return a.astype(F32).T.astype(BF)


def normalize(values, norm_gain, norm_shift):
    centre = values - jnp.mean(values, axis=-1, keepdims=True)
    spread = jnp.mean(centre * centre, axis=-1, keepdims=True)
    return centre * lax.rsqrt(spread + EPSILON) * norm_gain + norm_shift


def prepare_kernel(scale, *refs):
    rows_ref, query_ref, content_ref, position_ref, coarse_ref, fine_ref, weight_ref, targets_ref = refs[:8]
    qc_ref, qp_ref, out_ref, halves_ref, done_ref = refs[8:]
    halves_ref[...] = targets_ref[...]
    done_ref[0] = 0
    queries = dot(rows_ref[...], query_ref[...])
    qc_ref[...] = (queries + content_ref[...]).astype(BF) * BF(scale)
    qp_ref[...] = (queries + position_ref[...]).astype(BF) * BF(scale)
    half = coarse_ref.shape[2]
    group = 256 // STEP
    sin_fine = fine_ref[0][None]
    cos_fine = fine_ref[1][None]
    for block in range(coarse_ref.shape[1] // group):
        sin_coarse = coarse_ref[0, block * group : (block + 1) * group][:, None]
        cos_coarse = coarse_ref[1, block * group : (block + 1) * group][:, None]
        sines = (sin_coarse * cos_fine + cos_coarse * sin_fine).reshape(256, half).astype(BF)
        cosines = (cos_coarse * cos_fine - sin_coarse * sin_fine).reshape(256, half).astype(BF)
        rel = dot(sines, weight_ref[:half]) + dot(cosines, weight_ref[half:])
        out_ref[:, block * 256 : (block + 1) * 256] = rel.T.astype(BF)


def prepare(embedded, w_query, content_bias, position_bias, w_rel, targets, scale):
    seg_rows, features = embedded.shape
    length = 2 * seg_rows
    width = w_query.shape[1]
    frequency = 10000.0 ** (-jnp.arange(0, features, 2).astype(F32) / features)
    coarse = (jnp.arange(length // STEP)[::-1] * STEP).astype(F32)[:, None] * frequency[None]
    fine = jnp.arange(STEP)[::-1].astype(F32)[:, None] * frequency[None]
    queries = jax.ShapeDtypeStruct((seg_rows, width), BF)
    return pl.pallas_call(
        lambda *refs: prepare_kernel(scale, *refs),
        out_shape=(
            queries,
            queries,
            jax.ShapeDtypeStruct((width, length), BF),
            jax.ShapeDtypeStruct((2, seg_rows // 2), jnp.int32),
            jax.ShapeDtypeStruct((1,), jnp.int32),
        ),
        in_specs=[IN_VMEM] * 8,
        out_specs=[IN_VMEM] * 4 + [IN_SMEM],
        compiler_params=room(12),
        name="prepare",
    )(
        near(embedded),
        near(w_query),
        content_bias,
        position_bias,
        near(jnp.stack([jnp.sin(coarse), jnp.cos(coarse)])),
        near(jnp.stack([jnp.sin(fine), jnp.cos(fine)])),
        near(w_rel),
        targets.reshape(2, seg_rows // 2),
    )


def head_lanes(width, head_dim):
    lanes = min(width, max(128, head_dim))
    at = lax.broadcasted_iota(jnp.int32, (1, lanes), 1)
    for head in range(width // head_dim):
        start = head * head_dim // lanes * lanes
        first = head * head_dim - start
        yield head, slice(start, start + lanes), (at >= first) & (at < first + head_dim)


def now_kernel(head_dim, *refs):
    qc_ref, qp_ref, own_ref, rel_ref, pos_ref, top_ref, total_ref, acc_ref, key_ref = refs
    seg_rows, width = qc_ref.shape
    span = rel_ref.shape[1]
    key_ref[...] = turned(own_ref[:seg_rows])
    for block in range(seg_rows // ROWS):
        first = block * ROWS
        rows = slice(first, first + ROWS)
        keys = first + ROWS
        columns = lax.broadcasted_iota(jnp.int32, (ROWS, keys), 1)
        causal = columns <= lax.broadcasted_iota(jnp.int32, (ROWS, keys), 0) + first
        for head, lanes, mask in head_lanes(width, head_dim):
            with_content = jnp.where(mask, qc_ref[rows, lanes], 0)
            with_position = jnp.where(mask, qp_ref[rows, lanes], 0)
            skewed = dot(with_position, rel_ref[lanes])
            position = pltpu.roll(skewed, (seg_rows + 1 + first) % span, 1, stride=1, stride_axis=0)
            pos_ref[head, rows] = position[:, :seg_rows]
            score = dot(with_content, key_ref[lanes, :keys]) + position[:, seg_rows : seg_rows + keys]
            score = jnp.where(causal, score, MASKED)
            top = jnp.max(score, axis=1, keepdims=True)
            weight = jnp.exp(score - top)
            top_ref[rows, head : head + 1] = top
            total_ref[rows, head : head + 1] = jnp.sum(weight, axis=1, keepdims=True)
            mixed = dot(weight.astype(BF), own_ref[seg_rows : seg_rows + keys, lanes])
            old = acc_ref[rows, lanes] if head * head_dim > lanes.start else 0.0
            acc_ref[rows, lanes] = jnp.where(mask, mixed, old)


def past_kernel(head_dim, pred_ref, *refs):
    qc_ref, pair_ref, ahead_ref, back_ref, pos_ref, top_ref, total_ref, acc_ref = refs[:8]
    out_ref, key_ref, value_ref = refs[8:]
    seg_rows, width = qc_ref.shape
    index = lax.axis_index("seg")
    present = pred_ref[0] >= 0
    behind = index - pred_ref[0]
    in_pair = behind == 2 * (index % 2) - 1
    for start in (0, seg_rows):
        part = slice(start, start + seg_rows)
        chosen = jnp.where(behind == -1, back_ref[part], ahead_ref[part])
        chosen = jnp.where(in_pair, pair_ref[part], chosen)
        if start:
            value_ref[...] = chosen
        else:
            key_ref[...] = turned(chosen)
    for block in range(seg_rows // ROWS):
        rows = slice(block * ROWS, (block + 1) * ROWS)
        out = {}
        for head, lanes, mask in head_lanes(width, head_dim):
            with_content = jnp.where(mask, qc_ref[rows, lanes], 0)
            score = dot(with_content, key_ref[lanes]) + pos_ref[head, rows]
            score = jnp.where(present, score, MASKED)
            now_top = top_ref[rows, head : head + 1]
            top = jnp.maximum(now_top, jnp.max(score, axis=1, keepdims=True))
            weight = jnp.exp(score - top)
            decay = jnp.exp(now_top - top)
            total = total_ref[rows, head : head + 1] * decay + jnp.sum(weight, axis=1, keepdims=True)
            mixed = acc_ref[rows, lanes] * decay + dot(weight.astype(BF), value_ref[:, lanes])
            mixed = mixed * (1.0 / total)
            old = out.get(lanes.start, 0.0)
            out[lanes.start] = jnp.where(mask, mixed, old)
        for start, value in out.items():
            out_ref[rows, start : start + value.shape[1]] = value.astype(BF)


def attend_now(with_content, with_position, own, rel_keys, head_dim):
    seg_rows, width = with_content.shape
    heads = width // head_dim
    stats = jax.ShapeDtypeStruct((seg_rows, 128), F32)
    return pl.pallas_call(
        lambda *refs: now_kernel(head_dim, *refs),
        out_shape=(
            jax.ShapeDtypeStruct((heads, seg_rows, seg_rows), F32),
            stats,
            stats,
            jax.ShapeDtypeStruct((seg_rows, width), F32),
        ),
        in_specs=[IN_VMEM] * 4,
        out_specs=[IN_VMEM] * 4,
        scratch_shapes=[pltpu.VMEM((width, seg_rows), BF)],
        compiler_params=room(12),
        name="attend_now",
    )(*[near(a) for a in (with_content, with_position, own, rel_keys)])


def attend_past(pred, with_content, sources, local, head_dim):
    seg_rows, width = with_content.shape
    return pl.pallas_call(
        lambda *refs: past_kernel(head_dim, *refs),
        out_shape=jax.ShapeDtypeStruct((seg_rows, width), BF),
        in_specs=[IN_SMEM] + [IN_VMEM] * 8,
        out_specs=IN_VMEM,
        scratch_shapes=[pltpu.VMEM((width, seg_rows), BF), pltpu.VMEM((seg_rows, width), BF)],
        compiler_params=room(12),
        name="attend_past",
    )(pred, *[near(a) for a in (with_content, *sources, *local)])


def fetch_first(own, behind):
    count = lax.axis_size("seg")
    onward = [(k, k + (1 if k % 2 else 3)) for k in range(count)]
    onward = [(k, j) for k, j in onward if j < count]
    pair = swapped(own, "seg", 1)
    older = lax.ppermute(own, "seg", [(k, k + 2) for k in range(1, count - 2, 2)])
    wanted = lax.ppermute(behind, "seg", [(j, k) for k, j in onward])
    return pair, older, wanted, onward


def choose_kernel(wanted_ref, done_ref, own_ref, pair_ref, older_ref, out_ref):
    odd = lax.axis_index("seg") % 2
    wanted = wanted_ref[0] + done_ref[0]
    use_own = wanted == 3 - 2 * odd
    use_older = (odd == 1) & (wanted == 3)
    out_ref[...] = jnp.where(use_own, own_ref[...], jnp.where(use_older, older_ref[...], pair_ref[...]))


def fetch_second(own, pair, older, wanted, done, onward):
    count = lax.axis_size("seg")
    passed = pl.pallas_call(
        choose_kernel,
        out_shape=jax.ShapeDtypeStruct(own.shape, BF),
        in_specs=[IN_SMEM] * 2 + [IN_VMEM] * 3,
        out_specs=IN_VMEM,
        compiler_params=room(8),
        name="choose",
    )(wanted, done, near(own), near(pair), near(older))
    ahead = lax.ppermute(passed, "seg", onward)
    back = lax.ppermute(pair, "seg", [(k, k - 2) for k in range(3, count, 2)])
    return ahead, back


def gathered(block, axis):
    distance = lax.axis_size(axis) // 2
    far = {0: block}
    while distance >= 1:
        far = {**far, **{d | distance: swapped(b, axis, distance) for d, b in far.items()}}
        distance //= 2
    return [far[d] for d in range(lax.axis_size(axis))]


def mid_kernel(parts, role, *refs):
    heads = refs[:parts]
    outs = refs[parts : 2 * parts]
    (embedded, gain, shift, w_up, up_bias, w_down, partial_ref, first_ref) = refs[2 * parts :]
    count = partial_ref.shape[0]
    half = (lax.axis_index("mp") + role) % 2
    for block in range(count // ROWS):
        rows = pl.ds(pl.multiple_of(half * count + block * ROWS, ROWS), ROWS)
        put = slice(block * ROWS, (block + 1) * ROWS)
        total = embedded[rows].astype(F32)
        for head, out in zip(heads, outs):
            total = total + dot(head[rows], out[...]).astype(BF).astype(F32)
        first = normalize(total, gain[...], shift[...]).astype(BF)
        first_ref[put] = first
        units = jnp.maximum(dot(first, w_up[...]) + up_bias[...], 0.0).astype(BF)
        partial_ref[put] = dot(units, w_down[...]).astype(BF)


def feed_forward(role, attended, outs, embedded, gain, shift, w_up, up_bias, w_down):
    seg_rows, features = embedded.shape
    parts = len(attended)
    return pl.pallas_call(
        lambda *refs: mid_kernel(parts, role, *refs),
        in_specs=[IN_VMEM] * (2 * parts + 6),
        out_specs=[IN_VMEM, IN_VMEM],
        out_shape=(jax.ShapeDtypeStruct((seg_rows // 2, features), BF),) * 2,
        compiler_params=room(16),
        name="feed_forward",
    )(*[near(a) for a in (*attended, *outs, embedded)], gain, shift, near(w_up), up_bias, near(w_down))


def second_kernel(count, *refs):
    terms = refs[:count]
    first, bias, gain, shift, out_ref = refs[count:]
    total = first[...].astype(F32) + bias[...]
    for term in terms:
        total = total + term[...].astype(F32)
    out_ref[...] = normalize(total, gain[...], shift[...]).astype(BF)


def vocab_kernel(role, rows_ref, w_ref, targets_ref, out_ref, logits_ref):
    count = rows_ref.shape[0]
    words = w_ref.shape[1]
    rows = rows_ref[...]
    index = lax.axis_index("mp")
    ids = jnp.where((index + role) % 2 == 0, targets_ref[0:1], targets_ref[1:2])
    ids = (ids - index * words).astype(F32)
    ids = jnp.broadcast_to(ids, (8, count)).T[:, :1].astype(jnp.int32)
    lanes = lax.broadcasted_iota(jnp.int32, (count, 128), 1)
    chunk = 512
    tops = None
    for start in range(0, words, chunk):
        logits = dot(rows, w_ref[:, start : start + chunk])
        logits_ref[:, start : start + chunk] = logits
        for at in range(0, chunk, 128):
            piece = logits[:, at : at + 128]
            tops = piece if tops is None else jnp.maximum(tops, piece)
    top = jnp.max(tops, axis=1, keepdims=True)
    total = jnp.zeros((count, 128), F32)
    picked = jnp.zeros((count, 128), F32)
    for start in range(0, words, 128):
        piece = logits_ref[:, start : start + 128]
        total = total + jnp.exp(piece - top)
        picked = picked + jnp.where(lanes == ids - start, piece, 0.0)
    total = jnp.sum(total, axis=1, keepdims=True)
    picked = jnp.sum(picked, axis=1, keepdims=True)
    packed = jnp.where(lanes == 0, top, jnp.where(lanes == 1, total, picked))
    out_ref[...] = packed.T[:8]


def vocab_stats(role, rows, w_vocab, targets):
    count = rows.shape[0]
    return pl.pallas_call(
        lambda *refs: vocab_kernel(role, *refs),
        in_specs=[IN_VMEM] * 3,
        out_specs=IN_VMEM,
        out_shape=jax.ShapeDtypeStruct((8, count), F32),
        scratch_shapes=[pltpu.VMEM((count, w_vocab.shape[1]), F32)],
        compiler_params=room(16),
        name="vocab_stats",
    )(near(rows), near(w_vocab), targets)


def on_device(
    embedded,
    targets,
    pred_device,
    doc_ids,
    valid_rows,
    w_query,
    w_key,
    w_value,
    w_rel,
    content_bias,
    position_bias,
    attn_out,
    attn_gain,
    attn_shift,
    w_up,
    up_bias,
    w_down,
    down_bias,
    ffn_gain,
    ffn_shift,
    w_vocab,
):
    seg_rows, _ = embedded.shape
    head_dim = content_bias.shape[1]
    score_scale = head_dim ** (-0.5)
    row = lambda a: a.reshape(1, -1)
    behind = lax.axis_index("seg") - pred_device
    own = keys_and_values(embedded, w_key, w_value)
    pair, older, wanted, onward = fetch_first(own, behind)
    with_content, with_position, rel_keys, halves, done = prepare(
        embedded, w_query, row(content_bias), row(position_bias), w_rel, targets, score_scale
    )
    local = attend_now(with_content, with_position, own, rel_keys, head_dim)
    ahead, back = fetch_second(own, pair, older, wanted, done, onward)
    outs = gathered(attn_out, "mp")
    attended = attend_past(pred_device, with_content, (pair, ahead, back), local, head_dim)
    w_up, w_down = load([w_up, w_down], attended)
    attended = gathered(attended, "mp")
    mp_count = lax.axis_size("mp")
    forward = lambda role: feed_forward(
        role,
        attended,
        outs,
        embedded,
        row(attn_gain),
        row(attn_shift),
        w_up,
        row(up_bias),
        w_down,
    )
    given, _ = forward(1)
    kept, first_out = forward(0)
    (w_vocab,) = load([w_vocab], kept)
    terms = [kept, swapped(given, "mp", 1)]
    distance = 2
    while distance < mp_count:
        terms = [(terms[0].astype(F32) + terms[1].astype(F32)).astype(BF)]
        terms.append(swapped(terms[0], "mp", distance))
        distance *= 2
    second = pl.pallas_call(
        lambda *refs: second_kernel(len(terms), *refs),
        out_shape=jax.ShapeDtypeStruct(first_out.shape, BF),
        compiler_params=room(8),
        name="second",
    )(*[near(t) for t in terms], near(first_out), row(down_bias), row(ffn_gain), row(ffn_shift))
    other = swapped(second, "mp", 1)
    stats_mine = vocab_stats(0, second, w_vocab, halves)
    stats_other = vocab_stats(1, other, w_vocab, halves)
    stats = lax.all_gather(jnp.concatenate([stats_mine[:3], stats_other[:3]], axis=0), "mp")
    stats = stats.reshape(mp_count, 2, 3, seg_rows // 2)
    stats = jnp.stack([stats[k, :: 1 - 2 * (k % 2)] for k in range(mp_count)])
    top = jnp.max(stats[:, :, 0], axis=0)
    total = jnp.sum(stats[:, :, 1] * jnp.exp(stats[:, :, 0] - top[None]), axis=0)
    token_terms = jnp.sum(stats[:, :, 2], axis=0) - (top + jnp.log(total))
    token_terms = token_terms.reshape(seg_rows)
    token_terms = jnp.where(jnp.arange(seg_rows) < valid_rows[0], token_terms, 0.0)
    doc_slots = lax.axis_size("seg") // DOC_SPAN
    marker = jnp.arange(doc_slots) == doc_ids[0]
    pair = jnp.stack([jnp.sum(token_terms), valid_rows[0].astype(F32)])
    sums = jnp.where(marker[None], pair[:, None], 0.0)
    distance = 1
    while distance < lax.axis_size("seg"):
        wide = distance > 1 and 4 * distance <= lax.axis_size("seg")
        steps = (1, 2, 3) if wide else (1,)
        sums = sum([swapped(sums, "seg", distance * step) for step in steps], sums)
        distance *= 1 + len(steps)
    return (token_terms, sums[0] / sums[1])


def solution(mesh):
    return jax.shard_map(
        on_device,
        mesh=mesh,
        in_specs=(
            P("seg", None),
            P("seg"),
            P("seg"),
            P("seg"),
            P("seg"),
            P(None, "mp"),
            P(None, "mp"),
            P(None, "mp"),
            P(None, "mp"),
            P("mp", None),
            P("mp", None),
            P("mp", None),
            P(),
            P(),
            P(None, "mp"),
            P("mp"),
            P("mp", None),
            P(),
            P(),
            P(),
            P(None, "mp"),
        ),
        out_specs=(P("seg"), P()),
        check_vma=False,
    )
```

time: 148 us -> 98.9 us (0.67)
  Pallas kernels: 51.9 us -> 30.9 us
  other arithmetic: 10.5 us -> 3.53 us
  waiting for transfers between devices: 32 us -> 25.6 us
  matrix products: 6.14 us -> 0 us
  starting transfers between devices: 31.2 us -> 27.9 us
  local copies, waits for them, and re-layouts: 5.7 us -> 2.48 us
  between operations: 4.72 us -> 2.95 us
    pallas_call x7 -> x11, Pallas kernels: 49.2 us -> 30.4 us  [the longest x1 5.83 us: attend_now(): pl.pallas_call(lambda *refs: now_kernel(head_dim, *refs), out_shape=(jax....]
    ppermute x14, waiting for transfers between devices: 31.3 us -> 22.9 us  [swapped(): lax.ppermute(block, axis, [(i, i ^ distance) for i in range(lax.axis_size...]
    ppermute x7 -> x4, starting transfers between devices: 18.2 us -> 10.6 us  [the longest x1 6.92 us: fetch_second(): ahead = lax.ppermute(passed, 'seg', onward)]
    dot_general x3 -> x0, matrix products: 6.14 us -> none  [dot(): return jnp.dot(a, b, preferred_element_type=F32)]
    ppermute x14, starting transfers between devices: 13 us -> 17.4 us  [swapped(): lax.ppermute(block, axis, [(i, i ^ distance) for i in range(lax.axis_size...]
    select_n x5 -> x0, other arithmetic: 3.75 us -> none  [the longest x2 1.54 us: fetch_past(): jnp.where(odd, jnp.where(behind == -1, back, jnp.where(behind == 1, other...]
    pallas_call x1, Pallas kernels: 2.68 us -> 0.51 us  [on_device(): pl.pallas_call(lambda *refs: second_kernel(len(terms), *refs), out_shape=...]
    ppermute x7 -> x4, waiting for transfers between devices: 0.65 us -> 2.68 us  [the longest x1 2.64 us: fetch_second(): ahead = lax.ppermute(passed, 'seg', onward)]
  transfers between devices with their start and end apart: 21 -> 18, of which waited for: 7 -> 7; matrix products, arithmetic and copies ran while one was open for 9% -> 1% of each run, Pallas kernels for 25% -> 23%
where the time goes in v2:
time: 98.9 us; the launch traced here: 98.5 us
  Pallas kernels  30.9 us (31%)
  starting transfers between devices  27.9 us (28%)
  waiting for transfers between devices  25.6 us (26%)
  blocking collectives  5.19 us (5%)
  other arithmetic  3.53 us (4%)
  between operations  2.95 us (3%)
  local copies, waits for them, and re-layouts  2.48 us (3%)
    ppermute x14, waiting for transfers between devices, swapped(): lax.ppermute(block, axis, [(i, i ^ distance) for i in range(lax.axis_size...  22.9 us
    ppermute x14, starting transfers between devices, swapped(): lax.ppermute(block, axis, [(i, i ^ distance) for i in range(lax.axis_size...  17.4 us
    ppermute x1, starting transfers between devices, fetch_second(): ahead = lax.ppermute(passed, 'seg', onward)  6.92 us
    pallas_call x1, Pallas kernels, attend_now(): pl.pallas_call(lambda *refs: now_kernel(head_dim, *refs), out_shape=(jax....  5.83 us
    pallas_call x2, Pallas kernels, feed_forward(): pl.pallas_call(lambda *refs: mid_kernel(parts, role, *refs), in_specs=[IN...  5.33 us
    all_gather x1, blocking collectives, on_device(): lax.all_gather(jnp.concatenate([stats_mine[:3], stats_other[:3]], axis=0)...  5.19 us
    pallas_call x2, Pallas kernels, load(): pl.pallas_call(lambda *refs: load_kernel(count, *refs), out_shape=[jax.Sh...  4.75 us
    pallas_call x2, Pallas kernels, vocab_stats(): pl.pallas_call(lambda *refs: vocab_kernel(role, *refs), in_specs=[IN_VMEM...  4.5 us
  transfers between devices with their start and end apart: 18, of which 7 were waited for; matrix products, arithmetic and copies ran while one was open for 1% of the time, Pallas kernels for 23%

profile of v2, /device:TPU:0, one launch (start us, length us, event | category | flops | bytes accessed | tf_op | source)
XLA Modules:
  0.0 98.5 jit_solution(10515349318923198484)
XLA Ops:
  0.7 3.0 %keys_and_values.1.own_ref.refs_2_ = bf16[1024,256]{1,0:T(8,128)(2,1)S(1)} custom-call(bf16[512,1024]{1,0:T(8,128)(2,1)} %refs_8_.3, bf16[1024,256]{1,0:T(8,128)(2,1)} %key_ref.1, bf16[1024,256]{1,0:T(8,128)(2,1)} %value_ref.1), custom_call_target="tpu_custom_call" | custom-call | tf_op jit(solution)/shard_map/keys_and_values/pallas_call | solution.py:73
  3.7 3.0 %collective-permute-start = (bf16[1024,256]{1,0:T(8,128)(2,1)S(1)}, bf16[1024,256]{1,0:T(8,128)(2,1)S(1)}, u32[]{:S(2)}, u32[]{:S(2)}) collective-permute-start(bf16[1024,256]{1,0:T(8,128)(2,1)S(1)} %keys_and_values.1.own_ref.refs_2_), channel_id=1, source_target_pairs={{0,4},{4,0},{8,12},{12,8},{16,20},{20,16},{24,28},{28,24},{1,5},{5... | collective-permute-start | bytes 1572872 | tf_op jit(solution)/shard_map/ppermute | solution.py:19
  6.8 1.5 %collective-permute-start.2 = (bf16[1024,256]{1,0:T(8,128)(2,1)S(1)}, bf16[1024,256]{1,0:T(8,128)(2,1)}, u32[]{:S(2)}, u32[]{:S(2)}) collective-permute-start(bf16[1024,256]{1,0:T(8,128)(2,1)S(1)} %keys_and_values.1.own_ref.refs_2_), channel_id=1, source_target_pairs={{4,12},{12,20},{20,28},{5,13},{13,21},{21,29},{6,14},{14,22},{22,3... | collective-permute-start | bytes 1572872 | tf_op jit(solution)/shard_map/ppermute | solution.py:288
  10.2 1.6 %collective-permute-start.9 = (bf16[256,1024]{1,0:T(8,128)(2,1)S(1)}, bf16[256,1024]{1,0:T(8,128)(2,1)S(1)}, u32[]{:S(2)}, u32[]{:S(2)}) collective-permute-start(bf16[256,1024]{1,0:T(8,128)(2,1)S(1)} %copy-done.1), channel_id=1, source_target_pairs={{0,2},{1,3},{2,0},{3,1},{4,6},{5,7},{6,4},{7,5},{8,10},{9,11},{10,... | collective-permute-start | bytes 1572872 | tf_op jit(solution)/shard_map/ppermute | solution.py:19
  16.0 2.7 %collective-permute-done.pair_ref.refs_2_ = bf16[1024,256]{1,0:T(8,128)(2,1)S(1)} collective-permute-done((bf16[1024,256]{1,0:T(8,128)(2,1)S(1)}, bf16[1024,256]{1,0:T(8,128)(2,1)S(1)}, u32[]{:S(2)}, u32[]{:S(2)}) %collective-permute-start) | collective-permute-done | bytes 524320 | tf_op jit(solution)/shard_map/ppermute | solution.py:19
  18.7 2.3 %choose.1 = bf16[1024,256]{1,0:T(8,128)(2,1)S(1)} custom-call(s32[1]{0:T(128)} %collective-permute-done.1.wanted_ref, s32[1]{0:T(128)} %get-tuple-element.17.done_ref, bf16[1024,256]{1,0:T(8,128)(2,1)S(1)} %keys_and_values.1.own_ref.refs_2_, bf16[1024,256]{1,0:T(8,128)(2,1)S(1)} %collective-permute-done.pair_ref.refs_2_, ...), custom_call_target="tpu_custom_call" | custom-call | tf_op jit(solution)/shard_map/choose/pallas_call | solution.py:303
  21.0 6.9 %collective-permute-start.3 = (bf16[1024,256]{1,0:T(8,128)(2,1)S(1)}, bf16[1024,256]{1,0:T(8,128)(2,1)S(1)}, u32[]{:S(2)}, u32[]{:S(2)}) collective-permute-start(bf16[1024,256]{1,0:T(8,128)(2,1)S(1)} %choose.1), channel_id=1, source_target_pairs={{0,12},{4,8},{8,20},{12,16},{16,28},{20,24},{1,13},{5,9},{9,21},{1... | collective-permute-start | bytes 1572872 | tf_op jit(solution)/shard_map/ppermute | solution.py:311
  28.9 5.8 %attend_now.1 = (f32[4,512,512]{2,1,0:T(8,128)S(1)}, f32[512,128]{1,0:T(8,128)S(1)}, f32[512,128]{1,0:T(8,128)S(1)}, f32[512,256]{1,0:T(8,128)S(1)}) custom-call(bf16[512,256]{1,0:T(8,128)(2,1)S(1)} %get-tuple-element.16.refs_0_.refs_1_, bf16[512,256]{1,0:T(8,128)(2,1)S(1)} %get-tuple-element.18.refs_1_, ...), custom_call_target="tpu_custom_call" | custom-call | tf_op jit(solution)/shard_map/attend_now/pallas_call | solution.py:254
  35.3 2.6 %collective-permute-done.3.refs_3_ = bf16[1024,256]{1,0:T(8,128)(2,1)S(1)} collective-permute-done((bf16[1024,256]{1,0:T(8,128)(2,1)S(1)}, bf16[1024,256]{1,0:T(8,128)(2,1)S(1)}, u32[]{:S(2)}, u32[]{:S(2)}) %collective-permute-start.3) | collective-permute-done | bytes 524320 | tf_op jit(solution)/shard_map/ppermute | solution.py:311
  38.0 3.4 %attend_past.1.refs_2_.refs_0_ = bf16[512,256]{1,0:T(8,128)(2,1)S(1)} custom-call(s32[1]{0:T(128)S(6)} %copy.28.refs_0_, bf16[512,256]{1,0:T(8,128)(2,1)S(1)} %get-tuple-element.16.refs_0_.refs_1_, bf16[1024,256]{1,0:T(8,128)(2,1)S(1)} %collective-permute-done.pair_ref.refs_2_, bf16[1024,256]{1,0:T(8,128)(2,1)S(1)} %collective-permute-done.3.refs_3_, ...), custom_call_target="tpu_custom_call" | custom-call | tf_op jit(solution)/shard_map/attend_past/pallas_call | solution.py:272
  41.4 1.6 %collective-permute-start.6 = (bf16[512,256]{1,0:T(8,128)(2,1)S(1)}, bf16[512,256]{1,0:T(8,128)(2,1)S(1)}, u32[]{:S(2)}, u32[]{:S(2)}) collective-permute-start(bf16[512,256]{1,0:T(8,128)(2,1)S(1)} %attend_past.1.refs_2_.refs_0_), channel_id=1, source_target_pairs={{0,2},{1,3},{2,0},{3,1},{4,6},{5,7},{6,4},{7,5},{8,10},{9,11},{10,... | collective-permute-start | bytes 786440 | tf_op jit(solution)/shard_map/ppermute | solution.py:19
  43.0 4.8 %collective-permute-done.6.refs_2_ = bf16[512,256]{1,0:T(8,128)(2,1)S(1)} collective-permute-done((bf16[512,256]{1,0:T(8,128)(2,1)S(1)}, bf16[512,256]{1,0:T(8,128)(2,1)S(1)}, u32[]{:S(2)}, u32[]{:S(2)}) %collective-permute-start.6) | collective-permute-done | bytes 262176 | tf_op jit(solution)/shard_map/ppermute | solution.py:19
  47.8 2.2 %load.2 = (bf16[1024,1024]{1,0:T(8,128)(2,1)S(1)}, bf16[1024,1024]{1,0:T(8,128)(2,1)S(1)}) custom-call(bf16[1024,1024]{1,0:T(8,128)(2,1)} %refs_0_.5, bf16[1024,1024]{1,0:T(8,128)(2,1)} %refs_1_.3, bf16[512,256]{1,0:T(8,128)(2,1)S(1)} %attend_past.1.refs_2_.refs_0_), custom_call_target="tpu_custom_call" | custom-call | tf_op jit(solution)/shard_map/load/pallas_call | solution.py:102
  50.1 2.9 %feed_forward.3 = (bf16[256,1024]{1,0:T(8,128)(2,1)S(1)}, bf16[256,1024]{1,0:T(8,128)(2,1)}) custom-call(bf16[512,256]{1,0:T(8,128)(2,1)S(1)} %attend_past.1.refs_2_.refs_0_, bf16[512,256]{1,0:T(8,128)(2,1)S(1)} %collective-permute-done.5.refs_1_, bf16[512,256]{1,0:T(8,128)(2,1)S(1)} %collective-permute-done.6.refs_2_, ...), custom_call_target="tpu_custom_call" | custom-call | tf_op jit(solution)/shard_map/feed_forward/pallas_call | solution.py:346
  53.5 2.5 %feed_forward.2 = (bf16[256,1024]{1,0:T(8,128)(2,1)S(1)}, bf16[256,1024]{1,0:T(8,128)(2,1)S(1)}) custom-call(bf16[512,256]{1,0:T(8,128)(2,1)S(1)} %attend_past.1.refs_2_.refs_0_, bf16[512,256]{1,0:T(8,128)(2,1)S(1)} %collective-permute-done.5.refs_1_, bf16[512,256]{1,0:T(8,128)(2,1)S(1)} %collective-permute-done.6.refs_2_, ...), custom_call_target="tpu_custom_call" | custom-call | tf_op jit(solution)/shard_map/feed_forward/pallas_call | solution.py:346
  56.2 1.6 %collective-permute-start.12 = (bf16[256,1024]{1,0:T(8,128)(2,1)S(1)}, bf16[256,1024]{1,0:T(8,128)(2,1)S(1)}, u32[]{:S(2)}, u32[]{:S(2)}) collective-permute-start(bf16[256,1024]{1,0:T(8,128)(2,1)S(1)} %add_convert_fusion.refs_0_), channel_id=1, source_target_pairs={{0,2},{1,3},{2,0},{3,1},{4,6},{5,7},{6,4},{7,5},{8,10},{9,11},{10,... | collective-permute-start | bytes 1572872 | tf_op jit(solution)/shard_map/ppermute | solution.py:19
  57.7 12.3 %collective-permute-done.12.refs_1_ = bf16[256,1024]{1,0:T(8,128)(2,1)S(1)} collective-permute-done((bf16[256,1024]{1,0:T(8,128)(2,1)S(1)}, bf16[256,1024]{1,0:T(8,128)(2,1)S(1)}, u32[]{:S(2)}, u32[]{:S(2)}) %collective-permute-start.12) | collective-permute-done | bytes 524320 | tf_op jit(solution)/shard_map/ppermute | solution.py:19
  72.0 2.5 %load.3.refs_1_ = bf16[1024,2560]{1,0:T(8,128)(2,1)S(1)} custom-call(bf16[1024,2560]{1,0:T(8,128)(2,1)} %refs_0_.6, bf16[256,1024]{1,0:T(8,128)(2,1)S(1)} %get-tuple-element.26.refs_1_), custom_call_target="tpu_custom_call" | custom-call | tf_op jit(solution)/shard_map/load/pallas_call | solution.py:102
  74.5 2.3 %vocab_stats.2 = f32[8,256]{1,0:T(8,128)S(1)} custom-call(bf16[256,1024]{1,0:T(8,128)(2,1)S(1)} %second.1.refs_0_, bf16[1024,2560]{1,0:T(8,128)(2,1)S(1)} %load.3.refs_1_, s32[2,256]{1,0:T(2,128)S(1)} %get-tuple-element.29.refs_2_), custom_call_target="tpu_custom_call" | custom-call | tf_op jit(solution)/shard_map/vocab_stats/pallas_call | solution.py:397
  76.8 2.2 %vocab_stats.3 = f32[8,256]{1,0:T(8,128)S(1)} custom-call(bf16[256,1024]{1,0:T(8,128)(2,1)S(1)} %collective-permute-done.13.refs_0_, bf16[1024,2560]{1,0:T(8,128)(2,1)S(1)} %load.3.refs_1_, s32[2,256]{1,0:T(2,128)S(1)} %get-tuple-element.29.refs_2_), custom_call_target="tpu_custom_call" | custom-call | tf_op jit(solution)/shard_map/vocab_stats/pallas_call | solution.py:397
  79.1 5.2 %all-gather.1 = f32[4,6,256]{2,1,0:T(8,128)S(1)} all-gather(f32[1,6,256]{2,1,0:T(8,128)S(1)} %maximum_bitcast_fusion), channel_id=2, replica_groups=mesh['seg'=8,'mp'=4] {'mp'}, dimensions={0}, use_global_device_ids=true | all-gather | bytes 30720 | tf_op jit(solution)/shard_map/all_gather | solution.py:477
  85.9 4.0 %collective-permute-start.14 = (f32[2,2]{1,0:T(2,128)S(1)}, f32[2,2]{1,0:T(2,128)S(1)}, u32[]{:S(2)}, u32[]{:S(2)}) collective-permute-start(f32[2,2]{1,0:T(2,128)S(1)} %broadcast_select_fusion), channel_id=1, source_target_pairs={{0,4},{4,0},{8,12},{12,8},{16,20},{20,16},{24,28},{28,24},{1,5},{5... | collective-permute-start | bytes 56 | tf_op jit(solution)/shard_map/ppermute | solution.py:19
  91.5 2.0 %collective-permute-start.17 = (f32[2,2]{1,0:T(2,128)S(1)}, f32[2,2]{1,0:T(2,128)S(1)}, u32[]{:S(2)}, u32[]{:S(2)}) collective-permute-start(f32[2,2]{1,0:T(2,128)S(1)} %fusion.6), channel_id=1, source_target_pairs={{0,24},{4,28},{8,16},{12,20},{16,8},{20,12},{24,0},{28,4},{1,25},{... | collective-permute-start | bytes 56 | tf_op jit(solution)/shard_map/ppermute | solution.py:19
  93.9 2.0 %collective-permute-start.15 = (f32[2,2]{1,0:T(2,128)S(1)}, f32[2,2]{1,0:T(2,128)S(1)}, u32[]{:S(2)}, u32[]{:S(2)}) collective-permute-start(f32[2,2]{1,0:T(2,128)S(1)} %fusion.6), channel_id=1, source_target_pairs={{0,8},{4,12},{8,0},{12,4},{16,24},{20,28},{24,16},{28,20},{1,9},{5... | collective-permute-start | bytes 56 | tf_op jit(solution)/shard_map/ppermute | solution.py:19
  (84 shorter events, 14.6 us)
Async XLA Ops:
  0.6 12.0 %copy-start = (bf16[512,1024]{1,0:T(8,128)(2,1)S(1)}, bf16[512,1024]{1,0:T(8,128)(2,1)}, u32[]{:S(2)}) copy-start(bf16[512,1024]{1,0:T(8,128)(2,1)} %refs_8_.3) | copy-start | bytes 3145732
  0.7 11.2 %copy-start.11 = (f32[4,64]{1,0:T(4,128)S(1)}, f32[4,64]{1,0:T(4,128)}, u32[]{:S(2)}) copy-start(f32[4,64]{1,0:T(4,128)} %param.31) | copy-start | bytes 3076
  0.7 11.4 %copy-start.12 = (s32[512]{0:T(512)S(1)}, s32[512]{0:T(512)}, u32[]{:S(2)}) copy-start(s32[512]{0:T(512)} %param.22) | copy-start | bytes 6148
  3.7 15.0 %collective-permute-start = (bf16[1024,256]{1,0:T(8,128)(2,1)S(1)}, bf16[1024,256]{1,0:T(8,128)(2,1)S(1)}, u32[]{:S(2)}, u32[]{:S(2)}) collective-permute-start(bf16[1024,256]{1,0:T(8,128)(2,1)S(1)} %keys_and_values.1.own_ref.refs_2_), channel_id=1, source_target_pairs={{0,4},{4,0},{8,12},{12,8},{16,20},{20,16},{24,28},{28,24},{1,5},{5... | collective-permute-start | bytes 1572872 | tf_op jit(solution)/shard_map/ppermute | solution.py:19
  6.8 11.9 %collective-permute-start.2 = (bf16[1024,256]{1,0:T(8,128)(2,1)S(1)}, bf16[1024,256]{1,0:T(8,128)(2,1)}, u32[]{:S(2)}, u32[]{:S(2)}) collective-permute-start(bf16[1024,256]{1,0:T(8,128)(2,1)S(1)} %keys_and_values.1.own_ref.refs_2_), channel_id=1, source_target_pairs={{4,12},{12,20},{20,28},{5,13},{13,21},{21,29},{6,14},{14,22},{22,3... | collective-permute-start | bytes 1572872 | tf_op jit(solution)/shard_map/ppermute | solution.py:288
  8.9 7.1 %collective-permute-start.1 = (s32[1]{0:T(128)}, s32[1]{0:T(128)}, u32[]{:S(2)}, u32[]{:S(2)}) collective-permute-start(s32[1]{0:T(128)} %sub.23), channel_id=1, source_target_pairs={{12,0},{8,4},{20,8},{16,12},{28,16},{24,20},{13,1},{9,5},{21,9},{1... | collective-permute-start | bytes 20 | tf_op jit(solution)/shard_map/ppermute | solution.py:289
  10.2 24.6 %collective-permute-start.9 = (bf16[256,1024]{1,0:T(8,128)(2,1)S(1)}, bf16[256,1024]{1,0:T(8,128)(2,1)S(1)}, u32[]{:S(2)}, u32[]{:S(2)}) collective-permute-start(bf16[256,1024]{1,0:T(8,128)(2,1)S(1)} %copy-done.1), channel_id=1, source_target_pairs={{0,2},{1,3},{2,0},{3,1},{4,6},{5,7},{6,4},{7,5},{8,10},{9,11},{10,... | collective-permute-start | bytes 1572872 | tf_op jit(solution)/shard_map/ppermute | solution.py:19
  21.0 16.9 %collective-permute-start.3 = (bf16[1024,256]{1,0:T(8,128)(2,1)S(1)}, bf16[1024,256]{1,0:T(8,128)(2,1)S(1)}, u32[]{:S(2)}, u32[]{:S(2)}) collective-permute-start(bf16[1024,256]{1,0:T(8,128)(2,1)S(1)} %choose.1), channel_id=1, source_target_pairs={{0,12},{4,8},{8,20},{12,16},{16,28},{20,24},{1,13},{5,9},{9,21},{1... | collective-permute-start | bytes 1572872 | tf_op jit(solution)/shard_map/ppermute | solution.py:311
  27.9 10.0 %collective-permute-start.4 = (bf16[1024,256]{1,0:T(8,128)(2,1)S(1)}, bf16[1024,256]{1,0:T(8,128)(2,1)S(1)}, u32[]{:S(2)}, u32[]{:S(2)}) collective-permute-start(bf16[1024,256]{1,0:T(8,128)(2,1)S(1)} %collective-permute-done.pair_ref.refs_2_), channel_id=1, source_target_pairs={{12,4},{20,12},{28,20},{13,5},{21,13},{29,21},{14,6},{22,14},{30,2... | collective-permute-start | bytes 1572872 | tf_op jit(solution)/shard_map/ppermute | solution.py:312
  28.8 21.2 %collective-permute-start.8 = (bf16[256,1024]{1,0:T(8,128)(2,1)S(1)}, bf16[256,1024]{1,0:T(8,128)(2,1)S(1)}, u32[]{:S(2)}, u32[]{:S(2)}) collective-permute-start(bf16[256,1024]{1,0:T(8,128)(2,1)S(1)} %copy-done.1), channel_id=1, source_target_pairs={{0,1},{1,0},{2,3},{3,2},{4,5},{5,4},{6,7},{7,6},{8,9},{9,8},{10,11... | collective-permute-start | bytes 1572872 | tf_op jit(solution)/shard_map/ppermute | solution.py:19
  34.8 15.3 %collective-permute-start.10 = (bf16[256,1024]{1,0:T(8,128)(2,1)S(1)}, bf16[256,1024]{1,0:T(8,128)(2,1)S(1)}, u32[]{:S(2)}, u32[]{:S(2)}) collective-permute-start(bf16[256,1024]{1,0:T(8,128)(2,1)S(1)} %collective-permute-done.9.refs_6_), channel_id=1, source_target_pairs={{0,1},{1,0},{2,3},{3,2},{4,5},{5,4},{6,7},{7,6},{8,9},{9,8},{10,11... | collective-permute-start | bytes 1572872 | tf_op jit(solution)/shard_map/ppermute | solution.py:19
  41.4 6.4 %collective-permute-start.6 = (bf16[512,256]{1,0:T(8,128)(2,1)S(1)}, bf16[512,256]{1,0:T(8,128)(2,1)S(1)}, u32[]{:S(2)}, u32[]{:S(2)}) collective-permute-start(bf16[512,256]{1,0:T(8,128)(2,1)S(1)} %attend_past.1.refs_2_.refs_0_), channel_id=1, source_target_pairs={{0,2},{1,3},{2,0},{3,1},{4,6},{5,7},{6,4},{7,5},{8,10},{9,11},{10,... | collective-permute-start | bytes 786440 | tf_op jit(solution)/shard_map/ppermute | solution.py:19
  43.0 7.1 %collective-permute-start.5 = (bf16[512,256]{1,0:T(8,128)(2,1)S(1)}, bf16[512,256]{1,0:T(8,128)(2,1)S(1)}, u32[]{:S(2)}, u32[]{:S(2)}) collective-permute-start(bf16[512,256]{1,0:T(8,128)(2,1)S(1)} %attend_past.1.refs_2_.refs_0_), channel_id=1, source_target_pairs={{0,1},{1,0},{2,3},{3,2},{4,5},{5,4},{6,7},{7,6},{8,9},{9,8},{10,11... | collective-permute-start | bytes 786440 | tf_op jit(solution)/shard_map/ppermute | solution.py:19
  47.8 2.3 %collective-permute-start.7 = (bf16[512,256]{1,0:T(8,128)(2,1)S(1)}, bf16[512,256]{1,0:T(8,128)(2,1)S(1)}, u32[]{:S(2)}, u32[]{:S(2)}) collective-permute-start(bf16[512,256]{1,0:T(8,128)(2,1)S(1)} %collective-permute-done.6.refs_2_), channel_id=1, source_target_pairs={{0,1},{1,0},{2,3},{3,2},{4,5},{5,4},{6,7},{7,6},{8,9},{9,8},{10,11... | collective-permute-start | bytes 786440 | tf_op jit(solution)/shard_map/ppermute | solution.py:19
  53.0 17.1 %copy-start.7 = (f32[1024]{0:T(1024)S(1)}, f32[1024]{0:T(1024)}, u32[]{:S(2)}) copy-start(f32[1024]{0:T(1024)} %param.38) | copy-start | bytes 12292
  53.0 17.1 %copy-start.8 = (f32[1024]{0:T(1024)S(1)}, f32[1024]{0:T(1024)}, u32[]{:S(2)}) copy-start(f32[1024]{0:T(1024)} %param.39) | copy-start | bytes 12292
  53.0 17.1 %copy-start.9 = (f32[1024]{0:T(1024)S(1)}, f32[1024]{0:T(1024)}, u32[]{:S(2)}) copy-start(f32[1024]{0:T(1024)} %param.40) | copy-start | bytes 12292
  53.0 3.0 %collective-permute-start.11 = (bf16[256,1024]{1,0:T(8,128)(2,1)S(1)}, bf16[256,1024]{1,0:T(8,128)(2,1)S(1)}, u32[]{:S(2)}, u32[]{:S(2)}) collective-permute-start(bf16[256,1024]{1,0:T(8,128)(2,1)S(1)} %get-tuple-element.27), channel_id=1, source_target_pairs={{0,1},{1,0},{2,3},{3,2},{4,5},{5,4},{6,7},{7,6},{8,9},{9,8},{10,11... | collective-permute-start | bytes 1572872 | tf_op jit(solution)/shard_map/ppermute | solution.py:19
  56.2 13.9 %collective-permute-start.12 = (bf16[256,1024]{1,0:T(8,128)(2,1)S(1)}, bf16[256,1024]{1,0:T(8,128)(2,1)S(1)}, u32[]{:S(2)}, u32[]{:S(2)}) collective-permute-start(bf16[256,1024]{1,0:T(8,128)(2,1)S(1)} %add_convert_fusion.refs_0_), channel_id=1, source_target_pairs={{0,2},{1,3},{2,0},{3,1},{4,6},{5,7},{6,4},{7,5},{8,10},{9,11},{10,... | collective-permute-start | bytes 1572872 | tf_op jit(solution)/shard_map/ppermute | solution.py:19
  70.6 6.2 %collective-permute-start.13 = (bf16[256,1024]{1,0:T(8,128)(2,1)S(1)}, bf16[256,1024]{1,0:T(8,128)(2,1)S(1)}, u32[]{:S(2)}, u32[]{:S(2)}) collective-permute-start(bf16[256,1024]{1,0:T(8,128)(2,1)S(1)} %second.1.refs_0_), channel_id=1, source_target_pairs={{0,1},{1,0},{2,3},{3,2},{4,5},{5,4},{6,7},{7,6},{8,9},{9,8},{10,11... | collective-permute-start | bytes 1572872 | tf_op jit(solution)/shard_map/ppermute | solution.py:19
  85.9 5.5 %collective-permute-start.14 = (f32[2,2]{1,0:T(2,128)S(1)}, f32[2,2]{1,0:T(2,128)S(1)}, u32[]{:S(2)}, u32[]{:S(2)}) collective-permute-start(f32[2,2]{1,0:T(2,128)S(1)} %broadcast_select_fusion), channel_id=1, source_target_pairs={{0,4},{4,0},{8,12},{12,8},{16,20},{20,16},{24,28},{28,24},{1,5},{5... | collective-permute-start | bytes 56 | tf_op jit(solution)/shard_map/ppermute | solution.py:19
  91.5 5.4 %collective-permute-start.17 = (f32[2,2]{1,0:T(2,128)S(1)}, f32[2,2]{1,0:T(2,128)S(1)}, u32[]{:S(2)}, u32[]{:S(2)}) collective-permute-start(f32[2,2]{1,0:T(2,128)S(1)} %fusion.6), channel_id=1, source_target_pairs={{0,24},{4,28},{8,16},{12,20},{16,8},{20,12},{24,0},{28,4},{1,25},{... | collective-permute-start | bytes 56 | tf_op jit(solution)/shard_map/ppermute | solution.py:19
  93.4 4.5 %collective-permute-start.16 = (f32[2,2]{1,0:T(2,128)S(1)}, f32[2,2]{1,0:T(2,128)S(1)}, u32[]{:S(2)}, u32[]{:S(2)}) collective-permute-start(f32[2,2]{1,0:T(2,128)S(1)} %fusion.6), channel_id=1, source_target_pairs={{0,16},{4,20},{8,24},{12,28},{16,0},{20,4},{24,8},{28,12},{1,17},{... | collective-permute-start | bytes 56 | tf_op jit(solution)/shard_map/ppermute | solution.py:19
  93.9 4.0 %collective-permute-start.15 = (f32[2,2]{1,0:T(2,128)S(1)}, f32[2,2]{1,0:T(2,128)S(1)}, u32[]{:S(2)}, u32[]{:S(2)}) collective-permute-start(f32[2,2]{1,0:T(2,128)S(1)} %fusion.6), channel_id=1, source_target_pairs={{0,8},{4,12},{8,0},{12,4},{16,24},{20,28},{24,16},{28,20},{1,9},{5... | collective-permute-start | bytes 56 | tf_op jit(solution)/shard_map/ppermute | solution.py:19
  (7 other events, 49.0 us)

commit v3 on v2

--- a/solution.py
+++ b/solution.py
@@ -61,9 +61,14 @@
     for copies in loads:
         for copy in copies:
             copy.start()
-    for copy in loads[0] + loads[1]:
+    for copy in loads[0]:
         copy.wait()
-    out_ref[:seg_rows] = dot(rows_ref[...], key_near[...]).astype(BF)
+    half = seg_rows // 2
+    for k in range(2):
+        for copy in loads[1][k * PARTS // 2 : (k + 1) * PARTS // 2]:
+            copy.wait()
+        part = slice(k * half, (k + 1) * half)
+        out_ref[part] = dot(rows_ref[part], key_near[...]).astype(BF)
     for copy in loads[2]:
         copy.wait()
     out_ref[seg_rows:] = dot(rows_ref[...], value_near[...]).astype(BF)
@@ -122,9 +127,11 @@
 
 def prepare_kernel(scale, *refs):
     rows_ref, query_ref, content_ref, position_ref, coarse_ref, fine_ref, weight_ref, targets_ref = refs[:8]
-    qc_ref, qp_ref, out_ref, halves_ref, done_ref = refs[8:]
+    valid_ref, doc_ref, qc_ref, qp_ref, out_ref, halves_ref, facts_ref = refs[8:]
     halves_ref[...] = targets_ref[...]
-    done_ref[0] = 0
+    facts_ref[0] = 0
+    facts_ref[1] = valid_ref[0]
+    facts_ref[2] = doc_ref[0]
     queries = dot(rows_ref[...], query_ref[...])
     qc_ref[...] = (queries + content_ref[...]).astype(BF) * BF(scale)
     qp_ref[...] = (queries + position_ref[...]).astype(BF) * BF(scale)
@@ -141,7 +148,7 @@
         out_ref[:, block * 256 : (block + 1) * 256] = rel.T.astype(BF)
 
 
-def prepare(embedded, w_query, content_bias, position_bias, w_rel, targets, scale):
+def prepare(embedded, w_query, content_bias, position_bias, w_rel, targets, valid_rows, doc_ids, scale):
     seg_rows, features = embedded.shape
     length = 2 * seg_rows
     width = w_query.shape[1]
@@ -156,9 +163,9 @@
             queries,
             jax.ShapeDtypeStruct((width, length), BF),
             jax.ShapeDtypeStruct((2, seg_rows // 2), jnp.int32),
-            jax.ShapeDtypeStruct((1,), jnp.int32),
+            jax.ShapeDtypeStruct((3,), jnp.int32),
         ),
-        in_specs=[IN_VMEM] * 8,
+        in_specs=[IN_VMEM] * 8 + [IN_SMEM] * 2,
         out_specs=[IN_VMEM] * 4 + [IN_SMEM],
         compiler_params=room(12),
         name="prepare",
@@ -171,6 +178,8 @@
         near(jnp.stack([jnp.sin(fine), jnp.cos(fine)])),
         near(w_rel),
         targets.reshape(2, seg_rows // 2),
+        valid_rows,
+        doc_ids,
     )
 
 
@@ -290,24 +299,34 @@
     return pair, older, wanted, onward
 
 
-def choose_kernel(wanted_ref, done_ref, own_ref, pair_ref, older_ref, out_ref):
+def choose_kernel(wanted_ref, facts_ref, own_ref, pair_ref, older_ref, out_ref, sem):
     odd = lax.axis_index("seg") % 2
-    wanted = wanted_ref[0] + done_ref[0]
+    wanted = wanted_ref[0] + facts_ref[0]
     use_own = wanted == 3 - 2 * odd
     use_older = (odd == 1) & (wanted == 3)
-    out_ref[...] = jnp.where(use_own, own_ref[...], jnp.where(use_older, older_ref[...], pair_ref[...]))
-
-
-def fetch_second(own, pair, older, wanted, done, onward):
+
+    @pl.when(use_older)
+    def _():
+        copy = pltpu.make_async_copy(older_ref, out_ref, sem)
+        copy.start()
+        copy.wait()
+
+    @pl.when(jnp.logical_not(use_older))
+    def _():
+        out_ref[...] = jnp.where(use_own, own_ref[...], pair_ref[...])
+
+
+def fetch_second(own, pair, older, wanted, facts, onward):
     count = lax.axis_size("seg")
     passed = pl.pallas_call(
         choose_kernel,
         out_shape=jax.ShapeDtypeStruct(own.shape, BF),
-        in_specs=[IN_SMEM] * 2 + [IN_VMEM] * 3,
+        in_specs=[IN_SMEM] * 2 + [IN_VMEM] * 2 + [IN_PLACE],
         out_specs=IN_VMEM,
+        scratch_shapes=[pltpu.SemaphoreType.DMA],
         compiler_params=room(8),
         name="choose",
-    )(wanted, done, near(own), near(pair), near(older))
+    )(wanted, facts, near(own), near(pair), afar(older))
     ahead = lax.ppermute(passed, "seg", onward)
     back = lax.ppermute(pair, "seg", [(k, k - 2) for k in range(3, count, 2)])
     return ahead, back
@@ -403,6 +422,43 @@
         compiler_params=room(16),
         name="vocab_stats",
     )(near(rows), near(w_vocab), targets)
+
+
+def token_kernel(facts_ref, stats_ref, token_ref, sums_ref):
+    count, _, half_rows = stats_ref.shape
+    valid = facts_ref[1]
+    whole = jnp.zeros((1, 1), F32)
+    for half in range(2):
+        at = [3 * (half ^ (k & 1)) for k in range(count)]
+        tops = [stats_ref[k, a : a + 1] for k, a in enumerate(at)]
+        top = tops[0]
+        for other in tops[1:]:
+            top = jnp.maximum(top, other)
+        total = sum(stats_ref[k, a + 1 : a + 2] * jnp.exp(tops[k] - top) for k, a in enumerate(at))
+        picked = sum(stats_ref[k, a + 2 : a + 3] for k, a in enumerate(at))
+        rows = lax.broadcasted_iota(jnp.int32, (1, half_rows), 1) + half * half_rows
+        terms = jnp.where(rows < valid, picked - (top + jnp.log(total)), 0.0)
+        token_ref[:, half * half_rows : (half + 1) * half_rows] = terms
+        whole = whole + jnp.sum(terms, axis=1, keepdims=True)
+    shape = sums_ref.shape
+    row = lax.broadcasted_iota(jnp.int32, shape, 0)
+    slot = lax.broadcasted_iota(jnp.int32, shape, 1)
+    values = jnp.where(row == 0, jnp.broadcast_to(whole, shape), valid.astype(F32))
+    sums_ref[...] = jnp.where(slot == facts_ref[2], values, 0.0)
+
+
+def token_terms_of(facts, stats):
+    return pl.pallas_call(
+        token_kernel,
+        in_specs=[IN_SMEM, IN_VMEM],
+        out_specs=[IN_VMEM] * 2,
+        out_shape=(
+            jax.ShapeDtypeStruct((1, 2 * stats.shape[2]), F32),
+            jax.ShapeDtypeStruct((8, 128), F32),
+        ),
+        compiler_params=room(4),
+        name="token_terms",
+    )(facts, near(stats))
 
 
 def on_device(
@@ -435,11 +491,11 @@
     behind = lax.axis_index("seg") - pred_device
     own = keys_and_values(embedded, w_key, w_value)
     pair, older, wanted, onward = fetch_first(own, behind)
-    with_content, with_position, rel_keys, halves, done = prepare(
-        embedded, w_query, row(content_bias), row(position_bias), w_rel, targets, score_scale
+    with_content, with_position, rel_keys, halves, facts = prepare(
+        embedded, w_query, row(content_bias), row(position_bias), w_rel, targets, valid_rows, doc_ids, score_scale
     )
     local = attend_now(with_content, with_position, own, rel_keys, head_dim)
-    ahead, back = fetch_second(own, pair, older, wanted, done, onward)
+    ahead, back = fetch_second(own, pair, older, wanted, facts, onward)
     outs = gathered(attn_out, "mp")
     attended = attend_past(pred_device, with_content, (pair, ahead, back), local, head_dim)
     w_up, w_down = load([w_up, w_down], attended)
@@ -475,24 +531,15 @@
     stats_mine = vocab_stats(0, second, w_vocab, halves)
     stats_other = vocab_stats(1, other, w_vocab, halves)
     stats = lax.all_gather(jnp.concatenate([stats_mine[:3], stats_other[:3]], axis=0), "mp")
-    stats = stats.reshape(mp_count, 2, 3, seg_rows // 2)
-    stats = jnp.stack([stats[k, :: 1 - 2 * (k % 2)] for k in range(mp_count)])
-    top = jnp.max(stats[:, :, 0], axis=0)
-    total = jnp.sum(stats[:, :, 1] * jnp.exp(stats[:, :, 0] - top[None]), axis=0)
-    token_terms = jnp.sum(stats[:, :, 2], axis=0) - (top + jnp.log(total))
-    token_terms = token_terms.reshape(seg_rows)
-    token_terms = jnp.where(jnp.arange(seg_rows) < valid_rows[0], token_terms, 0.0)
+    token_terms, sums = token_terms_of(facts, stats)
     doc_slots = lax.axis_size("seg") // DOC_SPAN
-    marker = jnp.arange(doc_slots) == doc_ids[0]
-    pair = jnp.stack([jnp.sum(token_terms), valid_rows[0].astype(F32)])
-    sums = jnp.where(marker[None], pair[:, None], 0.0)
     distance = 1
     while distance < lax.axis_size("seg"):
         wide = distance > 1 and 4 * distance <= lax.axis_size("seg")
         steps = (1, 2, 3) if wide else (1,)
         sums = sum([swapped(sums, "seg", distance * step) for step in steps], sums)
         distance *= 1 + len(steps)
-    return (token_terms, sums[0] / sums[1])
+    return (token_terms.reshape(seg_rows), sums[0, :doc_slots] / sums[1, :doc_slots])
 
 
 def solution(mesh):

time: 98.9 us -> 96.4 us (0.975)
  other arithmetic: 3.53 us -> 1.3 us
  starting transfers between devices: 27.9 us -> 29.2 us
  waiting for transfers between devices: 25.6 us -> 24.4 us
    ppermute x14, starting transfers between devices: 17.4 us -> 18.7 us  [swapped(): lax.ppermute(block, axis, [(i, i ^ distance) for i in range(lax.axis_size...]
    pallas_call x0 -> x1, Pallas kernels: none -> 1.15 us  [token_terms_of(): pl.pallas_call(token_kernel, in_specs=[IN_SMEM, IN_VMEM], out_specs=[IN_V...]
    ppermute x14, waiting for transfers between devices: 22.9 us -> 21.8 us  [swapped(): lax.ppermute(block, axis, [(i, i ^ distance) for i in range(lax.axis_size...]
    pallas_call x1, Pallas kernels: 2.32 us -> 1.24 us  [fetch_second(): pl.pallas_call(choose_kernel, out_shape=jax.ShapeDtypeStruct(own.shape, B...]
    unnamed x27 -> x26, local copies, waits for them, and re-layouts: 2.13 us -> 2.13 us
  transfers between devices with their start and end apart: 18 -> 18, of which waited for: 7 -> 8; matrix products, arithmetic and copies ran while one was open for 1% -> 1% of each run, Pallas kernels for 23% -> 22%
where the time goes in v3:
time: 96.4 us; the launch traced here: 96.1 us
  Pallas kernels  30.6 us (32%)
  starting transfers between devices  29.2 us (30%)
  waiting for transfers between devices  24.4 us (25%)
  blocking collectives  5.19 us (5%)
  between operations  2.93 us (3%)
  local copies, waits for them, and re-layouts  2.41 us (2%)
  other arithmetic  1.3 us (1%)
    ppermute x14, waiting for transfers between devices, swapped(): lax.ppermute(block, axis, [(i, i ^ distance) for i in range(lax.axis_size...  21.8 us
    ppermute x14, starting transfers between devices, swapped(): lax.ppermute(block, axis, [(i, i ^ distance) for i in range(lax.axis_size...  18.7 us
    ppermute x1, starting transfers between devices, fetch_second(): ahead = lax.ppermute(passed, 'seg', onward)  6.92 us
    pallas_call x1, Pallas kernels, attend_now(): pl.pallas_call(lambda *refs: now_kernel(head_dim, *refs), out_shape=(jax....  5.82 us
    pallas_call x2, Pallas kernels, feed_forward(): pl.pallas_call(lambda *refs: mid_kernel(parts, role, *refs), in_specs=[IN...  5.31 us
    all_gather x1, blocking collectives, on_device(): lax.all_gather(jnp.concatenate([stats_mine[:3], stats_other[:3]], axis=0)...  5.19 us
    pallas_call x2, Pallas kernels, load(): pl.pallas_call(lambda *refs: load_kernel(count, *refs), out_shape=[jax.Sh...  4.75 us
    pallas_call x2, Pallas kernels, vocab_stats(): pl.pallas_call(lambda *refs: vocab_kernel(role, *refs), in_specs=[IN_VMEM...  4.45 us
  transfers between devices with their start and end apart: 18, of which 8 were waited for; matrix products, arithmetic and copies ran while one was open for 1% of the time, Pallas kernels for 22%

profile of v3, /device:TPU:0, one launch (start us, length us, event | category | flops | bytes accessed | tf_op | source)
XLA Modules:
  0.0 96.1 jit_solution(13069858573918368998)
XLA Ops:
  0.7 2.8 %keys_and_values.1.own_ref.refs_2_ = bf16[1024,256]{1,0:T(8,128)(2,1)S(1)} custom-call(bf16[512,1024]{1,0:T(8,128)(2,1)} %refs_8_.4, bf16[1024,256]{1,0:T(8,128)(2,1)} %key_ref.1, bf16[1024,256]{1,0:T(8,128)(2,1)} %value_ref.1), custom_call_target="tpu_custom_call" | custom-call | tf_op jit(solution)/shard_map/keys_and_values/pallas_call | solution.py:78
  3.5 3.0 %collective-permute-start = (bf16[1024,256]{1,0:T(8,128)(2,1)S(1)}, bf16[1024,256]{1,0:T(8,128)(2,1)S(1)}, u32[]{:S(2)}, u32[]{:S(2)}) collective-permute-start(bf16[1024,256]{1,0:T(8,128)(2,1)S(1)} %keys_and_values.1.own_ref.refs_2_), channel_id=1, source_target_pairs={{0,4},{4,0},{8,12},{12,8},{16,20},{20,16},{24,28},{28,24},{1,5},{5... | collective-permute-start | bytes 1572872 | tf_op jit(solution)/shard_map/ppermute | solution.py:19
  6.5 1.4 %collective-permute-start.2 = (bf16[1024,256]{1,0:T(8,128)(2,1)S(1)}, bf16[1024,256]{1,0:T(8,128)(2,1)}, u32[]{:S(2)}, u32[]{:S(2)}) collective-permute-start(bf16[1024,256]{1,0:T(8,128)(2,1)S(1)} %keys_and_values.1.own_ref.refs_2_), channel_id=1, source_target_pairs={{4,12},{12,20},{20,28},{5,13},{13,21},{21,29},{6,14},{14,22},{22,3... | collective-permute-start | bytes 1572872 | tf_op jit(solution)/shard_map/ppermute | solution.py:297
  8.6 1.3 %collective-permute-start.1 = (s32[1]{0:T(128)}, s32[1]{0:T(128)}, u32[]{:S(2)}, u32[]{:S(2)}) collective-permute-start(s32[1]{0:T(128)} %sub.7), channel_id=1, source_target_pairs={{12,0},{8,4},{20,8},{16,12},{28,16},{24,20},{13,1},{9,5},{21,9},{1... | collective-permute-start | bytes 20 | tf_op jit(solution)/shard_map/ppermute | solution.py:298
  9.9 1.6 %collective-permute-start.9 = (bf16[256,1024]{1,0:T(8,128)(2,1)S(1)}, bf16[256,1024]{1,0:T(8,128)(2,1)S(1)}, u32[]{:S(2)}, u32[]{:S(2)}) collective-permute-start(bf16[256,1024]{1,0:T(8,128)(2,1)S(1)} %copy-done.1), channel_id=1, source_target_pairs={{0,2},{1,3},{2,0},{3,1},{4,6},{5,7},{6,4},{7,5},{8,10},{9,11},{10,... | collective-permute-start | bytes 1572872 | tf_op jit(solution)/shard_map/ppermute | solution.py:19
  17.0 1.4 %collective-permute-done.pair_ref.refs_2_ = bf16[1024,256]{1,0:T(8,128)(2,1)S(1)} collective-permute-done((bf16[1024,256]{1,0:T(8,128)(2,1)S(1)}, bf16[1024,256]{1,0:T(8,128)(2,1)S(1)}, u32[]{:S(2)}, u32[]{:S(2)}) %collective-permute-start) | collective-permute-done | bytes 524320 | tf_op jit(solution)/shard_map/ppermute | solution.py:19
  19.7 6.9 %collective-permute-start.3 = (bf16[1024,256]{1,0:T(8,128)(2,1)S(1)}, bf16[1024,256]{1,0:T(8,128)(2,1)S(1)}, u32[]{:S(2)}, u32[]{:S(2)}) collective-permute-start(bf16[1024,256]{1,0:T(8,128)(2,1)S(1)} %choose.1), channel_id=1, source_target_pairs={{0,12},{4,8},{8,20},{12,16},{16,28},{20,24},{1,13},{5,9},{9,21},{1... | collective-permute-start | bytes 1572872 | tf_op jit(solution)/shard_map/ppermute | solution.py:330
  27.6 5.8 %attend_now.1 = (f32[4,512,512]{2,1,0:T(8,128)S(1)}, f32[512,128]{1,0:T(8,128)S(1)}, f32[512,128]{1,0:T(8,128)S(1)}, f32[512,256]{1,0:T(8,128)S(1)}) custom-call(bf16[512,256]{1,0:T(8,128)(2,1)S(1)} %get-tuple-element.19.refs_0_.refs_1_, bf16[512,256]{1,0:T(8,128)(2,1)S(1)} %get-tuple-element.20.refs_1_, ...), custom_call_target="tpu_custom_call" | custom-call | tf_op jit(solution)/shard_map/attend_now/pallas_call | solution.py:263
  34.0 2.6 %collective-permute-done.3.refs_3_ = bf16[1024,256]{1,0:T(8,128)(2,1)S(1)} collective-permute-done((bf16[1024,256]{1,0:T(8,128)(2,1)S(1)}, bf16[1024,256]{1,0:T(8,128)(2,1)S(1)}, u32[]{:S(2)}, u32[]{:S(2)}) %collective-permute-start.3) | collective-permute-done | bytes 524320 | tf_op jit(solution)/shard_map/ppermute | solution.py:330
  36.6 3.4 %attend_past.1.refs_2_.refs_0_ = bf16[512,256]{1,0:T(8,128)(2,1)S(1)} custom-call(s32[1]{0:T(128)S(6)} %copy.23.refs_0_, bf16[512,256]{1,0:T(8,128)(2,1)S(1)} %get-tuple-element.19.refs_0_.refs_1_, bf16[1024,256]{1,0:T(8,128)(2,1)S(1)} %collective-permute-done.pair_ref.refs_2_, bf16[1024,256]{1,0:T(8,128)(2,1)S(1)} %collective-permute-done.3.refs_3_, ...), custom_call_target="tpu_custom_call" | custom-call | tf_op jit(solution)/shard_map/attend_past/pallas_call | solution.py:281
  40.0 1.6 %collective-permute-start.6 = (bf16[512,256]{1,0:T(8,128)(2,1)S(1)}, bf16[512,256]{1,0:T(8,128)(2,1)S(1)}, u32[]{:S(2)}, u32[]{:S(2)}) collective-permute-start(bf16[512,256]{1,0:T(8,128)(2,1)S(1)} %attend_past.1.refs_2_.refs_0_), channel_id=1, source_target_pairs={{0,2},{1,3},{2,0},{3,1},{4,6},{5,7},{6,4},{7,5},{8,10},{9,11},{10,... | collective-permute-start | bytes 786440 | tf_op jit(solution)/shard_map/ppermute | solution.py:19
  41.6 4.9 %collective-permute-done.6.refs_2_ = bf16[512,256]{1,0:T(8,128)(2,1)S(1)} collective-permute-done((bf16[512,256]{1,0:T(8,128)(2,1)S(1)}, bf16[512,256]{1,0:T(8,128)(2,1)S(1)}, u32[]{:S(2)}, u32[]{:S(2)}) %collective-permute-start.6) | collective-permute-done | bytes 262176 | tf_op jit(solution)/shard_map/ppermute | solution.py:19
  46.5 2.2 %load.2 = (bf16[1024,1024]{1,0:T(8,128)(2,1)S(1)}, bf16[1024,1024]{1,0:T(8,128)(2,1)S(1)}) custom-call(bf16[1024,1024]{1,0:T(8,128)(2,1)} %refs_0_.5, bf16[1024,1024]{1,0:T(8,128)(2,1)} %refs_1_.3, bf16[512,256]{1,0:T(8,128)(2,1)S(1)} %attend_past.1.refs_2_.refs_0_), custom_call_target="tpu_custom_call" | custom-call | tf_op jit(solution)/shard_map/load/pallas_call | solution.py:107
  48.8 2.8 %feed_forward.3 = (bf16[256,1024]{1,0:T(8,128)(2,1)S(1)}, bf16[256,1024]{1,0:T(8,128)(2,1)}) custom-call(bf16[512,256]{1,0:T(8,128)(2,1)S(1)} %attend_past.1.refs_2_.refs_0_, bf16[512,256]{1,0:T(8,128)(2,1)S(1)} %collective-permute-done.5.refs_1_, bf16[512,256]{1,0:T(8,128)(2,1)S(1)} %collective-permute-done.6.refs_2_, ...), custom_call_target="tpu_custom_call" | custom-call | tf_op jit(solution)/shard_map/feed_forward/pallas_call | solution.py:365
  52.1 2.5 %feed_forward.2 = (bf16[256,1024]{1,0:T(8,128)(2,1)S(1)}, bf16[256,1024]{1,0:T(8,128)(2,1)S(1)}) custom-call(bf16[512,256]{1,0:T(8,128)(2,1)S(1)} %attend_past.1.refs_2_.refs_0_, bf16[512,256]{1,0:T(8,128)(2,1)S(1)} %collective-permute-done.5.refs_1_, bf16[512,256]{1,0:T(8,128)(2,1)S(1)} %collective-permute-done.6.refs_2_, ...), custom_call_target="tpu_custom_call" | custom-call | tf_op jit(solution)/shard_map/feed_forward/pallas_call | solution.py:365
  54.8 1.6 %collective-permute-start.12 = (bf16[256,1024]{1,0:T(8,128)(2,1)S(1)}, bf16[256,1024]{1,0:T(8,128)(2,1)S(1)}, u32[]{:S(2)}, u32[]{:S(2)}) collective-permute-start(bf16[256,1024]{1,0:T(8,128)(2,1)S(1)} %add_convert_fusion.refs_0_), channel_id=1, source_target_pairs={{0,2},{1,3},{2,0},{3,1},{4,6},{5,7},{6,4},{7,5},{8,10},{9,11},{10,... | collective-permute-start | bytes 1572872 | tf_op jit(solution)/shard_map/ppermute | solution.py:19
  56.4 12.3 %collective-permute-done.12.refs_1_ = bf16[256,1024]{1,0:T(8,128)(2,1)S(1)} collective-permute-done((bf16[256,1024]{1,0:T(8,128)(2,1)S(1)}, bf16[256,1024]{1,0:T(8,128)(2,1)S(1)}, u32[]{:S(2)}, u32[]{:S(2)}) %collective-permute-start.12) | collective-permute-done | bytes 524320 | tf_op jit(solution)/shard_map/ppermute | solution.py:19
  69.3 2.5 %load.3.refs_1_ = bf16[1024,2560]{1,0:T(8,128)(2,1)S(1)} custom-call(bf16[1024,2560]{1,0:T(8,128)(2,1)} %refs_0_.6, bf16[256,1024]{1,0:T(8,128)(2,1)S(1)} %get-tuple-element.28.refs_1_), custom_call_target="tpu_custom_call" | custom-call | tf_op jit(solution)/shard_map/load/pallas_call | solution.py:107
  71.9 2.2 %vocab_stats.2 = f32[8,256]{1,0:T(8,128)S(1)} custom-call(bf16[256,1024]{1,0:T(8,128)(2,1)S(1)} %second.1.refs_0_, bf16[1024,2560]{1,0:T(8,128)(2,1)S(1)} %load.3.refs_1_, s32[2,256]{1,0:T(2,128)S(1)} %get-tuple-element.31.refs_2_), custom_call_target="tpu_custom_call" | custom-call | tf_op jit(solution)/shard_map/vocab_stats/pallas_call | solution.py:416
  74.1 2.2 %vocab_stats.3 = f32[8,256]{1,0:T(8,128)S(1)} custom-call(bf16[256,1024]{1,0:T(8,128)(2,1)S(1)} %collective-permute-done.13.refs_0_, bf16[1024,2560]{1,0:T(8,128)(2,1)S(1)} %load.3.refs_1_, s32[2,256]{1,0:T(2,128)S(1)} %get-tuple-element.31.refs_2_), custom_call_target="tpu_custom_call" | custom-call | tf_op jit(solution)/shard_map/vocab_stats/pallas_call | solution.py:416
  76.4 5.2 %all-gather.1.stats_ref = f32[4,6,256]{2,1,0:T(8,128)S(1)} all-gather(f32[1,6,256]{2,1,0:T(8,128)S(1)} %maximum_bitcast_fusion), channel_id=2, replica_groups=mesh['seg'=8,'mp'=4] {'mp'}, dimensions={0}, use_global_device_ids=true | all-gather | bytes 30720 | tf_op jit(solution)/shard_map/all_gather | solution.py:533
  82.7 5.3 %collective-permute-start.14 = (f32[8,128]{1,0:T(8,128)S(1)}, f32[8,128]{1,0:T(8,128)S(1)}, u32[]{:S(2)}, u32[]{:S(2)}) collective-permute-start(f32[8,128]{1,0:T(8,128)S(1)} %get-tuple-element.33), channel_id=1, source_target_pairs={{0,4},{4,0},{8,12},{12,8},{16,20},{20,16},{24,28},{28,24},{1,5},{5... | collective-permute-start | bytes 12296 | tf_op jit(solution)/shard_map/ppermute | solution.py:19
  88.0 1.6 %collective-permute-done.14 = f32[8,128]{1,0:T(8,128)S(1)} collective-permute-done((f32[8,128]{1,0:T(8,128)S(1)}, f32[8,128]{1,0:T(8,128)S(1)}, u32[]{:S(2)}, u32[]{:S(2)}) %collective-permute-start.14) | collective-permute-done | bytes 4128 | tf_op jit(solution)/shard_map/ppermute | solution.py:19
  91.8 2.2 %collective-permute-start.15 = (f32[8,128]{1,0:T(8,128)S(1)}, f32[8,128]{1,0:T(8,128)S(1)}, u32[]{:S(2)}, u32[]{:S(2)}) collective-permute-start(f32[8,128]{1,0:T(8,128)S(1)} %add.16), channel_id=1, source_target_pairs={{0,8},{4,12},{8,0},{12,4},{16,24},{20,28},{24,16},{28,20},{1,9},{5... | collective-permute-start | bytes 12296 | tf_op jit(solution)/shard_map/ppermute | solution.py:19
  (68 shorter events, 13.8 us)
Async XLA Ops:
  0.6 13.1 %copy-start = (bf16[512,1024]{1,0:T(8,128)(2,1)S(1)}, bf16[512,1024]{1,0:T(8,128)(2,1)}, u32[]{:S(2)}) copy-start(bf16[512,1024]{1,0:T(8,128)(2,1)} %refs_8_.4) | copy-start | bytes 3145732
  0.7 10.9 %copy-start.11 = (f32[4,64]{1,0:T(4,128)S(1)}, f32[4,64]{1,0:T(4,128)}, u32[]{:S(2)}) copy-start(f32[4,64]{1,0:T(4,128)} %param.31) | copy-start | bytes 3076
  0.7 11.1 %copy-start.12 = (s32[512]{0:T(512)S(1)}, s32[512]{0:T(512)}, u32[]{:S(2)}) copy-start(s32[512]{0:T(512)} %param.22) | copy-start | bytes 6148
  3.5 15.0 %collective-permute-start = (bf16[1024,256]{1,0:T(8,128)(2,1)S(1)}, bf16[1024,256]{1,0:T(8,128)(2,1)S(1)}, u32[]{:S(2)}, u32[]{:S(2)}) collective-permute-start(bf16[1024,256]{1,0:T(8,128)(2,1)S(1)} %keys_and_values.1.own_ref.refs_2_), channel_id=1, source_target_pairs={{0,4},{4,0},{8,12},{12,8},{16,20},{20,16},{24,28},{28,24},{1,5},{5... | collective-permute-start | bytes 1572872 | tf_op jit(solution)/shard_map/ppermute | solution.py:19
  6.5 11.9 %collective-permute-start.2 = (bf16[1024,256]{1,0:T(8,128)(2,1)S(1)}, bf16[1024,256]{1,0:T(8,128)(2,1)}, u32[]{:S(2)}, u32[]{:S(2)}) collective-permute-start(bf16[1024,256]{1,0:T(8,128)(2,1)S(1)} %keys_and_values.1.own_ref.refs_2_), channel_id=1, source_target_pairs={{4,12},{12,20},{20,28},{5,13},{13,21},{21,29},{6,14},{14,22},{22,3... | collective-permute-start | bytes 1572872 | tf_op jit(solution)/shard_map/ppermute | solution.py:297
  8.6 8.4 %collective-permute-start.1 = (s32[1]{0:T(128)}, s32[1]{0:T(128)}, u32[]{:S(2)}, u32[]{:S(2)}) collective-permute-start(s32[1]{0:T(128)} %sub.7), channel_id=1, source_target_pairs={{12,0},{8,4},{20,8},{16,12},{28,16},{24,20},{13,1},{9,5},{21,9},{1... | collective-permute-start | bytes 20 | tf_op jit(solution)/shard_map/ppermute | solution.py:298
  9.9 23.5 %collective-permute-start.9 = (bf16[256,1024]{1,0:T(8,128)(2,1)S(1)}, bf16[256,1024]{1,0:T(8,128)(2,1)S(1)}, u32[]{:S(2)}, u32[]{:S(2)}) collective-permute-start(bf16[256,1024]{1,0:T(8,128)(2,1)S(1)} %copy-done.1), channel_id=1, source_target_pairs={{0,2},{1,3},{2,0},{3,1},{4,6},{5,7},{6,4},{7,5},{8,10},{9,11},{10,... | collective-permute-start | bytes 1572872 | tf_op jit(solution)/shard_map/ppermute | solution.py:19
  19.7 16.9 %collective-permute-start.3 = (bf16[1024,256]{1,0:T(8,128)(2,1)S(1)}, bf16[1024,256]{1,0:T(8,128)(2,1)S(1)}, u32[]{:S(2)}, u32[]{:S(2)}) collective-permute-start(bf16[1024,256]{1,0:T(8,128)(2,1)S(1)} %choose.1), channel_id=1, source_target_pairs={{0,12},{4,8},{8,20},{12,16},{16,28},{20,24},{1,13},{5,9},{9,21},{1... | collective-permute-start | bytes 1572872 | tf_op jit(solution)/shard_map/ppermute | solution.py:330
  26.6 10.0 %collective-permute-start.4 = (bf16[1024,256]{1,0:T(8,128)(2,1)S(1)}, bf16[1024,256]{1,0:T(8,128)(2,1)S(1)}, u32[]{:S(2)}, u32[]{:S(2)}) collective-permute-start(bf16[1024,256]{1,0:T(8,128)(2,1)S(1)} %collective-permute-done.pair_ref.refs_2_), channel_id=1, source_target_pairs={{12,4},{20,12},{28,20},{13,5},{21,13},{29,21},{14,6},{22,14},{30,2... | collective-permute-start | bytes 1572872 | tf_op jit(solution)/shard_map/ppermute | solution.py:331
  27.5 21.2 %collective-permute-start.8 = (bf16[256,1024]{1,0:T(8,128)(2,1)S(1)}, bf16[256,1024]{1,0:T(8,128)(2,1)S(1)}, u32[]{:S(2)}, u32[]{:S(2)}) collective-permute-start(bf16[256,1024]{1,0:T(8,128)(2,1)S(1)} %copy-done.1), channel_id=1, source_target_pairs={{0,1},{1,0},{2,3},{3,2},{4,5},{5,4},{6,7},{7,6},{8,9},{9,8},{10,11... | collective-permute-start | bytes 1572872 | tf_op jit(solution)/shard_map/ppermute | solution.py:19
  33.4 15.3 %collective-permute-start.10 = (bf16[256,1024]{1,0:T(8,128)(2,1)S(1)}, bf16[256,1024]{1,0:T(8,128)(2,1)S(1)}, u32[]{:S(2)}, u32[]{:S(2)}) collective-permute-start(bf16[256,1024]{1,0:T(8,128)(2,1)S(1)} %collective-permute-done.9.refs_6_), channel_id=1, source_target_pairs={{0,1},{1,0},{2,3},{3,2},{4,5},{5,4},{6,7},{7,6},{8,9},{9,8},{10,11... | collective-permute-start | bytes 1572872 | tf_op jit(solution)/shard_map/ppermute | solution.py:19
  40.0 6.4 %collective-permute-start.6 = (bf16[512,256]{1,0:T(8,128)(2,1)S(1)}, bf16[512,256]{1,0:T(8,128)(2,1)S(1)}, u32[]{:S(2)}, u32[]{:S(2)}) collective-permute-start(bf16[512,256]{1,0:T(8,128)(2,1)S(1)} %attend_past.1.refs_2_.refs_0_), channel_id=1, source_target_pairs={{0,2},{1,3},{2,0},{3,1},{4,6},{5,7},{6,4},{7,5},{8,10},{9,11},{10,... | collective-permute-start | bytes 786440 | tf_op jit(solution)/shard_map/ppermute | solution.py:19
  41.6 7.1 %collective-permute-start.5 = (bf16[512,256]{1,0:T(8,128)(2,1)S(1)}, bf16[512,256]{1,0:T(8,128)(2,1)S(1)}, u32[]{:S(2)}, u32[]{:S(2)}) collective-permute-start(bf16[512,256]{1,0:T(8,128)(2,1)S(1)} %attend_past.1.refs_2_.refs_0_), channel_id=1, source_target_pairs={{0,1},{1,0},{2,3},{3,2},{4,5},{5,4},{6,7},{7,6},{8,9},{9,8},{10,11... | collective-permute-start | bytes 786440 | tf_op jit(solution)/shard_map/ppermute | solution.py:19
  46.5 2.3 %collective-permute-start.7 = (bf16[512,256]{1,0:T(8,128)(2,1)S(1)}, bf16[512,256]{1,0:T(8,128)(2,1)S(1)}, u32[]{:S(2)}, u32[]{:S(2)}) collective-permute-start(bf16[512,256]{1,0:T(8,128)(2,1)S(1)} %collective-permute-done.6.refs_2_), channel_id=1, source_target_pairs={{0,1},{1,0},{2,3},{3,2},{4,5},{5,4},{6,7},{7,6},{8,9},{9,8},{10,11... | collective-permute-start | bytes 786440 | tf_op jit(solution)/shard_map/ppermute | solution.py:19
  51.6 17.1 %copy-start.7 = (f32[1024]{0:T(1024)S(1)}, f32[1024]{0:T(1024)}, u32[]{:S(2)}) copy-start(f32[1024]{0:T(1024)} %param.38) | copy-start | bytes 12292
  51.6 17.1 %copy-start.8 = (f32[1024]{0:T(1024)S(1)}, f32[1024]{0:T(1024)}, u32[]{:S(2)}) copy-start(f32[1024]{0:T(1024)} %param.39) | copy-start | bytes 12292
  51.6 17.1 %copy-start.9 = (f32[1024]{0:T(1024)S(1)}, f32[1024]{0:T(1024)}, u32[]{:S(2)}) copy-start(f32[1024]{0:T(1024)} %param.40) | copy-start | bytes 12292
  51.6 3.0 %collective-permute-start.11 = (bf16[256,1024]{1,0:T(8,128)(2,1)S(1)}, bf16[256,1024]{1,0:T(8,128)(2,1)S(1)}, u32[]{:S(2)}, u32[]{:S(2)}) collective-permute-start(bf16[256,1024]{1,0:T(8,128)(2,1)S(1)} %get-tuple-element.29), channel_id=1, source_target_pairs={{0,1},{1,0},{2,3},{3,2},{4,5},{5,4},{6,7},{7,6},{8,9},{9,8},{10,11... | collective-permute-start | bytes 1572872 | tf_op jit(solution)/shard_map/ppermute | solution.py:19
  54.8 13.9 %collective-permute-start.12 = (bf16[256,1024]{1,0:T(8,128)(2,1)S(1)}, bf16[256,1024]{1,0:T(8,128)(2,1)S(1)}, u32[]{:S(2)}, u32[]{:S(2)}) collective-permute-start(bf16[256,1024]{1,0:T(8,128)(2,1)S(1)} %add_convert_fusion.refs_0_), channel_id=1, source_target_pairs={{0,2},{1,3},{2,0},{3,1},{4,6},{5,7},{6,4},{7,5},{8,10},{9,11},{10,... | collective-permute-start | bytes 1572872 | tf_op jit(solution)/shard_map/ppermute | solution.py:19
  69.3 4.9 %collective-permute-start.13 = (bf16[256,1024]{1,0:T(8,128)(2,1)S(1)}, bf16[256,1024]{1,0:T(8,128)(2,1)S(1)}, u32[]{:S(2)}, u32[]{:S(2)}) collective-permute-start(bf16[256,1024]{1,0:T(8,128)(2,1)S(1)} %second.1.refs_0_), channel_id=1, source_target_pairs={{0,1},{1,0},{2,3},{3,2},{4,5},{5,4},{6,7},{7,6},{8,9},{9,8},{10,11... | collective-permute-start | bytes 1572872 | tf_op jit(solution)/shard_map/ppermute | solution.py:19
  82.7 6.9 %collective-permute-start.14 = (f32[8,128]{1,0:T(8,128)S(1)}, f32[8,128]{1,0:T(8,128)S(1)}, u32[]{:S(2)}, u32[]{:S(2)}) collective-permute-start(f32[8,128]{1,0:T(8,128)S(1)} %get-tuple-element.33), channel_id=1, source_target_pairs={{0,4},{4,0},{8,12},{12,8},{16,20},{20,16},{24,28},{28,24},{1,5},{5... | collective-permute-start | bytes 12296 | tf_op jit(solution)/shard_map/ppermute | solution.py:19
  89.6 5.4 %collective-permute-start.17 = (f32[8,128]{1,0:T(8,128)S(1)}, f32[8,128]{1,0:T(8,128)S(1)}, u32[]{:S(2)}, u32[]{:S(2)}) collective-permute-start(f32[8,128]{1,0:T(8,128)S(1)} %add.16), channel_id=1, source_target_pairs={{0,24},{4,28},{8,16},{12,20},{16,8},{20,12},{24,0},{28,4},{1,25},{... | collective-permute-start | bytes 12296 | tf_op jit(solution)/shard_map/ppermute | solution.py:19
  90.6 4.5 %collective-permute-start.16 = (f32[8,128]{1,0:T(8,128)S(1)}, f32[8,128]{1,0:T(8,128)S(1)}, u32[]{:S(2)}, u32[]{:S(2)}) collective-permute-start(f32[8,128]{1,0:T(8,128)S(1)} %add.16), channel_id=1, source_target_pairs={{0,16},{4,20},{8,24},{12,28},{16,0},{20,4},{24,8},{28,12},{1,17},{... | collective-permute-start | bytes 12296 | tf_op jit(solution)/shard_map/ppermute | solution.py:19
  91.8 3.7 %collective-permute-start.15 = (f32[8,128]{1,0:T(8,128)S(1)}, f32[8,128]{1,0:T(8,128)S(1)}, u32[]{:S(2)}, u32[]{:S(2)}) collective-permute-start(f32[8,128]{1,0:T(8,128)S(1)} %add.16), channel_id=1, source_target_pairs={{0,8},{4,12},{8,0},{12,4},{16,24},{20,28},{24,16},{28,20},{1,9},{5... | collective-permute-start | bytes 12296 | tf_op jit(solution)/shard_map/ppermute | solution.py:19
  (7 other events, 48.4 us)

commit v4 on v3

--- a/solution.py
+++ b/solution.py
@@ -10,6 +10,7 @@
 STEP = 32
 ROWS = 256
 PARTS = 4
+CHUNKS = 2
 MASKED = -1e30
 BF = jnp.bfloat16
 F32 = jnp.float32
@@ -341,32 +342,34 @@
     return [far[d] for d in range(lax.axis_size(axis))]
 
 
-def mid_kernel(parts, role, *refs):
+def mid_kernel(parts, chunk, *refs):
     heads = refs[:parts]
     outs = refs[parts : 2 * parts]
-    (embedded, gain, shift, w_up, up_bias, w_down, partial_ref, first_ref) = refs[2 * parts :]
-    count = partial_ref.shape[0]
-    half = (lax.axis_index("mp") + role) % 2
-    for block in range(count // ROWS):
-        rows = pl.ds(pl.multiple_of(half * count + block * ROWS, ROWS), ROWS)
-        put = slice(block * ROWS, (block + 1) * ROWS)
-        total = embedded[rows].astype(F32)
-        for head, out in zip(heads, outs):
-            total = total + dot(head[rows], out[...]).astype(BF).astype(F32)
-        first = normalize(total, gain[...], shift[...]).astype(BF)
-        first_ref[put] = first
-        units = jnp.maximum(dot(first, w_up[...]) + up_bias[...], 0.0).astype(BF)
-        partial_ref[put] = dot(units, w_down[...]).astype(BF)
-
-
-def feed_forward(role, attended, outs, embedded, gain, shift, w_up, up_bias, w_down):
+    embedded, gain, shift, w_up, up_bias, w_down, given_ref, kept_ref, first_ref = refs[2 * parts :]
+    count = given_ref.shape[0]
+    half_rows = embedded.shape[0] // 2
+    mine = lax.axis_index("mp") % 2
+    starts = [pl.multiple_of(h * half_rows + chunk * count, count) for h in (1 - mine, mine)]
+    rows_of = lambda ref: jnp.concatenate([ref[pl.ds(start, count)] for start in starts], axis=0)
+    total = rows_of(embedded).astype(F32)
+    for head, out in zip(heads, outs):
+        total = total + dot(rows_of(head), out[...]).astype(BF).astype(F32)
+    first = normalize(total, gain[...], shift[...]).astype(BF)
+    first_ref[...] = first[count:]
+    units = jnp.maximum(dot(first, w_up[...]) + up_bias[...], 0.0).astype(BF)
+    partial = dot(units, w_down[...]).astype(BF)
+    given_ref[...] = partial[:count]
+    kept_ref[...] = partial[count:]
+
+
+def feed_forward(chunk, attended, outs, embedded, gain, shift, w_up, up_bias, w_down):
     seg_rows, features = embedded.shape
     parts = len(attended)
     return pl.pallas_call(
-        lambda *refs: mid_kernel(parts, role, *refs),
+        lambda *refs: mid_kernel(parts, chunk, *refs),
         in_specs=[IN_VMEM] * (2 * parts + 6),
-        out_specs=[IN_VMEM, IN_VMEM],
-        out_shape=(jax.ShapeDtypeStruct((seg_rows // 2, features), BF),) * 2,
+        out_specs=[IN_VMEM] * 3,
+        out_shape=(jax.ShapeDtypeStruct((seg_rows // 2 // CHUNKS, features), BF),) * 3,
         compiler_params=room(16),
         name="feed_forward",
     )(*[near(a) for a in (*attended, *outs, embedded)], gain, shift, near(w_up), up_bias, near(w_down))
@@ -381,12 +384,17 @@
     out_ref[...] = normalize(total, gain[...], shift[...]).astype(BF)
 
 
-def vocab_kernel(role, rows_ref, w_ref, targets_ref, out_ref, logits_ref):
-    count = rows_ref.shape[0]
+def vocab_kernel(chunk, mine_ref, other_ref, w_ref, targets_ref, out_ref, logits_ref):
+    piece_rows = mine_ref.shape[0]
+    count = 2 * piece_rows
     words = w_ref.shape[1]
-    rows = rows_ref[...]
+    rows = jnp.concatenate([mine_ref[...], other_ref[...]], axis=0)
     index = lax.axis_index("mp")
-    ids = jnp.where((index + role) % 2 == 0, targets_ref[0:1], targets_ref[1:2])
+    piece = slice(chunk * piece_rows, (chunk + 1) * piece_rows)
+    low, high = targets_ref[0:1, piece], targets_ref[1:2, piece]
+    ids = jnp.concatenate(
+        [jnp.where(index % 2 == 0, low, high), jnp.where(index % 2 == 0, high, low)], axis=1
+    )
     ids = (ids - index * words).astype(F32)
     ids = jnp.broadcast_to(ids, (8, count)).T[:, :1].astype(jnp.int32)
     lanes = lax.broadcasted_iota(jnp.int32, (count, 128), 1)
@@ -411,34 +419,38 @@
     out_ref[...] = packed.T[:8]
 
 
-def vocab_stats(role, rows, w_vocab, targets):
-    count = rows.shape[0]
-    return pl.pallas_call(
-        lambda *refs: vocab_kernel(role, *refs),
-        in_specs=[IN_VMEM] * 3,
+def vocab_stats(chunk, mine, other, w_vocab, targets):
+    count = 2 * mine.shape[0]
+    return pl.pallas_call(
+        lambda *refs: vocab_kernel(chunk, *refs),
+        in_specs=[IN_VMEM] * 4,
         out_specs=IN_VMEM,
         out_shape=jax.ShapeDtypeStruct((8, count), F32),
         scratch_shapes=[pltpu.VMEM((count, w_vocab.shape[1]), F32)],
         compiler_params=room(16),
         name="vocab_stats",
-    )(near(rows), near(w_vocab), targets)
+    )(near(mine), near(other), near(w_vocab), targets)
 
 
 def token_kernel(facts_ref, stats_ref, token_ref, sums_ref):
-    count, _, half_rows = stats_ref.shape
+    count, _, width = stats_ref.shape
+    piece = width // 2
     valid = facts_ref[1]
     whole = jnp.zeros((1, 1), F32)
-    for half in range(2):
-        at = [3 * (half ^ (k & 1)) for k in range(count)]
-        tops = [stats_ref[k, a : a + 1] for k, a in enumerate(at)]
+    for block in range(2 * CHUNKS):
+        half, chunk = divmod(block, CHUNKS)
+        part = lambda k, row: stats_ref[
+            k, 3 * chunk + row : 3 * chunk + row + 1, (half ^ (k & 1)) * piece : ((half ^ (k & 1)) + 1) * piece
+        ]
+        tops = [part(k, 0) for k in range(count)]
         top = tops[0]
         for other in tops[1:]:
             top = jnp.maximum(top, other)
-        total = sum(stats_ref[k, a + 1 : a + 2] * jnp.exp(tops[k] - top) for k, a in enumerate(at))
-        picked = sum(stats_ref[k, a + 2 : a + 3] for k, a in enumerate(at))
-        rows = lax.broadcasted_iota(jnp.int32, (1, half_rows), 1) + half * half_rows
+        total = sum(part(k, 1) * jnp.exp(tops[k] - top) for k in range(count))
+        picked = sum(part(k, 2) for k in range(count))
+        rows = lax.broadcasted_iota(jnp.int32, (1, piece), 1) + block * piece
         terms = jnp.where(rows < valid, picked - (top + jnp.log(total)), 0.0)
-        token_ref[:, half * half_rows : (half + 1) * half_rows] = terms
+        token_ref[:, block * piece : (block + 1) * piece] = terms
         whole = whole + jnp.sum(terms, axis=1, keepdims=True)
     shape = sums_ref.shape
     row = lax.broadcasted_iota(jnp.int32, shape, 0)
@@ -453,7 +465,7 @@
         in_specs=[IN_SMEM, IN_VMEM],
         out_specs=[IN_VMEM] * 2,
         out_shape=(
-            jax.ShapeDtypeStruct((1, 2 * stats.shape[2]), F32),
+            jax.ShapeDtypeStruct((1, CHUNKS * stats.shape[2]), F32),
             jax.ShapeDtypeStruct((8, 128), F32),
         ),
         compiler_params=room(4),
@@ -498,39 +510,43 @@
     ahead, back = fetch_second(own, pair, older, wanted, facts, onward)
     outs = gathered(attn_out, "mp")
     attended = attend_past(pred_device, with_content, (pair, ahead, back), local, head_dim)
-    w_up, w_down = load([w_up, w_down], attended)
+    w_up, w_down, w_vocab = load([w_up, w_down, w_vocab], attended)
     attended = gathered(attended, "mp")
     mp_count = lax.axis_size("mp")
-    forward = lambda role: feed_forward(
-        role,
-        attended,
-        outs,
-        embedded,
-        row(attn_gain),
-        row(attn_shift),
-        w_up,
-        row(up_bias),
-        w_down,
-    )
-    given, _ = forward(1)
-    kept, first_out = forward(0)
-    (w_vocab,) = load([w_vocab], kept)
-    terms = [kept, swapped(given, "mp", 1)]
-    distance = 2
-    while distance < mp_count:
-        terms = [(terms[0].astype(F32) + terms[1].astype(F32)).astype(BF)]
-        terms.append(swapped(terms[0], "mp", distance))
-        distance *= 2
-    second = pl.pallas_call(
-        lambda *refs: second_kernel(len(terms), *refs),
-        out_shape=jax.ShapeDtypeStruct(first_out.shape, BF),
-        compiler_params=room(8),
-        name="second",
-    )(*[near(t) for t in terms], near(first_out), row(down_bias), row(ffn_gain), row(ffn_shift))
-    other = swapped(second, "mp", 1)
-    stats_mine = vocab_stats(0, second, w_vocab, halves)
-    stats_other = vocab_stats(1, other, w_vocab, halves)
-    stats = lax.all_gather(jnp.concatenate([stats_mine[:3], stats_other[:3]], axis=0), "mp")
+    terms, firsts = [], []
+    for chunk in range(CHUNKS):
+        given, kept, first_out = feed_forward(
+            chunk,
+            attended,
+            outs,
+            embedded,
+            row(attn_gain),
+            row(attn_shift),
+            w_up,
+            row(up_bias),
+            w_down,
+        )
+        parts = [kept, swapped(given, "mp", 1)]
+        distance = 2
+        while distance < mp_count:
+            parts = [(parts[0].astype(F32) + parts[1].astype(F32)).astype(BF)]
+            parts.append(swapped(parts[0], "mp", distance))
+            distance *= 2
+        terms.append(parts)
+        firsts.append(first_out)
+    stats = []
+    for chunk in range(CHUNKS):
+        parts = terms[chunk]
+        count = len(parts)
+        second = pl.pallas_call(
+            lambda *refs: second_kernel(count, *refs),
+            out_shape=jax.ShapeDtypeStruct(firsts[chunk].shape, BF),
+            compiler_params=room(8),
+            name="second",
+        )(*[near(t) for t in parts], near(firsts[chunk]), row(down_bias), row(ffn_gain), row(ffn_shift))
+        other = swapped(second, "mp", 1)
+        stats.append(vocab_stats(chunk, second, other, w_vocab, halves))
+    stats = lax.all_gather(jnp.concatenate([s[:3] for s in stats], axis=0), "mp")
     token_terms, sums = token_terms_of(facts, stats)
     doc_slots = lax.axis_size("seg") // DOC_SPAN
     distance = 1

time: 96.4 us -> 96.4 us (level)
  starting transfers between devices: 29.2 us -> 30.8 us
  Pallas kernels: 30.6 us -> 29.2 us
    ppermute x14 -> x17, starting transfers between devices: 18.7 us -> 20.3 us  [swapped(): lax.ppermute(block, axis, [(i, i ^ distance) for i in range(lax.axis_size...]
    pallas_call x2 -> x1, Pallas kernels: 4.75 us -> 3.83 us  [load(): pl.pallas_call(lambda *refs: load_kernel(count, *refs), out_shape=[jax.Sh...]
    pallas_call x5 -> x6, Pallas kernels: 10.3 us -> 9.75 us  [the longest x2 4.68 us: feed_forward(): pl.pallas_call(lambda *refs: mid_kernel(parts, chunk, *refs), in_specs=[I...]
    ppermute x14 -> x17, waiting for transfers between devices: 21.8 us -> 21.6 us  [swapped(): lax.ppermute(block, axis, [(i, i ^ distance) for i in range(lax.axis_size...]
  transfers between devices with their start and end apart: 18 -> 21, of which waited for: 8 -> 8; matrix products, arithmetic and copies ran while one was open for 1% -> 1% of each run, Pallas kernels for 22% -> 22%
where the time goes in v4:
time: 96.4 us; the launch traced here: 96.1 us
  starting transfers between devices  30.8 us (32%)
  Pallas kernels  29.2 us (30%)
  waiting for transfers between devices  24.2 us (25%)
  blocking collectives  5.19 us (5%)
  between operations  2.97 us (3%)
  local copies, waits for them, and re-layouts  2.42 us (3%)
  other arithmetic  1.24 us (1%)
    ppermute x17, waiting for transfers between devices, swapped(): lax.ppermute(block, axis, [(i, i ^ distance) for i in range(lax.axis_size...  21.6 us
    ppermute x17, starting transfers between devices, swapped(): lax.ppermute(block, axis, [(i, i ^ distance) for i in range(lax.axis_size...  20.3 us
    ppermute x1, starting transfers between devices, fetch_second(): ahead = lax.ppermute(passed, 'seg', onward)  6.92 us
    pallas_call x1, Pallas kernels, attend_now(): pl.pallas_call(lambda *refs: now_kernel(head_dim, *refs), out_shape=(jax....  5.81 us
    all_gather x1, blocking collectives, on_device(): lax.all_gather(jnp.concatenate([s[:3] for s in stats], axis=0), 'mp')  5.19 us
    pallas_call x2, Pallas kernels, feed_forward(): pl.pallas_call(lambda *refs: mid_kernel(parts, chunk, *refs), in_specs=[I...  4.68 us
    pallas_call x2, Pallas kernels, vocab_stats(): pl.pallas_call(lambda *refs: vocab_kernel(chunk, *refs), in_specs=[IN_VME...  4.47 us
    pallas_call x1, Pallas kernels, load(): pl.pallas_call(lambda *refs: load_kernel(count, *refs), out_shape=[jax.Sh...  3.83 us
  transfers between devices with their start and end apart: 21, of which 8 were waited for; matrix products, arithmetic and copies ran while one was open for 1% of the time, Pallas kernels for 22%

profile of v4, /device:TPU:0, one launch (start us, length us, event | category | flops | bytes accessed | tf_op | source)
XLA Modules:
  0.0 96.1 jit_solution(12544373619044845989)
XLA Ops:
  0.7 2.8 %keys_and_values.1.own_ref.refs_2_ = bf16[1024,256]{1,0:T(8,128)(2,1)S(1)} custom-call(bf16[512,1024]{1,0:T(8,128)(2,1)} %refs_8_.4, bf16[1024,256]{1,0:T(8,128)(2,1)} %key_ref.1, bf16[1024,256]{1,0:T(8,128)(2,1)} %value_ref.1), custom_call_target="tpu_custom_call" | custom-call | tf_op jit(solution)/shard_map/keys_and_values/pallas_call | solution.py:79
  3.5 3.0 %collective-permute-start = (bf16[1024,256]{1,0:T(8,128)(2,1)S(1)}, bf16[1024,256]{1,0:T(8,128)(2,1)S(1)}, u32[]{:S(2)}, u32[]{:S(2)}) collective-permute-start(bf16[1024,256]{1,0:T(8,128)(2,1)S(1)} %keys_and_values.1.own_ref.refs_2_), channel_id=1, source_target_pairs={{0,4},{4,0},{8,12},{12,8},{16,20},{20,16},{24,28},{28,24},{1,5},{5... | collective-permute-start | bytes 1572872 | tf_op jit(solution)/shard_map/ppermute | solution.py:20
  6.5 1.4 %collective-permute-start.2 = (bf16[1024,256]{1,0:T(8,128)(2,1)S(1)}, bf16[1024,256]{1,0:T(8,128)(2,1)}, u32[]{:S(2)}, u32[]{:S(2)}) collective-permute-start(bf16[1024,256]{1,0:T(8,128)(2,1)S(1)} %keys_and_values.1.own_ref.refs_2_), channel_id=1, source_target_pairs={{4,12},{12,20},{20,28},{5,13},{13,21},{21,29},{6,14},{14,22},{22,3... | collective-permute-start | bytes 1572872 | tf_op jit(solution)/shard_map/ppermute | solution.py:298
  9.9 1.6 %collective-permute-start.9 = (bf16[256,1024]{1,0:T(8,128)(2,1)S(1)}, bf16[256,1024]{1,0:T(8,128)(2,1)S(1)}, u32[]{:S(2)}, u32[]{:S(2)}) collective-permute-start(bf16[256,1024]{1,0:T(8,128)(2,1)S(1)} %copy-done.1), channel_id=1, source_target_pairs={{0,2},{1,3},{2,0},{3,1},{4,6},{5,7},{6,4},{7,5},{8,10},{9,11},{10,... | collective-permute-start | bytes 1572872 | tf_op jit(solution)/shard_map/ppermute | solution.py:20
  17.0 1.4 %collective-permute-done.pair_ref.refs_2_ = bf16[1024,256]{1,0:T(8,128)(2,1)S(1)} collective-permute-done((bf16[1024,256]{1,0:T(8,128)(2,1)S(1)}, bf16[1024,256]{1,0:T(8,128)(2,1)S(1)}, u32[]{:S(2)}, u32[]{:S(2)}) %collective-permute-start) | collective-permute-done | bytes 524320 | tf_op jit(solution)/shard_map/ppermute | solution.py:20
  19.7 6.9 %collective-permute-start.3 = (bf16[1024,256]{1,0:T(8,128)(2,1)S(1)}, bf16[1024,256]{1,0:T(8,128)(2,1)S(1)}, u32[]{:S(2)}, u32[]{:S(2)}) collective-permute-start(bf16[1024,256]{1,0:T(8,128)(2,1)S(1)} %choose.1), channel_id=1, source_target_pairs={{0,12},{4,8},{8,20},{12,16},{16,28},{20,24},{1,13},{5,9},{9,21},{1... | collective-permute-start | bytes 1572872 | tf_op jit(solution)/shard_map/ppermute | solution.py:331
  27.6 5.8 %attend_now.1 = (f32[4,512,512]{2,1,0:T(8,128)S(1)}, f32[512,128]{1,0:T(8,128)S(1)}, f32[512,128]{1,0:T(8,128)S(1)}, f32[512,256]{1,0:T(8,128)S(1)}) custom-call(bf16[512,256]{1,0:T(8,128)(2,1)S(1)} %get-tuple-element.23.refs_0_.refs_1_, bf16[512,256]{1,0:T(8,128)(2,1)S(1)} %get-tuple-element.24.refs_1_, ...), custom_call_target="tpu_custom_call" | custom-call | tf_op jit(solution)/shard_map/attend_now/pallas_call | solution.py:264
  34.0 2.6 %collective-permute-done.3.refs_3_ = bf16[1024,256]{1,0:T(8,128)(2,1)S(1)} collective-permute-done((bf16[1024,256]{1,0:T(8,128)(2,1)S(1)}, bf16[1024,256]{1,0:T(8,128)(2,1)S(1)}, u32[]{:S(2)}, u32[]{:S(2)}) %collective-permute-start.3) | collective-permute-done | bytes 524320 | tf_op jit(solution)/shard_map/ppermute | solution.py:331
  36.6 3.4 %attend_past.1.refs_3_.refs_0_ = bf16[512,256]{1,0:T(8,128)(2,1)S(1)} custom-call(s32[1]{0:T(128)S(6)} %copy.23.refs_0_, bf16[512,256]{1,0:T(8,128)(2,1)S(1)} %get-tuple-element.23.refs_0_.refs_1_, bf16[1024,256]{1,0:T(8,128)(2,1)S(1)} %collective-permute-done.pair_ref.refs_2_, bf16[1024,256]{1,0:T(8,128)(2,1)S(1)} %collective-permute-done.3.refs_3_, ...), custom_call_target="tpu_custom_call" | custom-call | tf_op jit(solution)/shard_map/attend_past/pallas_call | solution.py:282
  40.0 1.6 %collective-permute-start.6 = (bf16[512,256]{1,0:T(8,128)(2,1)S(1)}, bf16[512,256]{1,0:T(8,128)(2,1)S(1)}, u32[]{:S(2)}, u32[]{:S(2)}) collective-permute-start(bf16[512,256]{1,0:T(8,128)(2,1)S(1)} %attend_past.1.refs_3_.refs_0_), channel_id=1, source_target_pairs={{0,2},{1,3},{2,0},{3,1},{4,6},{5,7},{6,4},{7,5},{8,10},{9,11},{10,... | collective-permute-start | bytes 786440 | tf_op jit(solution)/shard_map/ppermute | solution.py:20
  41.6 4.8 %collective-permute-done.6.refs_2_ = bf16[512,256]{1,0:T(8,128)(2,1)S(1)} collective-permute-done((bf16[512,256]{1,0:T(8,128)(2,1)S(1)}, bf16[512,256]{1,0:T(8,128)(2,1)S(1)}, u32[]{:S(2)}, u32[]{:S(2)}) %collective-permute-start.6) | collective-permute-done | bytes 262176 | tf_op jit(solution)/shard_map/ppermute | solution.py:20
  46.5 3.8 %load.1 = (bf16[1024,1024]{1,0:T(8,128)(2,1)S(1)}, bf16[1024,1024]{1,0:T(8,128)(2,1)S(1)}, bf16[1024,2560]{1,0:T(8,128)(2,1)S(1)}) custom-call(bf16[1024,1024]{1,0:T(8,128)(2,1)} %refs_0_.4, bf16[1024,1024]{1,0:T(8,128)(2,1)} %refs_1_.3, bf16[1024,2560]{1,0:T(8,128)(2,1)} %refs_2_.1, bf16[512,256]{1,0:T(8,128)(2,1)S(1)} %attend_past.1.refs_3_.refs_0_), custom_call_target="tpu_custom_call" | custom-call | tf_op jit(solution)/shard_map/load/pallas_call | solution.py:108
  50.4 2.2 %feed_forward.2 = (bf16[128,1024]{1,0:T(8,128)(2,1)S(1)}, bf16[128,1024]{1,0:T(8,128)(2,1)S(1)}, bf16[128,1024]{1,0:T(8,128)(2,1)S(1)}) custom-call(bf16[512,256]{1,0:T(8,128)(2,1)S(1)} %attend_past.1.refs_3_.refs_0_, bf16[512,256]{1,0:T(8,128)(2,1)S(1)} %collective-permute-done.5.refs_1_, bf16[512,256]{1,0:T(8,128)(2,1)S(1)} %collective-permute-done.6.refs_2_, ...), custom_call_target="tpu_custom_call" | custom-call | tf_op jit(solution)/shard_map/feed_forward/pallas_call | solution.py:368
  53.2 2.4 %feed_forward.3 = (bf16[128,1024]{1,0:T(8,128)(2,1)S(1)}, bf16[128,1024]{1,0:T(8,128)(2,1)S(1)}, bf16[128,1024]{1,0:T(8,128)(2,1)S(1)}) custom-call(bf16[512,256]{1,0:T(8,128)(2,1)S(1)} %attend_past.1.refs_3_.refs_0_, bf16[512,256]{1,0:T(8,128)(2,1)S(1)} %collective-permute-done.5.refs_1_, bf16[512,256]{1,0:T(8,128)(2,1)S(1)} %collective-permute-done.6.refs_2_, ...), custom_call_target="tpu_custom_call" | custom-call | tf_op jit(solution)/shard_map/feed_forward/pallas_call | solution.py:368
  55.9 1.6 %collective-permute-start.12 = (bf16[128,1024]{1,0:T(8,128)(2,1)S(1)}, bf16[128,1024]{1,0:T(8,128)(2,1)S(1)}, u32[]{:S(2)}, u32[]{:S(2)}) collective-permute-start(bf16[128,1024]{1,0:T(8,128)(2,1)S(1)} %add_convert_fusion.1.refs_0_), channel_id=1, source_target_pairs={{0,2},{1,3},{2,0},{3,1},{4,6},{5,7},{6,4},{7,5},{8,10},{9,11},{10,... | collective-permute-start | bytes 786440 | tf_op jit(solution)/shard_map/ppermute | solution.py:20
  59.0 6.2 %collective-permute-done.12.refs_1_ = bf16[128,1024]{1,0:T(8,128)(2,1)S(1)} collective-permute-done((bf16[128,1024]{1,0:T(8,128)(2,1)S(1)}, bf16[128,1024]{1,0:T(8,128)(2,1)S(1)}, u32[]{:S(2)}, u32[]{:S(2)}) %collective-permute-start.12) | collective-permute-done | bytes 262176 | tf_op jit(solution)/shard_map/ppermute | solution.py:20
  65.5 4.7 %collective-permute-done.15.refs_1_ = bf16[128,1024]{1,0:T(8,128)(2,1)S(1)} collective-permute-done((bf16[128,1024]{1,0:T(8,128)(2,1)S(1)}, bf16[128,1024]{1,0:T(8,128)(2,1)S(1)}, u32[]{:S(2)}, u32[]{:S(2)}) %collective-permute-start.15) | collective-permute-done | bytes 262176 | tf_op jit(solution)/shard_map/ppermute | solution.py:20
  70.6 2.2 %vocab_stats.2 = f32[8,256]{1,0:T(8,128)S(1)} custom-call(bf16[128,1024]{1,0:T(8,128)(2,1)S(1)} %second.2.refs_0_, bf16[128,1024]{1,0:T(8,128)(2,1)S(1)} %collective-permute-done.13.refs_1_, bf16[1024,2560]{1,0:T(8,128)(2,1)S(1)} %get-tuple-element.35.refs_2_, s32[2,256]{1,0:T(2,128)S(1)} %get-tuple-element.36.refs_3_), custom_call_target="tpu_custom_call" | custom-call | tf_op jit(solution)/shard_map/vocab_stats/pallas_call | solution.py:424
  72.9 2.2 %vocab_stats.3 = f32[8,256]{1,0:T(8,128)S(1)} custom-call(bf16[128,1024]{1,0:T(8,128)(2,1)S(1)} %second.3.refs_0_, bf16[128,1024]{1,0:T(8,128)(2,1)S(1)} %collective-permute-done.16.refs_1_, bf16[1024,2560]{1,0:T(8,128)(2,1)S(1)} %get-tuple-element.35.refs_2_, s32[2,256]{1,0:T(2,128)S(1)} %get-tuple-element.36.refs_3_), custom_call_target="tpu_custom_call" | custom-call | tf_op jit(solution)/shard_map/vocab_stats/pallas_call | solution.py:424
  75.1 5.2 %all-gather.1.stats_ref = f32[4,6,256]{2,1,0:T(8,128)S(1)} all-gather(f32[1,6,256]{2,1,0:T(8,128)S(1)} %maximum_bitcast_fusion), channel_id=2, replica_groups=mesh['seg'=8,'mp'=4] {'mp'}, dimensions={0}, use_global_device_ids=true | all-gather | bytes 30720 | tf_op jit(solution)/shard_map/all_gather | solution.py:549
  81.5 5.3 %collective-permute-start.17 = (f32[8,128]{1,0:T(8,128)S(1)}, f32[8,128]{1,0:T(8,128)S(1)}, u32[]{:S(2)}, u32[]{:S(2)}) collective-permute-start(f32[8,128]{1,0:T(8,128)S(1)} %get-tuple-element.41), channel_id=1, source_target_pairs={{0,4},{4,0},{8,12},{12,8},{16,20},{20,16},{24,28},{28,24},{1,5},{5... | collective-permute-start | bytes 12296 | tf_op jit(solution)/shard_map/ppermute | solution.py:20
  86.7 1.6 %collective-permute-done.17 = f32[8,128]{1,0:T(8,128)S(1)} collective-permute-done((f32[8,128]{1,0:T(8,128)S(1)}, f32[8,128]{1,0:T(8,128)S(1)}, u32[]{:S(2)}, u32[]{:S(2)}) %collective-permute-start.17) | collective-permute-done | bytes 4128 | tf_op jit(solution)/shard_map/ppermute | solution.py:20
  90.1 2.6 %collective-permute-start.20 = (f32[8,128]{1,0:T(8,128)S(1)}, f32[8,128]{1,0:T(8,128)S(1)}, u32[]{:S(2)}, u32[]{:S(2)}) collective-permute-start(f32[8,128]{1,0:T(8,128)S(1)} %add.20), channel_id=1, source_target_pairs={{0,24},{4,28},{8,16},{12,20},{16,8},{20,12},{24,0},{28,4},{1,25},{... | collective-permute-start | bytes 12296 | tf_op jit(solution)/shard_map/ppermute | solution.py:20
  93.6 1.9 %collective-permute-done.20 = f32[8,128]{1,0:T(8,128)S(1)} collective-permute-done((f32[8,128]{1,0:T(8,128)S(1)}, f32[8,128]{1,0:T(8,128)S(1)}, u32[]{:S(2)}, u32[]{:S(2)}) %collective-permute-start.20) | collective-permute-done | bytes 4128 | tf_op jit(solution)/shard_map/ppermute | solution.py:20
  (75 shorter events, 15.6 us)
Async XLA Ops:
  0.6 13.0 %copy-start = (bf16[512,1024]{1,0:T(8,128)(2,1)S(1)}, bf16[512,1024]{1,0:T(8,128)(2,1)}, u32[]{:S(2)}) copy-start(bf16[512,1024]{1,0:T(8,128)(2,1)} %refs_8_.4) | copy-start | bytes 3145732
  3.5 15.0 %collective-permute-start = (bf16[1024,256]{1,0:T(8,128)(2,1)S(1)}, bf16[1024,256]{1,0:T(8,128)(2,1)S(1)}, u32[]{:S(2)}, u32[]{:S(2)}) collective-permute-start(bf16[1024,256]{1,0:T(8,128)(2,1)S(1)} %keys_and_values.1.own_ref.refs_2_), channel_id=1, source_target_pairs={{0,4},{4,0},{8,12},{12,8},{16,20},{20,16},{24,28},{28,24},{1,5},{5... | collective-permute-start | bytes 1572872 | tf_op jit(solution)/shard_map/ppermute | solution.py:20
  6.5 11.9 %collective-permute-start.2 = (bf16[1024,256]{1,0:T(8,128)(2,1)S(1)}, bf16[1024,256]{1,0:T(8,128)(2,1)}, u32[]{:S(2)}, u32[]{:S(2)}) collective-permute-start(bf16[1024,256]{1,0:T(8,128)(2,1)S(1)} %keys_and_values.1.own_ref.refs_2_), channel_id=1, source_target_pairs={{4,12},{12,20},{20,28},{5,13},{13,21},{21,29},{6,14},{14,22},{22,3... | collective-permute-start | bytes 1572872 | tf_op jit(solution)/shard_map/ppermute | solution.py:298
  8.6 8.4 %collective-permute-start.1 = (s32[1]{0:T(128)}, s32[1]{0:T(128)}, u32[]{:S(2)}, u32[]{:S(2)}) collective-permute-start(s32[1]{0:T(128)} %sub.7), channel_id=1, source_target_pairs={{12,0},{8,4},{20,8},{16,12},{28,16},{24,20},{13,1},{9,5},{21,9},{1... | collective-permute-start | bytes 20 | tf_op jit(solution)/shard_map/ppermute | solution.py:299
  9.9 23.5 %collective-permute-start.9 = (bf16[256,1024]{1,0:T(8,128)(2,1)S(1)}, bf16[256,1024]{1,0:T(8,128)(2,1)S(1)}, u32[]{:S(2)}, u32[]{:S(2)}) collective-permute-start(bf16[256,1024]{1,0:T(8,128)(2,1)S(1)} %copy-done.1), channel_id=1, source_target_pairs={{0,2},{1,3},{2,0},{3,1},{4,6},{5,7},{6,4},{7,5},{8,10},{9,11},{10,... | collective-permute-start | bytes 1572872 | tf_op jit(solution)/shard_map/ppermute | solution.py:20
  19.7 16.9 %collective-permute-start.3 = (bf16[1024,256]{1,0:T(8,128)(2,1)S(1)}, bf16[1024,256]{1,0:T(8,128)(2,1)S(1)}, u32[]{:S(2)}, u32[]{:S(2)}) collective-permute-start(bf16[1024,256]{1,0:T(8,128)(2,1)S(1)} %choose.1), channel_id=1, source_target_pairs={{0,12},{4,8},{8,20},{12,16},{16,28},{20,24},{1,13},{5,9},{9,21},{1... | collective-permute-start | bytes 1572872 | tf_op jit(solution)/shard_map/ppermute | solution.py:331
  26.6 10.0 %collective-permute-start.4 = (bf16[1024,256]{1,0:T(8,128)(2,1)S(1)}, bf16[1024,256]{1,0:T(8,128)(2,1)S(1)}, u32[]{:S(2)}, u32[]{:S(2)}) collective-permute-start(bf16[1024,256]{1,0:T(8,128)(2,1)S(1)} %collective-permute-done.pair_ref.refs_2_), channel_id=1, source_target_pairs={{12,4},{20,12},{28,20},{13,5},{21,13},{29,21},{14,6},{22,14},{30,2... | collective-permute-start | bytes 1572872 | tf_op jit(solution)/shard_map/ppermute | solution.py:332
  27.5 22.8 %collective-permute-start.8 = (bf16[256,1024]{1,0:T(8,128)(2,1)S(1)}, bf16[256,1024]{1,0:T(8,128)(2,1)S(1)}, u32[]{:S(2)}, u32[]{:S(2)}) collective-permute-start(bf16[256,1024]{1,0:T(8,128)(2,1)S(1)} %copy-done.1), channel_id=1, source_target_pairs={{0,1},{1,0},{2,3},{3,2},{4,5},{5,4},{6,7},{7,6},{8,9},{9,8},{10,11... | collective-permute-start | bytes 1572872 | tf_op jit(solution)/shard_map/ppermute | solution.py:20
  33.4 16.9 %collective-permute-start.10 = (bf16[256,1024]{1,0:T(8,128)(2,1)S(1)}, bf16[256,1024]{1,0:T(8,128)(2,1)S(1)}, u32[]{:S(2)}, u32[]{:S(2)}) collective-permute-start(bf16[256,1024]{1,0:T(8,128)(2,1)S(1)} %collective-permute-done.9.refs_6_), channel_id=1, source_target_pairs={{0,1},{1,0},{2,3},{3,2},{4,5},{5,4},{6,7},{7,6},{8,9},{9,8},{10,11... | collective-permute-start | bytes 1572872 | tf_op jit(solution)/shard_map/ppermute | solution.py:20
  40.0 6.4 %collective-permute-start.6 = (bf16[512,256]{1,0:T(8,128)(2,1)S(1)}, bf16[512,256]{1,0:T(8,128)(2,1)S(1)}, u32[]{:S(2)}, u32[]{:S(2)}) collective-permute-start(bf16[512,256]{1,0:T(8,128)(2,1)S(1)} %attend_past.1.refs_3_.refs_0_), channel_id=1, source_target_pairs={{0,2},{1,3},{2,0},{3,1},{4,6},{5,7},{6,4},{7,5},{8,10},{9,11},{10,... | collective-permute-start | bytes 786440 | tf_op jit(solution)/shard_map/ppermute | solution.py:20
  41.6 8.7 %collective-permute-start.5 = (bf16[512,256]{1,0:T(8,128)(2,1)S(1)}, bf16[512,256]{1,0:T(8,128)(2,1)S(1)}, u32[]{:S(2)}, u32[]{:S(2)}) collective-permute-start(bf16[512,256]{1,0:T(8,128)(2,1)S(1)} %attend_past.1.refs_3_.refs_0_), channel_id=1, source_target_pairs={{0,1},{1,0},{2,3},{3,2},{4,5},{5,4},{6,7},{7,6},{8,9},{9,8},{10,11... | collective-permute-start | bytes 786440 | tf_op jit(solution)/shard_map/ppermute | solution.py:20
  46.5 3.9 %collective-permute-start.7 = (bf16[512,256]{1,0:T(8,128)(2,1)S(1)}, bf16[512,256]{1,0:T(8,128)(2,1)S(1)}, u32[]{:S(2)}, u32[]{:S(2)}) collective-permute-start(bf16[512,256]{1,0:T(8,128)(2,1)S(1)} %collective-permute-done.6.refs_2_), channel_id=1, source_target_pairs={{0,1},{1,0},{2,3},{3,2},{4,5},{5,4},{6,7},{7,6},{8,9},{9,8},{10,11... | collective-permute-start | bytes 786440 | tf_op jit(solution)/shard_map/ppermute | solution.py:20
  52.6 12.5 %copy-start.7 = (f32[1024]{0:T(1024)S(1)}, f32[1024]{0:T(1024)}, u32[]{:S(2)}) copy-start(f32[1024]{0:T(1024)} %param.38) | copy-start | bytes 12292
  52.6 12.5 %copy-start.8 = (f32[1024]{0:T(1024)S(1)}, f32[1024]{0:T(1024)}, u32[]{:S(2)}) copy-start(f32[1024]{0:T(1024)} %param.39) | copy-start | bytes 12292
  52.7 3.1 %collective-permute-start.11 = (bf16[128,1024]{1,0:T(8,128)(2,1)S(1)}, bf16[128,1024]{1,0:T(8,128)(2,1)S(1)}, u32[]{:S(2)}, u32[]{:S(2)}) collective-permute-start(bf16[128,1024]{1,0:T(8,128)(2,1)S(1)} %get-tuple-element.33), channel_id=1, source_target_pairs={{0,1},{1,0},{2,3},{3,2},{4,5},{5,4},{6,7},{7,6},{8,9},{9,8},{10,11... | collective-permute-start | bytes 786440 | tf_op jit(solution)/shard_map/ppermute | solution.py:20
  55.7 1.8 %collective-permute-start.14 = (bf16[128,1024]{1,0:T(8,128)(2,1)S(1)}, bf16[128,1024]{1,0:T(8,128)(2,1)S(1)}, u32[]{:S(2)}, u32[]{:S(2)}) collective-permute-start(bf16[128,1024]{1,0:T(8,128)(2,1)S(1)} %get-tuple-element.38), channel_id=1, source_target_pairs={{0,1},{1,0},{2,3},{3,2},{4,5},{5,4},{6,7},{7,6},{8,9},{9,8},{10,11... | collective-permute-start | bytes 786440 | tf_op jit(solution)/shard_map/ppermute | solution.py:20
  55.9 9.2 %collective-permute-start.12 = (bf16[128,1024]{1,0:T(8,128)(2,1)S(1)}, bf16[128,1024]{1,0:T(8,128)(2,1)S(1)}, u32[]{:S(2)}, u32[]{:S(2)}) collective-permute-start(bf16[128,1024]{1,0:T(8,128)(2,1)S(1)} %add_convert_fusion.1.refs_0_), channel_id=1, source_target_pairs={{0,2},{1,3},{2,0},{3,1},{4,6},{5,7},{6,4},{7,5},{8,10},{9,11},{10,... | collective-permute-start | bytes 786440 | tf_op jit(solution)/shard_map/ppermute | solution.py:20
  57.5 12.7 %collective-permute-start.15 = (bf16[128,1024]{1,0:T(8,128)(2,1)S(1)}, bf16[128,1024]{1,0:T(8,128)(2,1)S(1)}, u32[]{:S(2)}, u32[]{:S(2)}) collective-permute-start(bf16[128,1024]{1,0:T(8,128)(2,1)S(1)} %add_convert_fusion.refs_0_), channel_id=1, source_target_pairs={{0,2},{1,3},{2,0},{3,1},{4,6},{5,7},{6,4},{7,5},{8,10},{9,11},{10,... | collective-permute-start | bytes 786440 | tf_op jit(solution)/shard_map/ppermute | solution.py:20
  65.4 5.2 %collective-permute-start.13 = (bf16[128,1024]{1,0:T(8,128)(2,1)S(1)}, bf16[128,1024]{1,0:T(8,128)(2,1)S(1)}, u32[]{:S(2)}, u32[]{:S(2)}) collective-permute-start(bf16[128,1024]{1,0:T(8,128)(2,1)S(1)} %second.2.refs_0_), channel_id=1, source_target_pairs={{0,1},{1,0},{2,3},{3,2},{4,5},{5,4},{6,7},{7,6},{8,9},{9,8},{10,11... | collective-permute-start | bytes 786440 | tf_op jit(solution)/shard_map/ppermute | solution.py:20
  70.5 2.3 %collective-permute-start.16 = (bf16[128,1024]{1,0:T(8,128)(2,1)S(1)}, bf16[128,1024]{1,0:T(8,128)(2,1)S(1)}, u32[]{:S(2)}, u32[]{:S(2)}) collective-permute-start(bf16[128,1024]{1,0:T(8,128)(2,1)S(1)} %second.3.refs_0_), channel_id=1, source_target_pairs={{0,1},{1,0},{2,3},{3,2},{4,5},{5,4},{6,7},{7,6},{8,9},{9,8},{10,11... | collective-permute-start | bytes 786440 | tf_op jit(solution)/shard_map/ppermute | solution.py:20
  81.5 6.8 %collective-permute-start.17 = (f32[8,128]{1,0:T(8,128)S(1)}, f32[8,128]{1,0:T(8,128)S(1)}, u32[]{:S(2)}, u32[]{:S(2)}) collective-permute-start(f32[8,128]{1,0:T(8,128)S(1)} %get-tuple-element.41), channel_id=1, source_target_pairs={{0,4},{4,0},{8,12},{12,8},{16,20},{20,16},{24,28},{28,24},{1,5},{5... | collective-permute-start | bytes 12296 | tf_op jit(solution)/shard_map/ppermute | solution.py:20
  88.3 4.4 %collective-permute-start.18 = (f32[8,128]{1,0:T(8,128)S(1)}, f32[8,128]{1,0:T(8,128)S(1)}, u32[]{:S(2)}, u32[]{:S(2)}) collective-permute-start(f32[8,128]{1,0:T(8,128)S(1)} %add.20), channel_id=1, source_target_pairs={{0,8},{4,12},{8,0},{12,4},{16,24},{20,28},{24,16},{28,20},{1,9},{5... | collective-permute-start | bytes 12296 | tf_op jit(solution)/shard_map/ppermute | solution.py:20
  89.1 4.5 %collective-permute-start.19 = (f32[8,128]{1,0:T(8,128)S(1)}, f32[8,128]{1,0:T(8,128)S(1)}, u32[]{:S(2)}, u32[]{:S(2)}) collective-permute-start(f32[8,128]{1,0:T(8,128)S(1)} %add.20), channel_id=1, source_target_pairs={{0,16},{4,20},{8,24},{12,28},{16,0},{20,4},{24,8},{28,12},{1,17},{... | collective-permute-start | bytes 12296 | tf_op jit(solution)/shard_map/ppermute | solution.py:20
  90.1 5.4 %collective-permute-start.20 = (f32[8,128]{1,0:T(8,128)S(1)}, f32[8,128]{1,0:T(8,128)S(1)}, u32[]{:S(2)}, u32[]{:S(2)}) collective-permute-start(f32[8,128]{1,0:T(8,128)S(1)} %add.20), channel_id=1, source_target_pairs={{0,24},{4,28},{8,16},{12,20},{16,8},{20,12},{24,0},{28,4},{1,25},{... | collective-permute-start | bytes 12296 | tf_op jit(solution)/shard_map/ppermute | solution.py:20
  (10 other events, 87.8 us)
